TPU v7x, 32 devices: a whole 2x2x4 slice. The times are simulated.
32 devices in a mesh: tm: 8 (over y, x, core), space: 4 (over z).
Axes of the slice: x: 2, y: 2, z: 4, core: 2. Of those that a mesh axis runs over, the one named last changes fastest.
Arguments:
- rhs: float32 [16, 1024, 1024], P('tm', 'space'), may hold values from -6 to 6
- guess: float32 [16, 1024, 1024], P('tm', 'space'), may hold values from -6 to 6
- diffusion: float32 [1024, 1024], P('space'), may hold values from 0.2 to 2
Outputs:
- solution: float32 [16, 1024, 1024], P('tm', 'space')
- norms: float32 [6], replicated
All inputs are finite; a program needn't handle non-finite values.
Results may differ from a plain program's by a relative error of at most 0.0001.
Values sent between devices are 32-bit elements; how exact they have to be, the bound alone decides.
No kernel may reach another device: no remote copies, remote signals or barrier semaphores. Data moves between devices by JAX's collectives and lax.ppermute only.
A program may use at most 64 MiB of HBM per device.

v0:
```python
import jax
import jax.numpy as jnp
from jax import lax
from jax.sharding import PartitionSpec as P

LEVELS = 5


damping = 0.8


def with_halo(block, sides, width):
    for axis, dim in sides:
        count = lax.axis_size(axis)
        forward = [(i, i + 1) for i in range(count - 1)]
        backward = [(target, source) for source, target in forward]
        low = lax.ppermute(
            lax.slice_in_dim(block, block.shape[dim] - width, None, axis=dim), axis, forward
        )
        high = lax.ppermute(lax.slice_in_dim(block, 0, width, axis=dim), axis, backward)
        block = jnp.concatenate([low, block, high], axis=dim)
    return block


def shifted(value, axis, steps):
    count = lax.axis_size(axis)
    first, last = (max(0, -steps), min(count, count - steps))
    return lax.ppermute(value, axis, [(source, source + steps) for source in range(first, last)])


def from_partner(value, axis, apart):
    mask = 2**apart
    pairs = [(source, source ^ mask) for source in range(lax.axis_size(axis))]
    return lax.ppermute(value, axis, pairs)


def neighbours(field):
    rows = with_halo(field, (("space", 1),), 1)
    padded = jnp.pad(rows, ((0, 0), (0, 0), (1, 1)))
    total = padded[:, 2:, 1:-1] + padded[:, :-2, 1:-1]
    total = total + padded[:, 1:-1, 2:] + padded[:, 1:-1, :-2]
    return total


def residual(field, source, scaled, diag, stride):
    earlier = shifted(field[-1:], "tm", stride)
    before = jnp.concatenate([earlier, field[:-1]], axis=0)
    image = diag * field - scaled * neighbours(field) - before
    return source - image


def stride_of(level):
    if level == 0:
        return 1
    return 2 ** (level - 1)


def body(rhs, guess, diffusion):
    position = lax.axis_index("tm")
    cells = rhs.shape[1] * lax.axis_size("space") * rhs.shape[2]
    partials = []

    def weight_of(level):
        if level <= 1:
            return jnp.float32(1.0)
        stride = stride_of(level)
        return jnp.where(position % stride == stride - 1, 1.0, 0.0).astype(jnp.float32)

    def record(resid, level):
        local_part = jnp.sum(resid * resid) * weight_of(level)
        partials.append(local_part)

    sources = [rhs]
    fields = []
    field = guess
    for level in range(LEVELS - 1):
        source = sources[level]
        scaled = 2.0**level * diffusion
        diag = 1.0 + 4.0 * scaled
        stride = stride_of(level)
        if level == 0:
            field = field + damping * residual(field, source, scaled, diag, stride) / diag
        else:
            field = damping * source / diag
        resid = residual(field, source, scaled, diag, stride)
        record(resid, level)
        fields.append(field)
        if level == 0:
            coarse = resid[0:1] + resid[1:2]
        else:
            coarse = resid + from_partner(resid, "tm", level - 1)
        sources.append(coarse)
    level = LEVELS - 1
    source = sources[level]
    scaled = 2.0**level * diffusion
    diag = 1.0 + 4.0 * scaled
    stride = stride_of(level)
    field = damping * source / diag
    field = field + damping * residual(field, source, scaled, diag, stride) / diag
    resid = residual(field, source, scaled, diag, stride)
    record(resid, level)
    correction = field
    for level in range(LEVELS - 2, -1, -1):
        scaled = 2.0**level * diffusion
        diag = 1.0 + 4.0 * scaled
        stride = stride_of(level)
        field = fields[level] + correction
        field = field + damping * residual(field, sources[level], scaled, diag, stride) / diag
        correction = field
    scaled = 1.0 * diffusion
    diag = 1.0 + 4.0 * scaled
    resid = residual(correction, rhs, scaled, diag, 1)
    record(resid, 0)
    totals = lax.psum(jnp.stack(partials), ("tm", "space"))
    norms = jnp.sqrt(totals / cells)
    return (correction, norms)


def solution(mesh):
    in_specs = (P("tm", "space", None), P("tm", "space", None), P("space", None))
    out_specs = (P("tm", "space", None), P())
    return jax.shard_map(body, mesh=mesh, in_specs=in_specs, out_specs=out_specs, check_vma=False)
```

profile of v0, /device:TPU:0, one launch (start us, length us, event | category | flops | bytes accessed | tf_op | source)
XLA Modules:
  0.0 330.1 jit_solution(2631628433382767291)
XLA Ops:
  6.3 4.9 %collective-permute-start.1 = (f32[2,1,1024]{2,1,0:T(1,128)S(1)}, f32[2,1,1024]{2,1,0:T(1,128)S(1)}, u32[]{:S(2)}, u32[]{:S(2)}) collective-permute-start(f32[2,1,1024]{2,1,0:T(1,128)S(1)} %get-tuple-element.32), channel_id=1, source_target_pairs={{0,1},{1,2},{2,3},{4,5},{5,6},{6,7},{8,9},{9,10},{10,11},{12,13},{... | collective-permute-start | bytes 24584 | tf_op jit(solution)/shard_map/ppermute | solution.py:17
  15.5 7.8 %collective-permute-start.5 = (f32[1,256,1024]{2,1,0:T(8,128)S(1)}, f32[1,256,1024]{2,1,0:T(8,128)S(1)}, u32[]{:S(2)}, u32[]{:S(2)}) collective-permute-start(f32[1,256,1024]{2,1,0:T(8,128)S(1)} %get-tuple-element.28), channel_id=1, source_target_pairs={{0,4},{4,8},{8,12},{12,16},{16,20},{20,24},{24,28},{1,5},{5,9},{9,... | collective-permute-start | bytes 3145736 | tf_op jit(solution)/shard_map/ppermute | solution.py:28
  24.6 4.5 %collective-permute-start.4 = (f32[2,1,1024]{2,1,0:T(1,128)S(1)}, f32[2,1,1024]{2,1,0:T(1,128)S(1)}, u32[]{:S(2)}, u32[]{:S(2)}) collective-permute-start(f32[2,1,1024]{2,1,0:T(1,128)S(1)} %get-tuple-element.26), channel_id=1, source_target_pairs={{0,1},{1,2},{2,3},{4,5},{5,6},{6,7},{8,9},{9,10},{10,11},{12,13},{... | collective-permute-start | bytes 24584 | tf_op jit(solution)/shard_map/ppermute | solution.py:17
  34.0 8.1 %collective-permute-start.8 = (f32[1,256,1024]{2,1,0:T(8,128)S(1)}, f32[1,256,1024]{2,1,0:T(8,128)S(1)}, u32[]{:S(2)}, u32[]{:S(2)}) collective-permute-start(f32[1,256,1024]{2,1,0:T(8,128)S(1)} %bitcast_divide_fusion.3), channel_id=1, source_target_pairs={{0,4},{4,8},{8,12},{12,16},{16,20},{20,24},{24,28},{1,5},{5,9},{9,... | collective-permute-start | bytes 3145736 | tf_op jit(solution)/shard_map/ppermute | solution.py:28
  43.4 4.5 %collective-permute-start.7 = (f32[1,1,1024]{2,1,0:T(1,128)S(1)}, f32[1,1,1024]{2,1,0:T(1,128)S(1)}, u32[]{:S(2)}, u32[]{:S(2)}) collective-permute-start(f32[1,1,1024]{2,1,0:T(1,128)S(1)} %get-tuple-element.48), channel_id=1, source_target_pairs={{0,1},{1,2},{2,3},{4,5},{5,6},{6,7},{8,9},{9,10},{10,11},{12,13},{... | collective-permute-start | bytes 12296 | tf_op jit(solution)/shard_map/ppermute | solution.py:17
  51.2 6.5 %collective-permute-start.9 = (f32[1,256,1024]{2,1,0:T(8,128)S(1)}, f32[1,256,1024]{2,1,0:T(8,128)S(1)}, u32[]{:S(2)}, u32[]{:S(2)}) collective-permute-start(f32[1,256,1024]{2,1,0:T(8,128)S(1)} %get-tuple-element.7), channel_id=1, source_target_pairs={{0,4},{4,0},{8,12},{12,8},{16,20},{20,16},{24,28},{28,24},{1,5},{5... | collective-permute-start | bytes 3145736 | tf_op jit(solution)/shard_map/ppermute | solution.py:34
  60.4 5.3 %collective-permute-start.12 = (f32[1,256,1024]{2,1,0:T(8,128)S(1)}, f32[1,256,1024]{2,1,0:T(8,128)S(1)}, u32[]{:S(2)}, u32[]{:S(2)}) collective-permute-start(f32[1,256,1024]{2,1,0:T(8,128)S(1)} %get-tuple-element.16), channel_id=1, source_target_pairs={{0,8},{4,12},{8,16},{12,20},{16,24},{20,28},{1,9},{5,13},{9,17},{1... | collective-permute-start | bytes 3145736 | tf_op jit(solution)/shard_map/ppermute | solution.py:28
  67.0 4.5 %collective-permute-start.11 = (f32[1,1,1024]{2,1,0:T(1,128)S(1)}, f32[1,1,1024]{2,1,0:T(1,128)S(1)}, u32[]{:S(2)}, u32[]{:S(2)}) collective-permute-start(f32[1,1,1024]{2,1,0:T(1,128)S(1)} %get-tuple-element.46), channel_id=1, source_target_pairs={{0,1},{1,2},{2,3},{4,5},{5,6},{6,7},{8,9},{9,10},{10,11},{12,13},{... | collective-permute-start | bytes 12296 | tf_op jit(solution)/shard_map/ppermute | solution.py:17
  73.2 15.3 %collective-permute-done.12 = f32[1,256,1024]{2,1,0:T(8,128)S(1)} collective-permute-done((f32[1,256,1024]{2,1,0:T(8,128)S(1)}, f32[1,256,1024]{2,1,0:T(8,128)S(1)}, u32[]{:S(2)}, u32[]{:S(2)}) %collective-permute-start.12) | collective-permute-done | bytes 1048608 | tf_op jit(solution)/shard_map/ppermute | solution.py:28
  90.0 3.4 %collective-permute-start.13 = (f32[1,256,1024]{2,1,0:T(8,128)S(1)}, f32[1,256,1024]{2,1,0:T(8,128)S(1)}, u32[]{:S(2)}, u32[]{:S(2)}) collective-permute-start(f32[1,256,1024]{2,1,0:T(8,128)S(1)} %get-tuple-element.5), channel_id=1, source_target_pairs={{0,8},{4,12},{8,0},{12,4},{16,24},{20,28},{24,16},{28,20},{1,9},{5... | collective-permute-start | bytes 3145736 | tf_op jit(solution)/shard_map/ppermute | solution.py:34
  93.4 22.6 %collective-permute-done.13 = f32[1,256,1024]{2,1,0:T(8,128)S(1)} collective-permute-done((f32[1,256,1024]{2,1,0:T(8,128)S(1)}, f32[1,256,1024]{2,1,0:T(8,128)S(1)}, u32[]{:S(2)}, u32[]{:S(2)}) %collective-permute-start.13) | collective-permute-done | bytes 1048608 | tf_op jit(solution)/shard_map/ppermute | solution.py:34
  116.4 5.6 %collective-permute-start.16 = (f32[1,256,1024]{2,1,0:T(8,128)S(1)}, f32[1,256,1024]{2,1,0:T(8,128)S(1)}, u32[]{:S(2)}, u32[]{:S(2)}) collective-permute-start(f32[1,256,1024]{2,1,0:T(8,128)S(1)} %get-tuple-element.14), channel_id=1, source_target_pairs={{0,16},{4,20},{8,24},{12,28},{1,17},{5,21},{9,25},{13,29},{2,18},{... | collective-permute-start | bytes 3145736 | tf_op jit(solution)/shard_map/ppermute | solution.py:28
  123.4 4.5 %collective-permute-start.15 = (f32[1,1,1024]{2,1,0:T(1,128)S(1)}, f32[1,1,1024]{2,1,0:T(1,128)S(1)}, u32[]{:S(2)}, u32[]{:S(2)}) collective-permute-start(f32[1,1,1024]{2,1,0:T(1,128)S(1)} %get-tuple-element.44), channel_id=1, source_target_pairs={{0,1},{1,2},{2,3},{4,5},{5,6},{6,7},{8,9},{9,10},{10,11},{12,13},{... | collective-permute-start | bytes 12296 | tf_op jit(solution)/shard_map/ppermute | solution.py:17
  129.7 13.3 %collective-permute-done.16 = f32[1,256,1024]{2,1,0:T(8,128)S(1)} collective-permute-done((f32[1,256,1024]{2,1,0:T(8,128)S(1)}, f32[1,256,1024]{2,1,0:T(8,128)S(1)}, u32[]{:S(2)}, u32[]{:S(2)}) %collective-permute-start.16) | collective-permute-done | bytes 1048608 | tf_op jit(solution)/shard_map/ppermute | solution.py:28
  144.4 2.5 collective-permute-start.17
  146.9 20.9 %collective-permute-done.17 = f32[1,256,1024]{2,1,0:T(8,128)S(1)} collective-permute-done((f32[1,256,1024]{2,1,0:T(8,128)S(1)}, f32[1,256,1024]{2,1,0:T(8,128)S(1)}, u32[]{:S(2)}, u32[]{:S(2)}) %collective-permute-start.17) | collective-permute-done | bytes 1048608 | tf_op jit(solution)/shard_map/ppermute | solution.py:34
  170.2 4.7 %collective-permute-start.19 = (f32[1,1,1024]{2,1,0:T(1,128)S(1)}, f32[1,1,1024]{2,1,0:T(1,128)S(1)}, u32[]{:S(2)}, u32[]{:S(2)}) collective-permute-start(f32[1,1,1024]{2,1,0:T(1,128)S(1)} %get-tuple-element.42), channel_id=1, source_target_pairs={{0,1},{1,2},{2,3},{4,5},{5,6},{6,7},{8,9},{9,10},{10,11},{12,13},{... | collective-permute-start | bytes 12296 | tf_op jit(solution)/shard_map/ppermute | solution.py:17
  178.5 3.7 %collective-permute-start.23 = (f32[1,256,1024]{2,1,0:T(8,128)S(1)}, f32[1,256,1024]{2,1,0:T(8,128)S(1)}, u32[]{:S(2)}, u32[]{:S(2)}) collective-permute-start(f32[1,256,1024]{2,1,0:T(8,128)S(1)} %get-tuple-element.10), channel_id=1, source_target_pairs={{0,16},{4,20},{8,24},{12,28},{1,17},{5,21},{9,25},{13,29},{2,18},{... | collective-permute-start | bytes 3145736 | tf_op jit(solution)/shard_map/ppermute | solution.py:28
  183.5 4.8 %collective-permute-start.22 = (f32[1,1,1024]{2,1,0:T(1,128)S(1)}, f32[1,1,1024]{2,1,0:T(1,128)S(1)}, u32[]{:S(2)}, u32[]{:S(2)}) collective-permute-start(f32[1,1,1024]{2,1,0:T(1,128)S(1)} %get-tuple-element.40), channel_id=1, source_target_pairs={{0,1},{1,2},{2,3},{4,5},{5,6},{6,7},{8,9},{9,10},{10,11},{12,13},{... | collective-permute-start | bytes 12296 | tf_op jit(solution)/shard_map/ppermute | solution.py:17
  190.0 10.2 %collective-permute-done.23 = f32[1,256,1024]{2,1,0:T(8,128)S(1)} collective-permute-done((f32[1,256,1024]{2,1,0:T(8,128)S(1)}, f32[1,256,1024]{2,1,0:T(8,128)S(1)}, u32[]{:S(2)}, u32[]{:S(2)}) %collective-permute-start.23) | collective-permute-done | bytes 1048608 | tf_op jit(solution)/shard_map/ppermute | solution.py:28
  201.4 3.1 collective-permute-start.26
  205.8 4.5 %collective-permute-start.25 = (f32[1,1,1024]{2,1,0:T(1,128)S(1)}, f32[1,1,1024]{2,1,0:T(1,128)S(1)}, u32[]{:S(2)}, u32[]{:S(2)}) collective-permute-start(f32[1,1,1024]{2,1,0:T(1,128)S(1)} %get-tuple-element.38), channel_id=1, source_target_pairs={{0,1},{1,2},{2,3},{4,5},{5,6},{6,7},{8,9},{9,10},{10,11},{12,13},{... | collective-permute-start | bytes 12296 | tf_op jit(solution)/shard_map/ppermute | solution.py:17
  212.1 9.9 %collective-permute-done.26 = f32[1,256,1024]{2,1,0:T(8,128)S(1)} collective-permute-done((f32[1,256,1024]{2,1,0:T(8,128)S(1)}, f32[1,256,1024]{2,1,0:T(8,128)S(1)}, u32[]{:S(2)}, u32[]{:S(2)}) %collective-permute-start.26) | collective-permute-done | bytes 1048608 | tf_op jit(solution)/shard_map/ppermute | solution.py:28
  225.6 4.5 %collective-permute-start.28 = (f32[1,1,1024]{2,1,0:T(1,128)S(1)}, f32[1,1,1024]{2,1,0:T(1,128)S(1)}, u32[]{:S(2)}, u32[]{:S(2)}) collective-permute-start(f32[1,1,1024]{2,1,0:T(1,128)S(1)} %get-tuple-element.36), channel_id=1, source_target_pairs={{0,1},{1,2},{2,3},{4,5},{5,6},{6,7},{8,9},{9,10},{10,11},{12,13},{... | collective-permute-start | bytes 12296 | tf_op jit(solution)/shard_map/ppermute | solution.py:17
  234.7 10.2 %collective-permute-start.32 = (f32[1,256,1024]{2,1,0:T(8,128)}, f32[1,256,1024]{2,1,0:T(8,128)}, u32[]{:S(2)}, u32[]{:S(2)}) collective-permute-start(f32[1,256,1024]{2,1,0:T(8,128)} %get-tuple-element.22), channel_id=1, source_target_pairs={{0,4},{4,8},{8,12},{12,16},{16,20},{20,24},{24,28},{1,5},{5,9},{9,... | collective-permute-start | bytes 3145736 | tf_op jit(solution)/shard_map/ppermute | solution.py:28
  247.4 4.5 %collective-permute-start.31 = (f32[2,1,1024]{2,1,0:T(1,128)S(1)}, f32[2,1,1024]{2,1,0:T(1,128)S(1)}, u32[]{:S(2)}, u32[]{:S(2)}) collective-permute-start(f32[2,1,1024]{2,1,0:T(1,128)S(1)} %get-tuple-element.24), channel_id=1, source_target_pairs={{0,1},{1,2},{2,3},{4,5},{5,6},{6,7},{8,9},{9,10},{10,11},{12,13},{... | collective-permute-start | bytes 24584 | tf_op jit(solution)/shard_map/ppermute | solution.py:17
  254.8 4.8 %collective-permute-start.34 = (f32[1,1,1024]{2,1,0:T(1,128)S(1)}, f32[1,1,1024]{2,1,0:T(1,128)S(1)}, u32[]{:S(2)}, u32[]{:S(2)}) collective-permute-start(f32[1,1,1024]{2,1,0:T(1,128)S(1)} %get-tuple-element.34), channel_id=1, source_target_pairs={{0,1},{1,2},{2,3},{4,5},{5,6},{6,7},{8,9},{9,10},{10,11},{12,13},{... | collective-permute-start | bytes 12296 | tf_op jit(solution)/shard_map/ppermute | solution.py:17
  260.5 2.9 fusion.14
  265.0 3.4 %collective-permute-start.38 = (f32[1,256,1024]{2,1,0:T(8,128)}, f32[1,256,1024]{2,1,0:T(8,128)}, u32[]{:S(2)}, u32[]{:S(2)}) collective-permute-start(f32[1,256,1024]{2,1,0:T(8,128)} %get-tuple-element.18), channel_id=1, source_target_pairs={{0,4},{4,8},{8,12},{12,16},{16,20},{20,24},{24,28},{1,5},{5,9},{9,... | collective-permute-start | bytes 3145736 | tf_op jit(solution)/shard_map/ppermute | solution.py:28
  270.1 4.9 %collective-permute-start.37 = (f32[2,1,1024]{2,1,0:T(1,128)S(1)}, f32[2,1,1024]{2,1,0:T(1,128)S(1)}, u32[]{:S(2)}, u32[]{:S(2)}) collective-permute-start(f32[2,1,1024]{2,1,0:T(1,128)S(1)} %get-tuple-element.20), channel_id=1, source_target_pairs={{0,1},{1,2},{2,3},{4,5},{5,6},{6,7},{8,9},{9,10},{10,11},{12,13},{... | collective-permute-start | bytes 24584 | tf_op jit(solution)/shard_map/ppermute | solution.py:17
  279.4 3.3 %fusion.6 = f32[]{:T(128)} fusion(f32[2,256,1024]{2,1,0:T(8,128)S(1)} %copy-done.5, f32[2,258,1026]{2,1,0:T(8,128)S(1)} %select_maximum_fusion, f32[2,256,1024]{2,1,0:T(8,128)S(1)} %copy-done.2, f32[2,1,1024]{2,1,0:T(1,128)S(1)} %collective-permute-done.37, f32[2,1,1024]{2,1,0:T(1,128)S(1)} %collective-permute-done.36, f32[1,256,1024]{2,1,0:T(8,128)S(1)} %copy-done.14, ...), kind=kLoop, calls=%fused_computation.17 | loop fusion | flops 6815743 | bytes 12599300 | tf_op jit(solution)/shard_map/reduce_sum | solution.py:70
  284.7 44.9 %psum.7 = f32[6]{0:T(128)S(1)} all-reduce(f32[6]{0:T(128)S(1)} %stack.27), channel_id=1, replica_groups=mesh['tm'=8,'space'=4] {'tm','space'}, use_global_device_ids=true, to_apply=%region_6.7 | all-reduce | flops 6 | bytes 48 | tf_op jit(solution)/shard_map/psum | solution.py:114
  (125 shorter events, 67.9 us)
Async XLA Ops:
  2.5 10.9 %collective-permute-start.2 = (f32[1,256,1024]{2,1,0:T(8,128)S(1)}, f32[1,256,1024]{2,1,0:T(8,128)S(1)}, u32[]{:S(2)}, u32[]{:S(2)}) collective-permute-start(f32[1,256,1024]{2,1,0:T(8,128)S(1)} %get-tuple-element.30), channel_id=1, source_target_pairs={{0,4},{4,8},{8,12},{12,16},{16,20},{20,24},{24,28},{1,5},{5,9},{9,... | collective-permute-start | bytes 3145736 | tf_op jit(solution)/shard_map/ppermute | solution.py:28
  5.0 6.4 %collective-permute-start = (f32[2,1,1024]{2,1,0:T(1,128)S(1)}, f32[2,1,1024]{2,1,0:T(1,128)S(1)}, u32[]{:S(2)}, u32[]{:S(2)}) collective-permute-start(f32[2,1,1024]{2,1,0:T(1,128)S(1)} %get-tuple-element.33), channel_id=1, source_target_pairs={{1,0},{2,1},{3,2},{5,4},{6,5},{7,6},{9,8},{10,9},{11,10},{13,12},{... | collective-permute-start | bytes 24584 | tf_op jit(solution)/shard_map/ppermute | solution.py:20
  6.3 6.3 %collective-permute-start.1 = (f32[2,1,1024]{2,1,0:T(1,128)S(1)}, f32[2,1,1024]{2,1,0:T(1,128)S(1)}, u32[]{:S(2)}, u32[]{:S(2)}) collective-permute-start(f32[2,1,1024]{2,1,0:T(1,128)S(1)} %get-tuple-element.32), channel_id=1, source_target_pairs={{0,1},{1,2},{2,3},{4,5},{5,6},{6,7},{8,9},{9,10},{10,11},{12,13},{... | collective-permute-start | bytes 24584 | tf_op jit(solution)/shard_map/ppermute | solution.py:17
  15.5 15.8 %collective-permute-start.5 = (f32[1,256,1024]{2,1,0:T(8,128)S(1)}, f32[1,256,1024]{2,1,0:T(8,128)S(1)}, u32[]{:S(2)}, u32[]{:S(2)}) collective-permute-start(f32[1,256,1024]{2,1,0:T(8,128)S(1)} %get-tuple-element.28), channel_id=1, source_target_pairs={{0,4},{4,8},{8,12},{12,16},{16,20},{20,24},{24,28},{1,5},{5,9},{9,... | collective-permute-start | bytes 3145736 | tf_op jit(solution)/shard_map/ppermute | solution.py:28
  24.6 5.9 %collective-permute-start.4 = (f32[2,1,1024]{2,1,0:T(1,128)S(1)}, f32[2,1,1024]{2,1,0:T(1,128)S(1)}, u32[]{:S(2)}, u32[]{:S(2)}) collective-permute-start(f32[2,1,1024]{2,1,0:T(1,128)S(1)} %get-tuple-element.26), channel_id=1, source_target_pairs={{0,1},{1,2},{2,3},{4,5},{5,6},{6,7},{8,9},{9,10},{10,11},{12,13},{... | collective-permute-start | bytes 24584 | tf_op jit(solution)/shard_map/ppermute | solution.py:17
  34.0 15.7 %collective-permute-start.8 = (f32[1,256,1024]{2,1,0:T(8,128)S(1)}, f32[1,256,1024]{2,1,0:T(8,128)S(1)}, u32[]{:S(2)}, u32[]{:S(2)}) collective-permute-start(f32[1,256,1024]{2,1,0:T(8,128)S(1)} %bitcast_divide_fusion.3), channel_id=1, source_target_pairs={{0,4},{4,8},{8,12},{12,16},{16,20},{20,24},{24,28},{1,5},{5,9},{9,... | collective-permute-start | bytes 3145736 | tf_op jit(solution)/shard_map/ppermute | solution.py:28
  43.4 5.9 %collective-permute-start.7 = (f32[1,1,1024]{2,1,0:T(1,128)S(1)}, f32[1,1,1024]{2,1,0:T(1,128)S(1)}, u32[]{:S(2)}, u32[]{:S(2)}) collective-permute-start(f32[1,1,1024]{2,1,0:T(1,128)S(1)} %get-tuple-element.48), channel_id=1, source_target_pairs={{0,1},{1,2},{2,3},{4,5},{5,6},{6,7},{8,9},{9,10},{10,11},{12,13},{... | collective-permute-start | bytes 12296 | tf_op jit(solution)/shard_map/ppermute | solution.py:17
  51.2 8.8 %collective-permute-start.9 = (f32[1,256,1024]{2,1,0:T(8,128)S(1)}, f32[1,256,1024]{2,1,0:T(8,128)S(1)}, u32[]{:S(2)}, u32[]{:S(2)}) collective-permute-start(f32[1,256,1024]{2,1,0:T(8,128)S(1)} %get-tuple-element.7), channel_id=1, source_target_pairs={{0,4},{4,0},{8,12},{12,8},{16,20},{20,16},{24,28},{28,24},{1,5},{5... | collective-permute-start | bytes 3145736 | tf_op jit(solution)/shard_map/ppermute | solution.py:34
  60.4 28.1 %collective-permute-start.12 = (f32[1,256,1024]{2,1,0:T(8,128)S(1)}, f32[1,256,1024]{2,1,0:T(8,128)S(1)}, u32[]{:S(2)}, u32[]{:S(2)}) collective-permute-start(f32[1,256,1024]{2,1,0:T(8,128)S(1)} %get-tuple-element.16), channel_id=1, source_target_pairs={{0,8},{4,12},{8,16},{12,20},{16,24},{20,28},{1,9},{5,13},{9,17},{1... | collective-permute-start | bytes 3145736 | tf_op jit(solution)/shard_map/ppermute | solution.py:28
  67.0 5.9 %collective-permute-start.11 = (f32[1,1,1024]{2,1,0:T(1,128)S(1)}, f32[1,1,1024]{2,1,0:T(1,128)S(1)}, u32[]{:S(2)}, u32[]{:S(2)}) collective-permute-start(f32[1,1,1024]{2,1,0:T(1,128)S(1)} %get-tuple-element.46), channel_id=1, source_target_pairs={{0,1},{1,2},{2,3},{4,5},{5,6},{6,7},{8,9},{9,10},{10,11},{12,13},{... | collective-permute-start | bytes 12296 | tf_op jit(solution)/shard_map/ppermute | solution.py:17
  90.0 26.0 %collective-permute-start.13 = (f32[1,256,1024]{2,1,0:T(8,128)S(1)}, f32[1,256,1024]{2,1,0:T(8,128)S(1)}, u32[]{:S(2)}, u32[]{:S(2)}) collective-permute-start(f32[1,256,1024]{2,1,0:T(8,128)S(1)} %get-tuple-element.5), channel_id=1, source_target_pairs={{0,8},{4,12},{8,0},{12,4},{16,24},{20,28},{24,16},{28,20},{1,9},{5... | collective-permute-start | bytes 3145736 | tf_op jit(solution)/shard_map/ppermute | solution.py:34
  116.4 26.6 %collective-permute-start.16 = (f32[1,256,1024]{2,1,0:T(8,128)S(1)}, f32[1,256,1024]{2,1,0:T(8,128)S(1)}, u32[]{:S(2)}, u32[]{:S(2)}) collective-permute-start(f32[1,256,1024]{2,1,0:T(8,128)S(1)} %get-tuple-element.14), channel_id=1, source_target_pairs={{0,16},{4,20},{8,24},{12,28},{1,17},{5,21},{9,25},{13,29},{2,18},{... | collective-permute-start | bytes 3145736 | tf_op jit(solution)/shard_map/ppermute | solution.py:28
  123.4 5.9 %collective-permute-start.15 = (f32[1,1,1024]{2,1,0:T(1,128)S(1)}, f32[1,1,1024]{2,1,0:T(1,128)S(1)}, u32[]{:S(2)}, u32[]{:S(2)}) collective-permute-start(f32[1,1,1024]{2,1,0:T(1,128)S(1)} %get-tuple-element.44), channel_id=1, source_target_pairs={{0,1},{1,2},{2,3},{4,5},{5,6},{6,7},{8,9},{9,10},{10,11},{12,13},{... | collective-permute-start | bytes 12296 | tf_op jit(solution)/shard_map/ppermute | solution.py:17
  144.4 23.4 %collective-permute-start.17 = (f32[1,256,1024]{2,1,0:T(8,128)S(1)}, f32[1,256,1024]{2,1,0:T(8,128)S(1)}, u32[]{:S(2)}, u32[]{:S(2)}) collective-permute-start(f32[1,256,1024]{2,1,0:T(8,128)S(1)} %get-tuple-element.3), channel_id=1, source_target_pairs={{0,16},{4,20},{8,24},{12,28},{16,0},{20,4},{24,8},{28,12},{1,17},{... | collective-permute-start | bytes 3145736 | tf_op jit(solution)/shard_map/ppermute | solution.py:34
  168.2 8.3 %collective-permute-start.20 = (f32[1,256,1024]{2,1,0:T(8,128)S(1)}, f32[1,256,1024]{2,1,0:T(8,128)S(1)}, u32[]{:S(2)}, u32[]{:S(2)}) collective-permute-start(f32[1,256,1024]{2,1,0:T(8,128)S(1)} %get-tuple-element.12), channel_id=1, source_target_pairs={} | collective-permute-start | bytes 3145736 | tf_op jit(solution)/shard_map/ppermute | solution.py:28
  168.9 6.0 %collective-permute-start.18 = (f32[1,1,1024]{2,1,0:T(1,128)S(1)}, f32[1,1,1024]{2,1,0:T(1,128)S(1)}, u32[]{:S(2)}, u32[]{:S(2)}) collective-permute-start(f32[1,1,1024]{2,1,0:T(1,128)S(1)} %get-tuple-element.43), channel_id=1, source_target_pairs={{1,0},{2,1},{3,2},{5,4},{6,5},{7,6},{9,8},{10,9},{11,10},{13,12},{... | collective-permute-start | bytes 12296 | tf_op jit(solution)/shard_map/ppermute | solution.py:20
  170.2 5.9 %collective-permute-start.19 = (f32[1,1,1024]{2,1,0:T(1,128)S(1)}, f32[1,1,1024]{2,1,0:T(1,128)S(1)}, u32[]{:S(2)}, u32[]{:S(2)}) collective-permute-start(f32[1,1,1024]{2,1,0:T(1,128)S(1)} %get-tuple-element.42), channel_id=1, source_target_pairs={{0,1},{1,2},{2,3},{4,5},{5,6},{6,7},{8,9},{9,10},{10,11},{12,13},{... | collective-permute-start | bytes 12296 | tf_op jit(solution)/shard_map/ppermute | solution.py:17
  178.5 21.8 %collective-permute-start.23 = (f32[1,256,1024]{2,1,0:T(8,128)S(1)}, f32[1,256,1024]{2,1,0:T(8,128)S(1)}, u32[]{:S(2)}, u32[]{:S(2)}) collective-permute-start(f32[1,256,1024]{2,1,0:T(8,128)S(1)} %get-tuple-element.10), channel_id=1, source_target_pairs={{0,16},{4,20},{8,24},{12,28},{1,17},{5,21},{9,25},{13,29},{2,18},{... | collective-permute-start | bytes 3145736 | tf_op jit(solution)/shard_map/ppermute | solution.py:28
  182.2 6.1 %collective-permute-start.21 = (f32[1,1,1024]{2,1,0:T(1,128)S(1)}, f32[1,1,1024]{2,1,0:T(1,128)S(1)}, u32[]{:S(2)}, u32[]{:S(2)}) collective-permute-start(f32[1,1,1024]{2,1,0:T(1,128)S(1)} %get-tuple-element.41), channel_id=1, source_target_pairs={{1,0},{2,1},{3,2},{5,4},{6,5},{7,6},{9,8},{10,9},{11,10},{13,12},{... | collective-permute-start | bytes 12296 | tf_op jit(solution)/shard_map/ppermute | solution.py:20
  183.5 6.1 %collective-permute-start.22 = (f32[1,1,1024]{2,1,0:T(1,128)S(1)}, f32[1,1,1024]{2,1,0:T(1,128)S(1)}, u32[]{:S(2)}, u32[]{:S(2)}) collective-permute-start(f32[1,1,1024]{2,1,0:T(1,128)S(1)} %get-tuple-element.40), channel_id=1, source_target_pairs={{0,1},{1,2},{2,3},{4,5},{5,6},{6,7},{8,9},{9,10},{10,11},{12,13},{... | collective-permute-start | bytes 12296 | tf_op jit(solution)/shard_map/ppermute | solution.py:17
  201.4 20.6 %collective-permute-start.26 = (f32[1,256,1024]{2,1,0:T(8,128)S(1)}, f32[1,256,1024]{2,1,0:T(8,128)S(1)}, u32[]{:S(2)}, u32[]{:S(2)}) collective-permute-start(f32[1,256,1024]{2,1,0:T(8,128)S(1)} %fusion.61), channel_id=1, source_target_pairs={{0,8},{4,12},{8,16},{12,20},{16,24},{20,28},{1,9},{5,13},{9,17},{1... | collective-permute-start | bytes 3145736 | tf_op jit(solution)/shard_map/ppermute | solution.py:28
  205.8 5.9 %collective-permute-start.25 = (f32[1,1,1024]{2,1,0:T(1,128)S(1)}, f32[1,1,1024]{2,1,0:T(1,128)S(1)}, u32[]{:S(2)}, u32[]{:S(2)}) collective-permute-start(f32[1,1,1024]{2,1,0:T(1,128)S(1)} %get-tuple-element.38), channel_id=1, source_target_pairs={{0,1},{1,2},{2,3},{4,5},{5,6},{6,7},{8,9},{9,10},{10,11},{12,13},{... | collective-permute-start | bytes 12296 | tf_op jit(solution)/shard_map/ppermute | solution.py:17
  223.0 9.0 %collective-permute-start.29 = (f32[1,256,1024]{2,1,0:T(8,128)S(1)}, f32[1,256,1024]{2,1,0:T(8,128)S(1)}, u32[]{:S(2)}, u32[]{:S(2)}) collective-permute-start(f32[1,256,1024]{2,1,0:T(8,128)S(1)} %fusion.52), channel_id=1, source_target_pairs={{0,4},{4,8},{8,12},{12,16},{16,20},{20,24},{24,28},{1,5},{5,9},{9,... | collective-permute-start | bytes 3145736 | tf_op jit(solution)/shard_map/ppermute | solution.py:28
  234.7 25.8 %collective-permute-start.32 = (f32[1,256,1024]{2,1,0:T(8,128)}, f32[1,256,1024]{2,1,0:T(8,128)}, u32[]{:S(2)}, u32[]{:S(2)}) collective-permute-start(f32[1,256,1024]{2,1,0:T(8,128)} %get-tuple-element.22), channel_id=1, source_target_pairs={{0,4},{4,8},{8,12},{12,16},{16,20},{20,24},{24,28},{1,5},{5,9},{9,... | collective-permute-start | bytes 3145736 | tf_op jit(solution)/shard_map/ppermute | solution.py:28
  246.1 8.7 %collective-permute-start.30 = (f32[2,1,1024]{2,1,0:T(1,128)S(1)}, f32[2,1,1024]{2,1,0:T(1,128)S(1)}, u32[]{:S(2)}, u32[]{:S(2)}) collective-permute-start(f32[2,1,1024]{2,1,0:T(1,128)S(1)} %get-tuple-element.25), channel_id=1, source_target_pairs={{1,0},{2,1},{3,2},{5,4},{6,5},{7,6},{9,8},{10,9},{11,10},{13,12},{... | collective-permute-start | bytes 24584 | tf_op jit(solution)/shard_map/ppermute | solution.py:20
  247.4 12.2 %collective-permute-start.31 = (f32[2,1,1024]{2,1,0:T(1,128)S(1)}, f32[2,1,1024]{2,1,0:T(1,128)S(1)}, u32[]{:S(2)}, u32[]{:S(2)}) collective-permute-start(f32[2,1,1024]{2,1,0:T(1,128)S(1)} %get-tuple-element.24), channel_id=1, source_target_pairs={{0,1},{1,2},{2,3},{4,5},{5,6},{6,7},{8,9},{9,10},{10,11},{12,13},{... | collective-permute-start | bytes 24584 | tf_op jit(solution)/shard_map/ppermute | solution.py:17
  252.7 22.3 %collective-permute-start.35 = (f32[1,256,1024]{2,1,0:T(8,128)}, f32[1,256,1024]{2,1,0:T(8,128)S(1)}, u32[]{:S(2)}, u32[]{:S(2)}) collective-permute-start(f32[1,256,1024]{2,1,0:T(8,128)} %get-tuple-element.11), channel_id=1, source_target_pairs={} | collective-permute-start | bytes 3145736 | tf_op jit(solution)/shard_map/ppermute | solution.py:28
  253.5 14.9 %collective-permute-start.33 = (f32[1,1,1024]{2,1,0:T(1,128)S(1)}, f32[1,1,1024]{2,1,0:T(1,128)S(1)}, u32[]{:S(2)}, u32[]{:S(2)}) collective-permute-start(f32[1,1,1024]{2,1,0:T(1,128)S(1)} %get-tuple-element.35), channel_id=1, source_target_pairs={{1,0},{2,1},{3,2},{5,4},{6,5},{7,6},{9,8},{10,9},{11,10},{13,12},{... | collective-permute-start | bytes 12296 | tf_op jit(solution)/shard_map/ppermute | solution.py:20
  254.8 13.6 %collective-permute-start.34 = (f32[1,1,1024]{2,1,0:T(1,128)S(1)}, f32[1,1,1024]{2,1,0:T(1,128)S(1)}, u32[]{:S(2)}, u32[]{:S(2)}) collective-permute-start(f32[1,1,1024]{2,1,0:T(1,128)S(1)} %get-tuple-element.34), channel_id=1, source_target_pairs={{0,1},{1,2},{2,3},{4,5},{5,6},{6,7},{8,9},{9,10},{10,11},{12,13},{... | collective-permute-start | bytes 12296 | tf_op jit(solution)/shard_map/ppermute | solution.py:17
  265.0 13.1 %collective-permute-start.38 = (f32[1,256,1024]{2,1,0:T(8,128)}, f32[1,256,1024]{2,1,0:T(8,128)}, u32[]{:S(2)}, u32[]{:S(2)}) collective-permute-start(f32[1,256,1024]{2,1,0:T(8,128)} %get-tuple-element.18), channel_id=1, source_target_pairs={{0,4},{4,8},{8,12},{12,16},{16,20},{20,24},{24,28},{1,5},{5,9},{9,... | collective-permute-start | bytes 3145736 | tf_op jit(solution)/shard_map/ppermute | solution.py:28
  268.8 8.4 %collective-permute-start.36 = (f32[2,1,1024]{2,1,0:T(1,128)S(1)}, f32[2,1,1024]{2,1,0:T(1,128)S(1)}, u32[]{:S(2)}, u32[]{:S(2)}) collective-permute-start(f32[2,1,1024]{2,1,0:T(1,128)S(1)} %get-tuple-element.21), channel_id=1, source_target_pairs={{1,0},{2,1},{3,2},{5,4},{6,5},{7,6},{9,8},{10,9},{11,10},{13,12},{... | collective-permute-start | bytes 24584 | tf_op jit(solution)/shard_map/ppermute | solution.py:20
  270.1 7.1 %collective-permute-start.37 = (f32[2,1,1024]{2,1,0:T(1,128)S(1)}, f32[2,1,1024]{2,1,0:T(1,128)S(1)}, u32[]{:S(2)}, u32[]{:S(2)}) collective-permute-start(f32[2,1,1024]{2,1,0:T(1,128)S(1)} %get-tuple-element.20), channel_id=1, source_target_pairs={{0,1},{1,2},{2,3},{4,5},{5,6},{6,7},{8,9},{9,10},{10,11},{12,13},{... | collective-permute-start | bytes 24584 | tf_op jit(solution)/shard_map/ppermute | solution.py:17
  (22 other events, 138.5 us)
where the time goes:
time: 331 us; the launch traced here: 330 us
  starting transfers between devices  136 us (41%)
  waiting for transfers between devices  106 us (32%)
  blocking collectives  44.9 us (14%)
  other arithmetic  30.2 us (9%)
  local copies, waits for them, and re-layouts  9.38 us (3%)
  between operations  3.35 us (1%)
    ppermute x12, starting transfers between devices, with_halo(): lax.ppermute(lax.slice_in_dim(block, block.shape[dim] - width, None, axis...  56 us
    ppermute x12, starting transfers between devices, shifted(): lax.ppermute(value, axis, [(source, source + steps) for source in range(f...  52.4 us
    ppermute x12, waiting for transfers between devices, shifted(): lax.ppermute(value, axis, [(source, source + steps) for source in range(f...  48.7 us
    ppermute x3, waiting for transfers between devices, from_partner(): return lax.ppermute(value, axis, pairs)  45.8 us
    psum x1, blocking collectives, body(): totals = lax.psum(jnp.stack(partials), ('tm', 'space'))  44.9 us
    ppermute x12, starting transfers between devices, with_halo(): lax.ppermute(lax.slice_in_dim(block, 0, width, axis=dim), axis, backward)  15.5 us
    ppermute x3, starting transfers between devices, from_partner(): return lax.ppermute(value, axis, pairs)  12.4 us
    reduce_sum x6, other arithmetic, record(): local_part = jnp.sum(resid * resid) * weight_of(level)  11.6 us
  transfers between devices with their start and end apart: 39, of which 16 were waited for; matrix products, arithmetic and copies ran while one was open for 4% of the time, Pallas kernels for 0%

commit v1 on v0

v1 whole, which is shorter than its diff:
```python
import functools
import jax
import jax.numpy as jnp
from jax import lax
from jax.experimental import pallas as pl
from jax.experimental.pallas import tpu as pltpu
from jax.sharding import PartitionSpec as P

LEVELS = 5
DAMPING = 0.8
KEEP = 1.0 - DAMPING
GROUP = 2 ** (LEVELS - 1)
TEAM = GROUP // 2
HALO = 2 * LEVELS + 1
EDGE = 2
REACH = 2 * LEVELS - 3


def vmem():
    return pl.BlockSpec(memory_space=pltpu.VMEM)


def shape(*dims):
    return jax.ShapeDtypeStruct(dims, jnp.float32)


def kernel_call(body, outs, scratch=(), flops=0, n_in=0, specs=None, grid=()):
    return pl.pallas_call(
        body,
        out_shape=outs,
        grid=grid,
        in_specs=specs or [vmem() for _ in range(n_in)],
        out_specs=[vmem() for _ in outs],
        scratch_shapes=[pltpu.VMEM(dims, jnp.float32) for dims in scratch],
        compiler_params=pltpu.CompilerParams(vmem_limit_bytes=56 * 2**20),
        cost_estimate=pl.CostEstimate(flops=flops, bytes_accessed=flops, transcendentals=0),
    )


def tiles(block):
    lead = block.shape[:-2]
    rows, cells = block.shape[-2:]
    split = block.reshape(*lead, rows // 8, 8, cells // 128, 128)
    return jnp.swapaxes(split, -3, -2).reshape(*lead, rows // 8, cells // 16, 128)


def untiles(block):
    lead = block.shape[:-3]
    groups, wide, _ = block.shape[-3:]
    split = block.reshape(*lead, groups, wide // 8, 8, 128)
    return jnp.swapaxes(split, -3, -2).reshape(*lead, groups * 8, wide * 16)


def masks():
    sub = lax.broadcasted_iota(jnp.int32, (8, 128), 0)
    lane = lax.broadcasted_iota(jnp.int32, (8, 128), 1)
    first = lane == 0
    last = lane == 127
    return first, last, first & (sub == 0), last & (sub == 7)


def beside(row, m):
    first, last, left_end, right_end = m
    left = pltpu.roll(row, 1, 1)
    left = jnp.where(first, pltpu.roll(left, 1, 0), left)
    right = pltpu.roll(row, 127, 1)
    right = jnp.where(last, pltpu.roll(right, 7, 0), right)
    return jnp.where(left_end, 0.0, left) + jnp.where(right_end, 0.0, right)


def around(ref, row, m):
    return beside(ref[row], m) + (ref[row - 1] + ref[row + 1])


def loop(low, high, body, carry=None, unroll=4):
    if carry is None:
        lax.fori_loop(low, high, lambda i, c: (body(i), c)[1], 0, unroll=unroll)
        return None
    return lax.fori_loop(low, high, body, carry, unroll=unroll)


def strided(ref, lead, row_group, k):
    return ref[lead + (row_group, pl.ds(k, 8, stride=8))]


def unpack_rows(src, lead, dst, offset, rows):
    def group(g):
        for k in range(8):
            dst[offset + g * 8 + k] = strided(src, lead, g, k)

    loop(0, rows // 8, group, unroll=2)


def pack_edges(g_top, r_top, d_top, g_end, r_end, d_end, top, end):
    count = g_top.shape[1] * 8

    def row_of(ref, lead, row):
        return strided(ref, lead, row // 8, row % 8)

    refs = [((g_top, (t,)), (g_end, (t,))) for t in range(2)]
    refs += [((r_top, (t,)), (r_end, (t,))) for t in range(2)]
    refs += [((d_top, ()), (d_end, ()))]
    for i, ((a, lead_a), (b, lead_b)) in enumerate(refs):
        for k in range(HALO):
            top[i * HALO + k] = row_of(a, lead_a, k)
            end[i * HALO + k] = row_of(b, lead_b, count - HALO + k)


def first_sweep(guess, rhs, diff, low, high, s_ext, w_ext, send, g0, g1):
    rows = guess.shape[1] * 8
    m = masks()
    unpack_rows(diff, (), s_ext, HALO, rows)
    unpack_rows(guess, (0,), g0, HALO, rows)
    unpack_rows(guess, (1,), g1, HALO, rows)
    for k in range(HALO):
        for dst, i in ((g0, 0), (g1, 1), (s_ext, 4)):
            dst[k] = low[i * HALO + k]
            dst[HALO + rows + k] = high[i * HALO + k]

    def weight(i):
        w_ext[i] = DAMPING / (1.0 + 4.0 * s_ext[i])

    loop(0, rows + 2 * HALO, weight)

    def sweep(i, source):
        return KEEP * g1[i] + w_ext[i] * (source + s_ext[i] * around(g1, i, m) + g0[i])

    def inner(g):
        for k in range(8):
            i = HALO + g * 8 + k
            send[i - 2] = sweep(i, strided(rhs, (1,), g, k))

    loop(0, rows // 8, inner, unroll=1)
    for k in range(2, HALO):
        send[k - 2] = sweep(k, low[3 * HALO + k])
    for k in range(0, HALO - 2):
        i = HALO + rows + k
        send[i - 2] = sweep(i, high[3 * HALO + k])
    tail = rows + 2 * (HALO - 2)
    for k in range(HALO - 1):
        send[tail + k] = g1[1 + k]
        send[tail + HALO - 1 + k] = g1[HALO + rows + k]


def local_parts(rhs, low, high, s_ext, w_ext, g0, g1, part0, left0, left1, v1):
    rows = rhs.shape[1] * 8
    m = masks()

    def sweep0(i, source):
        return KEEP * g0[i] + w_ext[i] * (source + s_ext[i] * around(g0, i, m))

    def sweep1(i, source):
        return KEEP * g1[i] + w_ext[i] * (source + s_ext[i] * around(g1, i, m) + g0[i])

    def fill(i, a, b):
        part0[i] = sweep0(i, a)
        v1[i] = sweep1(i, b)

    def inner(g):
        for k in range(8):
            fill(HALO + g * 8 + k, strided(rhs, (0,), g, k), strided(rhs, (1,), g, k))

    loop(0, rows // 8, inner, unroll=1)
    for k in range(1, HALO):
        fill(k, low[2 * HALO + k], low[3 * HALO + k])
    for k in range(0, HALO - 1):
        fill(HALO + rows + k, high[2 * HALO + k], high[3 * HALO + k])

    def rest(i, a, b):
        s = s_ext[i]
        diag = 1.0 + 4.0 * s
        left0[i] = a - diag * part0[i] + s * around(part0, i, m)
        left1[i] = b - diag * v1[i] + s * around(v1, i, m) + part0[i]

    def inner2(g):
        for k in range(8):
            rest(HALO + g * 8 + k, strided(rhs, (0,), g, k), strided(rhs, (1,), g, k))

    loop(0, rows // 8, inner2, unroll=1)
    for k in range(2, HALO):
        rest(k, low[2 * HALO + k], low[3 * HALO + k])
    for k in range(0, HALO - 2):
        rest(HALO + rows + k, high[2 * HALO + k], high[3 * HALO + k])


def windows_of(rows):
    piece = -(-(rows + 2 * EDGE) // TEAM)
    spare = rows + 2 * EDGE - piece
    starts = [-EDGE + j * spare // (TEAM - 1) for j in range(TEAM)]
    return piece, piece + 2 * REACH, starts


def join_first(starts, window, g_prev, got, s_ext, w_ext, part0, left0, left1, v1, out, base0, base1, back, norm, y, coarse):
    rows = g_prev.shape[0] * 8
    m = masks()
    tail = rows + 2 * (HALO - 2)

    def inner(g):
        for k in range(8):
            i = HALO + g * 8 + k
            y[i] = w_ext[i] * strided(g_prev, (), g, k)

    loop(0, rows // 8, inner, unroll=1)
    for k in range(HALO - 1):
        i = 1 + k
        y[i] = w_ext[i] * got[tail + k]
        i = HALO + rows + k
        y[i] = w_ext[i] * got[tail + HALO - 1 + k]

    def resid(i):
        s = s_ext[i]
        here = y[i]
        a = left0[i] - (1.0 + 4.0 * s) * here + s * around(y, i, m) + got[i - 2]
        return a, left1[i] + here

    def edge(i):
        a, b = resid(i)
        coarse[i] = a + b
        return a, b

    def based(i, a, b):
        w = w_ext[i]
        base0[i - HALO + 1] = part0[i] + y[i] + w * a
        value = v1[i] + w * b
        base1[i - HALO + 1] = value
        return value

    def main(i, acc):
        a, b = edge(i)
        back[i - HALO] = based(i, a, b)
        return acc + (a * a + b * b)

    norm[...] = loop(HALO, HALO + rows, main, jnp.zeros((8, 128), jnp.float32))
    for i in (HALO - 1, HALO + rows):
        a, b = edge(i)
        based(i, a, b)
    for i in list(range(2, HALO - 1)) + list(range(HALO + rows + 1, 2 * HALO + rows - 2)):
        edge(i)
    for j, start in enumerate(starts):
        low = start - REACH + HALO

        def copy(i, j=j, low=low):
            out[j, i] = coarse[low + i]

        loop(0, window, copy)


def coarse_levels(starts, rows, where, g_in, s_ext, out, norms, s_win, w_win, v_ref, e_ref, *bases):
    window = g_in.shape[1]
    piece = window - 2 * REACH
    m = masks()
    place = where[0]
    start = -EDGE + place * (rows + 2 * EDGE - piece) // (TEAM - 1) - REACH
    first_own = place * (rows // TEAM) - start
    last_own = first_own + rows // TEAM

    def level_weights(i):
        s = s_ext[start + HALO + i]
        s_win[i] = s
        for level in range(1, LEVELS):
            w_win[level - 1, i] = DAMPING / (1.0 + 4.0 * 2.0**level * s)

    loop(0, window, level_weights, unroll=2)

    def own(i):
        return jnp.where((i >= first_own) & (i < last_own), 1.0, 0.0).astype(jnp.float32)

    source = g_in
    zero = jnp.zeros((8, 128), jnp.float32)
    for level in range(1, LEVELS - 1):
        points = TEAM >> (level - 1)
        lost = level - 1
        base = bases[2 * (level - 1)]
        target = bases[2 * (level - 1) + 1]

        def smooth(i, level=level, points=points, source=source):
            w = w_win[level - 1, i]
            for p in range(points):
                v_ref[p, i] = w * source[p, i]

        loop(lost, window - lost, smooth, unroll=2)

        def descend(i, acc, level=level, points=points, source=source, base=base, target=target):
            s = 2.0**level * s_win[i]
            w = w_win[level - 1, i]
            pairs = []
            total = zero
            before = None
            for p in range(points):
                here = v_ref[p, i]
                r = KEEP * source[p, i] + s * (beside(here, m) + (v_ref[p, i - 1] + v_ref[p, i + 1]))
                if before is not None:
                    r = r + before
                base[p, i] = here + w * r
                total = total + r * r
                pairs.append(r)
                before = here
            for q in range(points // 2):
                target[q, i] = pairs[2 * q] + pairs[2 * q + 1]
            return acc + own(i) * total

        norms[level - 1] = loop(lost + 1, window - lost - 1, descend, zero, unroll=1)
        source = target

    level = LEVELS - 1
    lost = level - 1

    def smooth_last(i):
        v_ref[0, i] = w_win[level - 1, i] * source[0, i]

    loop(lost, window - lost, smooth_last)

    def again(i):
        s = 2.0**level * s_win[i]
        r = KEEP * source[0, i] + s * (beside(v_ref[0, i], m) + (v_ref[0, i - 1] + v_ref[0, i + 1]))
        e_ref[0, i] = v_ref[0, i] + w_win[level - 1, i] * r

    loop(lost + 1, window - lost - 1, again)

    def last_residual(i, acc):
        s = 2.0**level * s_win[i]
        here = e_ref[0, i]
        r = source[0, i] - (1.0 + 4.0 * s) * here
        r = r + s * (beside(here, m) + (e_ref[0, i - 1] + e_ref[0, i + 1]))
        return acc + own(i) * (r * r)

    norms[level - 1] = loop(lost + 2, window - lost - 2, last_residual, zero)

    lost = LEVELS - 1
    field, other = e_ref, v_ref
    for level in range(LEVELS - 2, 0, -1):
        points = TEAM >> (level - 1)
        lost += 1
        base = bases[2 * (level - 1)]

        def ascend(i, level=level, points=points, base=base, field=field, other=other):
            s = 2.0**level * s_win[i]
            w = w_win[level - 1, i]
            before = None
            for q in range(points // 2):
                e = field[q, i]
                part = KEEP * e + w * (s * (beside(e, m) + (field[q, i - 1] + field[q, i + 1])))
                kept = w * e
                for p in (2 * q, 2 * q + 1):
                    value = base[p, i] + part
                    drift = before if p == 2 * q else kept
                    if drift is not None:
                        value = value + drift
                    if level == 1:
                        out[p, i - REACH] = value
                        if p + 1 < points:
                            out[p + 1, i - REACH + piece] = value
                    else:
                        other[p, i] = value
                before = kept

        loop(lost, window - lost, ascend, unroll=1)
        field, other = other, field

    def blank(i):
        out[0, piece + i] = zero

    loop(0, piece, blank)


def finish(starts, piece, got, rhs, s_ext, w_ext, base0, base1, back, norm0, norms, out, sums, e, before, sol0, sol1):
    rows = rhs.shape[1] * 8
    m = masks()
    for j, start in enumerate(starts):

        def copy(i, j=j, start=start):
            e[start + EDGE + i] = got[j, i]
            before[start + EDGE + i] = got[j, piece + i]

        loop(0, piece, copy)

    def correct(i):
        s = s_ext[i + HALO - 1]
        w = w_ext[i + HALO - 1]
        here = e[i + 1]
        part = KEEP * here + w * (s * around(e, i + 1, m))
        sol0[i] = base0[i] + part + w * before[i + 1]
        sol1[i] = base1[i] + part + w * here

    loop(0, rows + 2, correct)

    def last(g, acc):
        for k in range(8):
            i = g * 8 + k
            s = s_ext[i + HALO]
            w = w_ext[i + HALO]
            diag = 1.0 + 4.0 * s
            past = before[i + EDGE]
            past = back[i] + KEEP * past + w * (s * around(before, i + EDGE, m) + past)
            a = sol0[i + 1]
            b = sol1[i + 1]
            ra = strided(rhs, (0,), g, k) - diag * a + s * around(sol0, i + 1, m) + past
            rb = strided(rhs, (1,), g, k) - diag * b + s * around(sol1, i + 1, m) + a
            out[0, g, pl.ds(k, 8, stride=8)] = a
            out[1, g, pl.ds(k, 8, stride=8)] = b
            acc = acc + (ra * ra + rb * rb)
        return acc

    final = loop(0, rows // 8, last, jnp.zeros((8, 128), jnp.float32), unroll=1)
    parts = [norm0[...]] + [norms[k] for k in range(LEVELS - 1)] + [final]
    for k, part in enumerate(parts):
        sums[pl.ds(k, 1)] = jnp.sum(part, axis=0, keepdims=True)
    for k in range(len(parts), 8):
        sums[pl.ds(k, 1)] = jnp.zeros((1, 128), jnp.float32)


def coarse_plain(g_in, s_win, own, earlier):
    cells = g_in.shape[-2] * 128

    def flat(x):
        return x.reshape(*x.shape[:-2], cells)

    def around_plain(v):
        padded = jnp.pad(v, ((0, 0), (1, 1), (1, 1)))
        total = padded[:, 2:, 1:-1] + padded[:, :-2, 1:-1]
        return total + padded[:, 1:-1, 2:] + padded[:, 1:-1, :-2]

    def resid(v, g, s, before):
        past = jnp.concatenate([before, v[:-1]], axis=0)
        return g - (1.0 + 4.0 * s) * v + s * around_plain(v) + past

    source = flat(g_in)
    s_win = flat(s_win)
    sources, fields, norms = [], [], []
    for level in range(1, LEVELS):
        s = 2.0**level * s_win
        w = DAMPING / (1.0 + 4.0 * s)
        v = w * source
        r = resid(v, source, s, earlier(v[-1:]))
        if level == LEVELS - 1:
            v = v + w * r
            r = resid(v, source, s, earlier(v[-1:]))
        masked = jnp.where(own[None, :, None], r, 0.0)
        norms.append((masked * masked).reshape(-1, 8, 128).sum(0))
        sources.append(source)
        fields.append(v)
        if level < LEVELS - 1:
            source = r[0::2] + r[1::2]
    field = fields[-1]
    for level in range(LEVELS - 2, 0, -1):
        s = 2.0**level * s_win
        w = DAMPING / (1.0 + 4.0 * s)
        field = fields[level - 1] + jnp.repeat(field, 2, axis=0)
        field = field + w * resid(field, sources[level - 1], s, earlier(field[-1:]))
    past = jnp.concatenate([earlier(field[-1:]), field[:-1]], axis=0)
    both = [x[:, REACH : x.shape[1] - REACH] for x in (field, past)]
    both = jnp.concatenate(both, axis=1)
    return both.reshape(*both.shape[:2], 8, 128), jnp.stack(norms)


def body(count, strips, rhs, guess, diffusion):
    points, rows, cells = rhs.shape
    assert points == 2 and cells == 1024 and count % TEAM == 0
    assert rows % (8 * TEAM) == 0
    total_cells = rows * strips * cells
    groups = rows // 8
    piece, window, starts = windows_of(rows)
    wide = cells // 16
    ext = rows + 2 * HALO
    up = [(i, i + 1) for i in range(strips - 1)]
    down = [(i + 1, i) for i in range(strips - 1)]
    later = [(i, i + 1) for i in range(count - 1)]

    rhs_t, guess_t, diff_t = tiles(rhs), tiles(guess), tiles(diffusion)
    edge_groups = -(-HALO // 8)
    assert groups % edge_groups == 0
    far = groups // edge_groups - 1

    def edge_specs(block):
        time = pl.BlockSpec((2, edge_groups, wide, 128), lambda i: (0, block, 0, 0))
        flat = pl.BlockSpec((edge_groups, wide, 128), lambda i: (block, 0, 0))
        return [time, time, flat]

    top, end = kernel_call(
        pack_edges, [shape(5 * HALO, 8, 128)] * 2, specs=edge_specs(0) + edge_specs(far), grid=(1,)
    )(guess_t, rhs_t, diff_t, guess_t, rhs_t, diff_t)
    low = lax.ppermute(end, "space", up)
    high = lax.ppermute(top, "space", down)
    g_prev = tiles(lax.ppermute(guess[1], "tm", later))

    sent = rows + 2 * (HALO - 2) + 2 * (HALO - 1)
    s_ext, w_ext, send, g0, g1 = kernel_call(
        first_sweep,
        [shape(ext, 8, 128), shape(ext, 8, 128), shape(sent, 8, 128), shape(ext, 8, 128), shape(ext, 8, 128)],
        n_in=5,
    )(guess_t, rhs_t, diff_t, low, high)
    got = lax.ppermute(send, "tm", later)
    part0, left0, left1, v1 = kernel_call(local_parts, [shape(ext, 8, 128)] * 4, n_in=7, flops=10**7)(
        rhs_t, low, high, s_ext, w_ext, g0, g1
    )
    mine, base0, base1, back, norm0 = kernel_call(
        functools.partial(join_first, starts, window),
        [shape(TEAM, window, 8, 128), shape(rows + 2, 8, 128), shape(rows + 2, 8, 128), shape(rows, 8, 128), shape(8, 128)],
        scratch=[(ext, 8, 128)] * 2,
        n_in=8,
    )(g_prev, got, s_ext, w_ext, part0, left0, left1, v1)

    teams = [list(range(k, k + TEAM)) for k in range(0, count, TEAM)]

    def exchange(x):
        return lax.all_to_all(x, "tm", 0, 0, axis_index_groups=teams if len(teams) > 1 else None)

    g_win = exchange(mine)
    g_win, back = lax.optimization_barrier((g_win, back))
    back = lax.ppermute(back, "tm", later)
    place = lax.axis_index("tm") % TEAM
    if len(teams) == 1:
        half = [(TEAM >> level, window, 8, 128) for level in range(LEVELS)]
        bases = []
        for level in range(1, LEVELS - 1):
            bases += [half[level - 1], half[level]]
        fields, norms = kernel_call(
            functools.partial(coarse_levels, starts, rows),
            [shape(TEAM, 2 * piece, 8, 128), shape(LEVELS - 1, 8, 128)],
            scratch=[(window, 8, 128), (LEVELS - 1, window, 8, 128), half[0], half[0]] + bases,
            specs=[pl.BlockSpec(memory_space=pltpu.SMEM), vmem(), vmem()],
        )(place.astype(jnp.int32).reshape(1), g_win, s_ext)
    else:
        start = -EDGE + place * (rows + 2 * EDGE - piece) // (TEAM - 1) - REACH
        s_win = lax.dynamic_slice_in_dim(s_ext, start + HALO, window, axis=0)
        at = start + jnp.arange(window) - place * (rows // TEAM)
        own = (at >= 0) & (at < rows // TEAM)
        jumps = [(i, i + TEAM) for i in range(count - TEAM)]
        fields, norms = coarse_plain(g_win, s_win, own, lambda v: lax.ppermute(v, "tm", jumps))
    fields = exchange(fields)

    out, sums = kernel_call(
        functools.partial(finish, starts, piece),
        [shape(2, groups, wide, 128), shape(8, 128)],
        scratch=[(rows + 2 * EDGE, 8, 128)] * 2 + [(rows + 2, 8, 128)] * 2,
        n_in=9,
    )(fields, rhs_t, s_ext, w_ext, base0, base1, back, norm0, norms)

    every = jnp.broadcast_to(sums[None], (count * strips, 8, 128))
    every = lax.all_to_all(every, ("tm", "space"), 0, 0)
    totals = every.sum(axis=(0, 2))[: LEVELS + 1]
    return untiles(out), jnp.sqrt(totals / total_cells)


def solution(mesh):
    in_specs = (P("tm", "space", None), P("tm", "space", None), P("space", None))
    out_specs = (P("tm", "space", None), P())
    step = functools.partial(body, mesh.shape["tm"], mesh.shape["space"])
    return jax.shard_map(step, mesh=mesh, in_specs=in_specs, out_specs=out_specs, check_vma=False)
```

time: 331 us -> 194 us (0.59)
  starting transfers between devices: 136 us -> 32.9 us
  Pallas kernels: 0 us -> 77.8 us
  waiting for transfers between devices: 106 us -> 53.3 us
  other arithmetic: 30.2 us -> 0.67 us
  blocking collectives: 44.9 us -> 22.7 us
  local copies, waits for them, and re-layouts: 9.38 us -> 5.27 us
    ppermute x39 -> x5, starting transfers between devices: 136 us -> 14.2 us  [the longest x1 4.96 us: body(): low = lax.ppermute(end, 'space', up)]
    ppermute x39 -> x5, waiting for transfers between devices: 106 us -> 10.2 us  [the longest x1 4.16 us: body(): high = lax.ppermute(top, 'space', down)]
    pallas_call x0 -> x6, Pallas kernels: none -> 77.8 us  [the longest x1 26.2 us: body(): kernel_call(functools.partial(coarse_levels, starts, rows), [shape(TEAM,...]
    psum x1 -> x0, blocking collectives: 44.9 us -> none  [body(): totals = lax.psum(jnp.stack(partials), ('tm', 'space'))]
    all_to_all x0 -> x2, waiting for transfers between devices: none -> 43.1 us  [exchange(): lax.all_to_all(x, 'tm', 0, 0, axis_index_groups=teams if len(teams) > 1 e...]
    all_to_all x0 -> x1, blocking collectives: none -> 22.7 us  [body(): every = lax.all_to_all(every, ('tm', 'space'), 0, 0)]
    all_to_all x0 -> x2, starting transfers between devices: none -> 18.7 us  [exchange(): lax.all_to_all(x, 'tm', 0, 0, axis_index_groups=teams if len(teams) > 1 e...]
    reduce_sum x6 -> x1, other arithmetic: 11.6 us -> 0.15 us  [body(): totals = every.sum(axis=(0, 2))[:LEVELS + 1]]
  transfers between devices with their start and end apart: 39 -> 7, of which waited for: 16 -> 5; matrix products, arithmetic and copies ran while one was open for 4% -> 0% of each run, Pallas kernels for 0% -> 6%
where the time goes in v1:
time: 194 us; the launch traced here: 193 us
  Pallas kernels  77.8 us (40%)
  waiting for transfers between devices  53.3 us (27%)
  starting transfers between devices  32.9 us (17%)
  blocking collectives  22.7 us (12%)
  local copies, waits for them, and re-layouts  5.27 us (3%)
    all_to_all x2, waiting for transfers between devices, exchange(): lax.all_to_all(x, 'tm', 0, 0, axis_index_groups=teams if len(teams) > 1 e...  43.1 us
    pallas_call x1, Pallas kernels, body(): kernel_call(functools.partial(coarse_levels, starts, rows), [shape(TEAM,...  26.2 us
    all_to_all x1, blocking collectives, body(): every = lax.all_to_all(every, ('tm', 'space'), 0, 0)  22.7 us
    all_to_all x2, starting transfers between devices, exchange(): lax.all_to_all(x, 'tm', 0, 0, axis_index_groups=teams if len(teams) > 1 e...  18.7 us
    pallas_call x1, Pallas kernels, body(): kernel_call(functools.partial(finish, starts, piece), [shape(2, groups, w...  15.1 us
    pallas_call x1, Pallas kernels, body(): kernel_call(functools.partial(join_first, starts, window), [shape(TEAM, w...  12.6 us
    pallas_call x1, Pallas kernels, body(): kernel_call(local_parts, [shape(ext, 8, 128)] * 4, n_in=7, flops=10 ** 7)  12.3 us
    pallas_call x1, Pallas kernels, body(): kernel_call(first_sweep, [shape(ext, 8, 128), shape(ext, 8, 128), shape(s...  9.52 us
  transfers between devices with their start and end apart: 7, of which 5 were waited for; matrix products, arithmetic and copies ran while one was open for 0% of the time, Pallas kernels for 6%

profile of v1, /device:TPU:0, one launch (start us, length us, event | category | flops | bytes accessed | tf_op | source)
XLA Modules:
  0.0 193.4 jit_solution(5642896239596860833)
XLA Ops:
  0.6 2.0 %shard_map.50 = (f32[55,8,128]{2,1,0:T(8,128)}, f32[55,8,128]{2,1,0:T(8,128)}) custom-call(f32[2,32,64,128]{3,2,1,0:T(8,128)} %bitcast.33, f32[2,32,64,128]{3,2,1,0:T(8,128)} %bitcast.28, f32[32,64,128]{2,1,0:T(8,128)} %bitcast.36, f32[2,32,64,128]{3,2,1,0:T(8,128)} %bitcast.34, f32[2,32,64,128]{3,2,1,0:T(8,128)} %bitcast.29, f32[32,64,128]{2,1,0:T(8,128)} %bitcast.37), custom_call_target="tpu_custom_call" | custom-call | tf_op jit(solution)/shard_map/pallas_call | solution.py:479
  2.6 5.0 %collective-permute-start.1 = (f32[55,8,128]{2,1,0:T(8,128)}, f32[55,8,128]{2,1,0:T(8,128)S(1)}, u32[]{:S(2)}, u32[]{:S(2)}) collective-permute-start(f32[55,8,128]{2,1,0:T(8,128)} %get-tuple-element.24), channel_id=1, source_target_pairs={{0,1},{1,2},{2,3},{4,5},{5,6},{6,7},{8,9},{9,10},{10,11},{12,13},{... | collective-permute-start | bytes 675848 | tf_op jit(solution)/shard_map/ppermute | solution.py:482
  7.6 0.0 copy-start
  7.6 1.4 collective-permute-start.2
  9.0 3.6 %collective-permute-done.1.low = f32[55,8,128]{2,1,0:T(8,128)S(1)} collective-permute-done((f32[55,8,128]{2,1,0:T(8,128)}, f32[55,8,128]{2,1,0:T(8,128)S(1)}, u32[]{:S(2)}, u32[]{:S(2)}) %collective-permute-start.1) | collective-permute-done | bytes 225312 | tf_op jit(solution)/shard_map/ppermute | solution.py:482
  12.6 4.2 %collective-permute-done.2.high = f32[55,8,128]{2,1,0:T(8,128)S(1)} collective-permute-done((f32[55,8,128]{2,1,0:T(8,128)}, f32[55,8,128]{2,1,0:T(8,128)S(1)}, u32[]{:S(2)}, u32[]{:S(2)}) %collective-permute-start.2) | collective-permute-done | bytes 225312 | tf_op jit(solution)/shard_map/ppermute | solution.py:483
  16.8 0.0 copy-done.6
  16.8 0.7 copy-done.7
  17.5 9.5 %shard_map.51 = (f32[278,8,128]{2,1,0:T(8,128)}, f32[278,8,128]{2,1,0:T(8,128)}, f32[294,8,128]{2,1,0:T(8,128)}, f32[278,8,128]{2,1,0:T(8,128)}, f32[278,8,128]{2,1,0:T(8,128)}) custom-call(f32[2,32,64,128]{3,2,1,0:T(8,128)} %bitcast.35, f32[2,32,64,128]{3,2,1,0:T(8,128)} %bitcast.30, f32[32,64,128]{2,1,0:T(8,128)} %bitcast.38, f32[55,8,128]{2,1,0:T(8,128)} %copy-done.6, ...), custom_call_target="tpu_custom_call" | custom-call | tf_op jit(solution)/shard_map/pallas_call | solution.py:487
  27.0 1.4 collective-permute-start.3
  28.4 0.1 slice_bitcast_fusion
  28.5 4.1 %collective-permute-start = (f32[256,1024]{1,0:T(8,128)S(1)}, f32[256,1024]{1,0:T(8,128)S(1)}, u32[]{:S(2)}, u32[]{:S(2)}) collective-permute-start(f32[256,1024]{1,0:T(8,128)S(1)} %slice_bitcast_fusion), channel_id=1, source_target_pairs={{0,4},{4,8},{8,12},{12,16},{16,20},{20,24},{24,28},{1,5},{5,9},{9,... | collective-permute-start | bytes 3145736 | tf_op jit(solution)/shard_map/ppermute | solution.py:484
  32.6 12.3 %shard_map.52 = (f32[278,8,128]{2,1,0:T(8,128)}, f32[278,8,128]{2,1,0:T(8,128)}, f32[278,8,128]{2,1,0:T(8,128)}, f32[278,8,128]{2,1,0:T(8,128)}) custom-call(f32[2,32,64,128]{3,2,1,0:T(8,128)} %bitcast.31, f32[55,8,128]{2,1,0:T(8,128)} %copy-done.6, f32[55,8,128]{2,1,0:T(8,128)} %copy-done.7, f32[278,8,128]{2,1,0:T(8,128)} %get-tuple-element.27.s_ext, ...), custom_call_target="tpu_custom_call" | custom-call | flops 10000000 | bytes 10000000 | tf_op jit(solution)/shard_map/pallas_call | solution.py:493
  44.9 0.0 collective-permute-done
  44.9 0.0 collective-permute-done.3.got
  44.9 1.0 copy-done.5
  45.9 0.3 copy-done.3
  46.2 12.6 %shard_map.53 = (f32[8,47,8,128]{3,2,1,0:T(8,128)}, f32[258,8,128]{2,1,0:T(8,128)}, f32[258,8,128]{2,1,0:T(8,128)}, f32[256,8,128]{2,1,0:T(8,128)}, f32[8,128]{1,0:T(8,128)}) custom-call(f32[32,64,128]{2,1,0:T(8,128)} %bitcast.39, f32[294,8,128]{2,1,0:T(8,128)} %copy-done.3, f32[278,8,128]{2,1,0:T(8,128)} %get-tuple-element.27.s_ext, ...), custom_call_target="tpu_custom_call" | custom-call | tf_op jit(solution)/shard_map/pallas_call | solution.py:496
  58.9 15.1 %all-to-all-start = ((f32[8,47,8,128]{3,2,1,0:T(8,128)}), f32[8,47,8,128]{3,2,1,0:T(8,128)S(1)}, u32[]{:S(2)}, u32[]{:S(2)}) async-start(f32[8,47,8,128]{3,2,1,0:T(8,128)} %get-tuple-element.35), calls=%async_computation | async-start | bytes 3080192 | tf_op jit(solution)/shard_map/all_to_all | solution.py:506
  73.9 20.6 %all-to-all-done.g_in = f32[8,47,8,128]{3,2,1,0:T(8,128)S(1)} async-done(((f32[8,47,8,128]{3,2,1,0:T(8,128)}), f32[8,47,8,128]{3,2,1,0:T(8,128)S(1)}, u32[]{:S(2)}, u32[]{:S(2)}) %all-to-all-start) | async-done | bytes 1540128 | tf_op jit(solution)/shard_map/all_to_all | solution.py:506
  94.6 1.1 copy-done.2
  95.7 26.2 %shard_map.54 = (f32[8,66,8,128]{3,2,1,0:T(8,128)}, f32[4,8,128]{2,1,0:T(8,128)}) custom-call(s32[1]{0:T(128)} %bitcast.where, f32[8,47,8,128]{3,2,1,0:T(8,128)} %copy-done.2, f32[278,8,128]{2,1,0:T(8,128)} %get-tuple-element.27.s_ext), custom_call_target="tpu_custom_call" | custom-call | tf_op jit(solution)/shard_map/pallas_call | solution.py:517
  121.9 3.6 %all-to-all-start.1 = ((f32[8,66,8,128]{3,2,1,0:T(8,128)}), f32[8,66,8,128]{3,2,1,0:T(8,128)S(1)}, u32[]{:S(2)}, u32[]{:S(2)}) async-start(f32[8,66,8,128]{3,2,1,0:T(8,128)} %get-tuple-element.38), calls=%async_computation.1 | async-start | bytes 4325376 | tf_op jit(solution)/shard_map/all_to_all | solution.py:506
  125.5 2.4 %collective-permute-start.4 = (f32[256,8,128]{2,1,0:T(8,128)}, f32[256,8,128]{2,1,0:T(8,128)S(1)}, u32[]{:S(2)}, u32[]{:S(2)}) collective-permute-start(f32[256,8,128]{2,1,0:T(8,128)} %get-tuple-element.41), channel_id=1, source_target_pairs={{0,4},{4,8},{8,12},{12,16},{16,20},{20,24},{24,28},{1,5},{5,9},{9,... | collective-permute-start | bytes 3145736 | tf_op jit(solution)/shard_map/ppermute | solution.py:510
  127.9 2.4 %collective-permute-done.4.back = f32[256,8,128]{2,1,0:T(8,128)S(1)} collective-permute-done((f32[256,8,128]{2,1,0:T(8,128)}, f32[256,8,128]{2,1,0:T(8,128)S(1)}, u32[]{:S(2)}, u32[]{:S(2)}) %collective-permute-start.4) | collective-permute-done | bytes 1048608 | tf_op jit(solution)/shard_map/ppermute | solution.py:510
  130.3 22.5 %all-to-all-done.1.got = f32[8,66,8,128]{3,2,1,0:T(8,128)S(1)} async-done(((f32[8,66,8,128]{3,2,1,0:T(8,128)}), f32[8,66,8,128]{3,2,1,0:T(8,128)S(1)}, u32[]{:S(2)}, u32[]{:S(2)}) %all-to-all-start.1) | async-done | bytes 2162720 | tf_op jit(solution)/shard_map/all_to_all | solution.py:506
  152.8 1.3 copy-done.1
  154.1 15.1 %shard_map.55 = (f32[2,32,64,128]{3,2,1,0:T(8,128)}, f32[8,128]{1,0:T(8,128)}) custom-call(f32[8,66,8,128]{3,2,1,0:T(8,128)} %copy-done.1, f32[2,32,64,128]{3,2,1,0:T(8,128)} %bitcast.32, f32[278,8,128]{2,1,0:T(8,128)} %get-tuple-element.27.s_ext, f32[278,8,128]{2,1,0:T(8,128)} %get-tuple-element.28.w_ext, f32[258,8,128]{2,1,0:T(8,128)} %get-tuple-element.39.base0, ...), custom_call_target="tpu_custom_call" | custom-call | tf_op jit(solution)/shard_map/pallas_call | solution.py:532
  169.3 0.7 broadcast_in_dim.2
  170.0 22.7 %all_to_all.15 = f32[32,8,128]{2,1,0:T(8,128)S(1)} all-to-all(f32[32,8,128]{2,1,0:T(8,128)S(1)} %broadcast_in_dim.2), channel_id=1, replica_groups=mesh['tm'=8,'space'=4] {'tm','space'}, dimensions={0} | all-to-all | bytes 262144 | tf_op jit(solution)/shard_map/all_to_all | solution.py:540
  192.7 0.1 reduce_sum.9
  192.8 0.5 multiply_sqrt_fusion
  (9 shorter events, 0.0 us)
Async XLA Ops:
  2.6 10.0 %collective-permute-start.1 = (f32[55,8,128]{2,1,0:T(8,128)}, f32[55,8,128]{2,1,0:T(8,128)S(1)}, u32[]{:S(2)}, u32[]{:S(2)}) collective-permute-start(f32[55,8,128]{2,1,0:T(8,128)} %get-tuple-element.24), channel_id=1, source_target_pairs={{0,1},{1,2},{2,3},{4,5},{5,6},{6,7},{8,9},{9,10},{10,11},{12,13},{... | collective-permute-start | bytes 675848 | tf_op jit(solution)/shard_map/ppermute | solution.py:482
  7.6 20.8 %copy-start = (f32[2,256,1024]{2,1,0:T(8,128)S(1)}, f32[2,256,1024]{2,1,0:T(8,128)}, u32[]{:S(2)}) copy-start(f32[2,256,1024]{2,1,0:T(8,128)} %param.4) | copy-start | bytes 6291460
  7.6 9.2 %collective-permute-start.2 = (f32[55,8,128]{2,1,0:T(8,128)}, f32[55,8,128]{2,1,0:T(8,128)S(1)}, u32[]{:S(2)}, u32[]{:S(2)}) collective-permute-start(f32[55,8,128]{2,1,0:T(8,128)} %get-tuple-element.25), channel_id=1, source_target_pairs={{1,0},{2,1},{3,2},{5,4},{6,5},{7,6},{9,8},{10,9},{11,10},{13,12},{... | collective-permute-start | bytes 675848 | tf_op jit(solution)/shard_map/ppermute | solution.py:483
  12.6 4.2 %copy-start.6 = (f32[55,8,128]{2,1,0:T(8,128)}, f32[55,8,128]{2,1,0:T(8,128)S(1)}, u32[]{:S(2)}) copy-start(f32[55,8,128]{2,1,0:T(8,128)S(1)} %collective-permute-done.1.low) | copy-start | bytes 675844
  16.8 0.7 copy-start.7
  27.0 17.9 %collective-permute-start.3 = (f32[294,8,128]{2,1,0:T(8,128)}, f32[294,8,128]{2,1,0:T(8,128)S(1)}, u32[]{:S(2)}, u32[]{:S(2)}) collective-permute-start(f32[294,8,128]{2,1,0:T(8,128)} %get-tuple-element.26), channel_id=1, source_target_pairs={{0,4},{4,8},{8,12},{12,16},{16,20},{20,24},{24,28},{1,5},{5,9},{9,... | collective-permute-start | bytes 3612680 | tf_op jit(solution)/shard_map/ppermute | solution.py:492
  28.5 16.4 %collective-permute-start = (f32[256,1024]{1,0:T(8,128)S(1)}, f32[256,1024]{1,0:T(8,128)S(1)}, u32[]{:S(2)}, u32[]{:S(2)}) collective-permute-start(f32[256,1024]{1,0:T(8,128)S(1)} %slice_bitcast_fusion), channel_id=1, source_target_pairs={{0,4},{4,8},{8,12},{12,16},{16,20},{20,24},{24,28},{1,5},{5,9},{9,... | collective-permute-start | bytes 3145736 | tf_op jit(solution)/shard_map/ppermute | solution.py:484
  44.9 1.0 copy-start.5
  44.9 1.3 copy-start.3
  58.9 35.7 %all-to-all-start = ((f32[8,47,8,128]{3,2,1,0:T(8,128)}), f32[8,47,8,128]{3,2,1,0:T(8,128)S(1)}, u32[]{:S(2)}, u32[]{:S(2)}) async-start(f32[8,47,8,128]{3,2,1,0:T(8,128)} %get-tuple-element.35), calls=%async_computation | async-start | bytes 3080192 | tf_op jit(solution)/shard_map/all_to_all | solution.py:506
  94.6 1.1 copy-start.2
  121.9 30.9 %all-to-all-start.1 = ((f32[8,66,8,128]{3,2,1,0:T(8,128)}), f32[8,66,8,128]{3,2,1,0:T(8,128)S(1)}, u32[]{:S(2)}, u32[]{:S(2)}) async-start(f32[8,66,8,128]{3,2,1,0:T(8,128)} %get-tuple-element.38), calls=%async_computation.1 | async-start | bytes 4325376 | tf_op jit(solution)/shard_map/all_to_all | solution.py:506
  125.5 4.8 %collective-permute-start.4 = (f32[256,8,128]{2,1,0:T(8,128)}, f32[256,8,128]{2,1,0:T(8,128)S(1)}, u32[]{:S(2)}, u32[]{:S(2)}) collective-permute-start(f32[256,8,128]{2,1,0:T(8,128)} %get-tuple-element.41), channel_id=1, source_target_pairs={{0,4},{4,8},{8,12},{12,16},{16,20},{20,24},{24,28},{1,5},{5,9},{9,... | collective-permute-start | bytes 3145736 | tf_op jit(solution)/shard_map/ppermute | solution.py:510
  130.3 22.5 %copy-start.4 = (f32[256,8,128]{2,1,0:T(8,128)}, f32[256,8,128]{2,1,0:T(8,128)S(1)}, u32[]{:S(2)}) copy-start(f32[256,8,128]{2,1,0:T(8,128)S(1)} %collective-permute-done.4.back) | copy-start | bytes 3145732
  152.8 1.3 copy-start.1

commit v2 on v1

--- a/solution.py
+++ b/solution.py
@@ -1,4 +1,5 @@
 import functools
+import math
 import jax
 import jax.numpy as jnp
 from jax import lax
@@ -24,17 +25,30 @@
     return jax.ShapeDtypeStruct(dims, jnp.float32)
 
 
+def kept(*dims):
+    return pltpu.VMEM(dims, jnp.float32)
+
+
+def keep(*arrays):
+    return [pltpu.with_memory_space_constraint(x, pltpu.VMEM) for x in arrays]
+
+
 def kernel_call(body, outs, scratch=(), flops=0, n_in=0, specs=None, grid=()):
-    return pl.pallas_call(
-        body,
-        out_shape=outs,
-        grid=grid,
-        in_specs=specs or [vmem() for _ in range(n_in)],
-        out_specs=[vmem() for _ in outs],
-        scratch_shapes=[pltpu.VMEM(dims, jnp.float32) for dims in scratch],
-        compiler_params=pltpu.CompilerParams(vmem_limit_bytes=56 * 2**20),
-        cost_estimate=pl.CostEstimate(flops=flops, bytes_accessed=flops, transcendentals=0),
-    )
+    def call(*args):
+        held = sum(math.prod(dims) for dims in scratch)
+        held += sum(math.prod(x.shape) for x in list(outs) + list(args))
+        return pl.pallas_call(
+            body,
+            out_shape=outs,
+            grid=grid,
+            in_specs=specs or [vmem() for _ in range(n_in)],
+            out_specs=[vmem() for _ in outs],
+            scratch_shapes=[pltpu.VMEM(dims, jnp.float32) for dims in scratch],
+            compiler_params=pltpu.CompilerParams(vmem_limit_bytes=4 * held + 2**21),
+            cost_estimate=pl.CostEstimate(flops=flops, bytes_accessed=flops, transcendentals=0),
+        )(*args)
+
+    return call
 
 
 def tiles(block):
@@ -73,54 +87,91 @@
 
 
 def loop(low, high, body, carry=None, unroll=4):
-    if carry is None:
-        lax.fori_loop(low, high, lambda i, c: (body(i), c)[1], 0, unroll=unroll)
-        return None
-    return lax.fori_loop(low, high, body, carry, unroll=unroll)
+    quiet = carry is None
+    steps = (high - low) // unroll
+
+    def block(n, value):
+        for k in range(unroll):
+            value = (body(low + n * unroll + k), value)[1] if quiet else body(low + n * unroll + k, value)
+        return value
+
+    value = lax.fori_loop(0, steps, block, 0 if quiet else carry)
+    for i in range(low + steps * unroll, high):
+        value = (body(i), value)[1] if quiet else body(i, value)
+    return None if quiet else value
+
+
+BLOCK = 32
+
+
+def padded(rows):
+    return -(-(rows - 2) // BLOCK) * BLOCK + 2
+
+
+def block_loop(low, high, body, carry, unroll):
+    high = low + -(-(high - low) // unroll) * unroll
+    return loop(low, high, body, carry, unroll)
 
 
 def strided(ref, lead, row_group, k):
     return ref[lead + (row_group, pl.ds(k, 8, stride=8))]
 
 
-def unpack_rows(src, lead, dst, offset, rows):
-    def group(g):
-        for k in range(8):
-            dst[offset + g * 8 + k] = strided(src, lead, g, k)
-
-    loop(0, rows // 8, group, unroll=2)
-
-
-def pack_edges(g_top, r_top, d_top, g_end, r_end, d_end, top, end):
+def place_of():
+    return lax.rem(lax.axis_index("tm"), TEAM)
+
+
+def odd_strip():
+    return lax.rem(lax.axis_index("space"), 2) == 1
+
+
+def either(flag, body, one, two):
+    pl.when(flag)(lambda: body(two, one))
+    pl.when(jnp.logical_not(flag))(lambda: body(one, two))
+
+
+def pack_edges(g_top, r_top, d_top, g_end, r_end, d_end, pair, other):
     count = g_top.shape[1] * 8
-
-    def row_of(ref, lead, row):
-        return strided(ref, lead, row // 8, row % 8)
-
     refs = [((g_top, (t,)), (g_end, (t,))) for t in range(2)]
     refs += [((r_top, (t,)), (r_end, (t,))) for t in range(2)]
     refs += [((d_top, ()), (d_end, ()))]
-    for i, ((a, lead_a), (b, lead_b)) in enumerate(refs):
-        for k in range(HALO):
-            top[i * HALO + k] = row_of(a, lead_a, k)
-            end[i * HALO + k] = row_of(b, lead_b, count - HALO + k)
-
-
-def first_sweep(guess, rhs, diff, low, high, s_ext, w_ext, send, g0, g1):
+
+    def fill(end, top):
+        for i, ((a, lead_a), (b, lead_b)) in enumerate(refs):
+            for k in range(HALO):
+                top[i * HALO + k] = strided(a, lead_a, k // 8, k % 8)
+                row = count - HALO + k
+                end[i * HALO + k] = strided(b, lead_b, row // 8, row % 8)
+
+    either(odd_strip(), fill, pair, other)
+
+
+def first_sweep(guess, rhs, diff, pair, other, s_ext, w_ext, send, g0, g1, low, high):
     rows = guess.shape[1] * 8
     m = masks()
-    unpack_rows(diff, (), s_ext, HALO, rows)
-    unpack_rows(guess, (0,), g0, HALO, rows)
-    unpack_rows(guess, (1,), g1, HALO, rows)
+
+    def unpack(g):
+        for k in range(8):
+            i = HALO + g * 8 + k
+            s = strided(diff, (), g, k)
+            s_ext[i] = s
+            w_ext[i] = DAMPING / (1.0 + 4.0 * s)
+            g0[i] = strided(guess, (0,), g, k)
+            g1[i] = strided(guess, (1,), g, k)
+
+    def order(after, before):
+        for k in range(5 * HALO):
+            low[k] = before[k]
+            high[k] = after[k]
+
+    either(odd_strip(), order, pair, other)
+    loop(0, rows // 8, unpack, unroll=2)
     for k in range(HALO):
         for dst, i in ((g0, 0), (g1, 1), (s_ext, 4)):
             dst[k] = low[i * HALO + k]
             dst[HALO + rows + k] = high[i * HALO + k]
-
-    def weight(i):
-        w_ext[i] = DAMPING / (1.0 + 4.0 * s_ext[i])
-
-    loop(0, rows + 2 * HALO, weight)
+        for i in (k, HALO + rows + k):
+            w_ext[i] = DAMPING / (1.0 + 4.0 * s_ext[i])
 
     def sweep(i, source):
         return KEEP * g1[i] + w_ext[i] * (source + s_ext[i] * around(g1, i, m) + g0[i])
@@ -130,7 +181,7 @@
             i = HALO + g * 8 + k
             send[i - 2] = sweep(i, strided(rhs, (1,), g, k))
 
-    loop(0, rows // 8, inner, unroll=1)
+    loop(0, rows // 8, inner, unroll=4)
     for k in range(2, HALO):
         send[k - 2] = sweep(k, low[3 * HALO + k])
     for k in range(0, HALO - 2):
@@ -160,7 +211,7 @@
         for k in range(8):
             fill(HALO + g * 8 + k, strided(rhs, (0,), g, k), strided(rhs, (1,), g, k))
 
-    loop(0, rows // 8, inner, unroll=1)
+    loop(0, rows // 8, inner, unroll=2)
     for k in range(1, HALO):
         fill(k, low[2 * HALO + k], low[3 * HALO + k])
     for k in range(0, HALO - 1):
@@ -176,7 +227,7 @@
         for k in range(8):
             rest(HALO + g * 8 + k, strided(rhs, (0,), g, k), strided(rhs, (1,), g, k))
 
-    loop(0, rows // 8, inner2, unroll=1)
+    loop(0, rows // 8, inner2, unroll=2)
     for k in range(2, HALO):
         rest(k, low[2 * HALO + k], low[3 * HALO + k])
     for k in range(0, HALO - 2):
@@ -186,11 +237,17 @@
 def windows_of(rows):
     piece = -(-(rows + 2 * EDGE) // TEAM)
     spare = rows + 2 * EDGE - piece
-    starts = [-EDGE + j * spare // (TEAM - 1) for j in range(TEAM)]
-    return piece, piece + 2 * REACH, starts
-
-
-def join_first(starts, window, g_prev, got, s_ext, w_ext, part0, left0, left1, v1, out, base0, base1, back, norm, y, coarse):
+
+    def start(j):
+        return j * spare // (TEAM - 1) - EDGE
+
+    return piece, piece + 2 * REACH, start
+
+
+def join_first(start_of, window, g_prev, got, s_ext, w_ext, part0, left0, left1, v1, *refs):
+    outs = refs[:TEAM]
+    base0, base1, back, norm, y, coarse = refs[TEAM:]
+    place = place_of()
     rows = g_prev.shape[0] * 8
     m = masks()
     tail = rows + 2 * (HALO - 2)
@@ -200,7 +257,7 @@
             i = HALO + g * 8 + k
             y[i] = w_ext[i] * strided(g_prev, (), g, k)
 
-    loop(0, rows // 8, inner, unroll=1)
+    loop(0, rows // 8, inner, unroll=2)
     for k in range(HALO - 1):
         i = 1 + k
         y[i] = w_ext[i] * got[tail + k]
@@ -230,27 +287,31 @@
         back[i - HALO] = based(i, a, b)
         return acc + (a * a + b * b)
 
-    norm[...] = loop(HALO, HALO + rows, main, jnp.zeros((8, 128), jnp.float32))
+    norm[...] = loop(HALO, HALO + rows, main, jnp.zeros((8, 128), jnp.float32), unroll=32)
     for i in (HALO - 1, HALO + rows):
         a, b = edge(i)
         based(i, a, b)
     for i in list(range(2, HALO - 1)) + list(range(HALO + rows + 1, 2 * HALO + rows - 2)):
         edge(i)
-    for j, start in enumerate(starts):
-        low = start - REACH + HALO
-
-        def copy(i, j=j, low=low):
-            out[j, i] = coarse[low + i]
-
-        loop(0, window, copy)
-
-
-def coarse_levels(starts, rows, where, g_in, s_ext, out, norms, s_win, w_win, v_ref, e_ref, *bases):
-    window = g_in.shape[1]
+    for k, out in enumerate(outs):
+        low = start_of(place ^ k) - REACH + HALO
+
+        def copy(i, out=out, low=low):
+            out[i] = coarse[low + i]
+
+        loop(0, window, copy, unroll=16)
+
+
+def coarse_levels(start_of, rows, s_ext, *refs):
+    g_in, refs = refs[:TEAM], refs[TEAM:]
+    outs, refs = refs[:TEAM], refs[TEAM:]
+    norms, s_win, w_win, v_ref, e_ref, final = refs[:6]
+    bases = refs[6:]
+    window = g_in[0].shape[0]
     piece = window - 2 * REACH
     m = masks()
-    place = where[0]
-    start = -EDGE + place * (rows + 2 * EDGE - piece) // (TEAM - 1) - REACH
+    place = place_of()
+    start = start_of(place) - REACH
     first_own = place * (rows // TEAM) - start
     last_own = first_own + rows // TEAM
 
@@ -260,12 +321,12 @@
         for level in range(1, LEVELS):
             w_win[level - 1, i] = DAMPING / (1.0 + 4.0 * 2.0**level * s)
 
-    loop(0, window, level_weights, unroll=2)
-
-    def own(i):
-        return jnp.where((i >= first_own) & (i < last_own), 1.0, 0.0).astype(jnp.float32)
-
-    source = g_in
+    loop(0, window, level_weights, unroll=4)
+
+    def own(i, value):
+        return jnp.where((i >= first_own) & (i < last_own), value, 0.0)
+
+    source = None
     zero = jnp.zeros((8, 128), jnp.float32)
     for level in range(1, LEVELS - 1):
         points = TEAM >> (level - 1)
@@ -276,9 +337,12 @@
         def smooth(i, level=level, points=points, source=source):
             w = w_win[level - 1, i]
             for p in range(points):
-                v_ref[p, i] = w * source[p, i]
-
-        loop(lost, window - lost, smooth, unroll=2)
+                if source is None:
+                    v_ref[place ^ p, i] = w * g_in[p][i]
+                else:
+                    v_ref[p, i] = w * source[p, i]
+
+        loop(0, window, smooth, unroll=4)
 
         def descend(i, acc, level=level, points=points, source=source, base=base, target=target):
             s = 2.0**level * s_win[i]
@@ -288,7 +352,7 @@
             before = None
             for p in range(points):
                 here = v_ref[p, i]
-                r = KEEP * source[p, i] + s * (beside(here, m) + (v_ref[p, i - 1] + v_ref[p, i + 1]))
+                r = 0.25 * here + s * (here + beside(here, m) + (v_ref[p, i - 1] + v_ref[p, i + 1]))
                 if before is not None:
                     r = r + before
                 base[p, i] = here + w * r
@@ -297,9 +361,9 @@
                 before = here
             for q in range(points // 2):
                 target[q, i] = pairs[2 * q] + pairs[2 * q + 1]
-            return acc + own(i) * total
-
-        norms[level - 1] = loop(lost + 1, window - lost - 1, descend, zero, unroll=1)
+            return acc + own(i, total)
+
+        norms[level - 1] = block_loop(1, window - 1, descend, zero, BLOCK // points)
         source = target
 
     level = LEVELS - 1
@@ -308,23 +372,24 @@
     def smooth_last(i):
         v_ref[0, i] = w_win[level - 1, i] * source[0, i]
 
-    loop(lost, window - lost, smooth_last)
+    loop(0, window, smooth_last, unroll=16)
 
     def again(i):
         s = 2.0**level * s_win[i]
-        r = KEEP * source[0, i] + s * (beside(v_ref[0, i], m) + (v_ref[0, i - 1] + v_ref[0, i + 1]))
-        e_ref[0, i] = v_ref[0, i] + w_win[level - 1, i] * r
-
-    loop(lost + 1, window - lost - 1, again)
+        here = v_ref[0, i]
+        r = 0.25 * here + s * (here + beside(here, m) + (v_ref[0, i - 1] + v_ref[0, i + 1]))
+        e_ref[0, i] = here + w_win[level - 1, i] * r
+
+    block_loop(1, window - 1, again, None, BLOCK)
 
     def last_residual(i, acc):
         s = 2.0**level * s_win[i]
         here = e_ref[0, i]
         r = source[0, i] - (1.0 + 4.0 * s) * here
         r = r + s * (beside(here, m) + (e_ref[0, i - 1] + e_ref[0, i + 1]))
-        return acc + own(i) * (r * r)
-
-    norms[level - 1] = loop(lost + 2, window - lost - 2, last_residual, zero)
+        return acc + own(i, r * r)
+
+    norms[level - 1] = block_loop(1, window - 1, last_residual, zero, BLOCK)
 
     lost = LEVELS - 1
     field, other = e_ref, v_ref
@@ -347,32 +412,45 @@
                     if drift is not None:
                         value = value + drift
                     if level == 1:
-                        out[p, i - REACH] = value
-                        if p + 1 < points:
-                            out[p + 1, i - REACH + piece] = value
+                        final[p + 1, i - REACH] = value
                     else:
                         other[p, i] = value
                 before = kept
 
-        loop(lost, window - lost, ascend, unroll=1)
+        span = BLOCK // points * 2
+        if level == 1:
+            loop(lost, window - lost, ascend, unroll=min(8, span))
+        else:
+            block_loop(1, window - 1, ascend, None, span)
         field, other = other, field
 
     def blank(i):
-        out[0, piece + i] = zero
-
-    loop(0, piece, blank)
-
-
-def finish(starts, piece, got, rhs, s_ext, w_ext, base0, base1, back, norm0, norms, out, sums, e, before, sol0, sol1):
+        final[0, i] = zero
+
+    loop(0, piece, blank, unroll=11)
+    for k, out in enumerate(outs):
+
+        def copy(i, k=k, out=out):
+            out[i] = final[(place ^ k) + 1, i]
+            out[piece + i] = final[place ^ k, i]
+
+        loop(0, piece, copy, unroll=11)
+
+
+def finish(start_of, piece, rhs, s_ext, w_ext, base0, base1, back, norm0, norms, *refs):
+    fields = refs[:TEAM]
+    out, sums, e, before, sol0, sol1 = refs[TEAM:]
     rows = rhs.shape[1] * 8
     m = masks()
-    for j, start in enumerate(starts):
-
-        def copy(i, j=j, start=start):
-            e[start + EDGE + i] = got[j, i]
-            before[start + EDGE + i] = got[j, piece + i]
-
-        loop(0, piece, copy)
+    place = place_of()
+    for k, got in enumerate(fields):
+        start = start_of(place ^ k) + EDGE
+
+        def copy(i, got=got, start=start):
+            e[start + i] = got[i]
+            before[start + i] = got[piece + i]
+
+        loop(0, piece, copy, unroll=11)
 
     def correct(i):
         s = s_ext[i + HALO - 1]
@@ -382,7 +460,7 @@
         sol0[i] = base0[i] + part + w * before[i + 1]
         sol1[i] = base1[i] + part + w * here
 
-    loop(0, rows + 2, correct)
+    loop(0, rows + 2, correct, unroll=24)
 
     def last(g, acc):
         for k in range(8):
@@ -401,7 +479,7 @@
             acc = acc + (ra * ra + rb * rb)
         return acc
 
-    final = loop(0, rows // 8, last, jnp.zeros((8, 128), jnp.float32), unroll=1)
+    final = loop(0, rows // 8, last, jnp.zeros((8, 128), jnp.float32), unroll=2)
     parts = [norm0[...]] + [norms[k] for k in range(LEVELS - 1)] + [final]
     for k, part in enumerate(parts):
         sums[pl.ds(k, 1)] = jnp.sum(part, axis=0, keepdims=True)
@@ -459,11 +537,14 @@
     assert rows % (8 * TEAM) == 0
     total_cells = rows * strips * cells
     groups = rows // 8
-    piece, window, starts = windows_of(rows)
+    piece, window, start_of = windows_of(rows)
     wide = cells // 16
     ext = rows + 2 * HALO
-    up = [(i, i + 1) for i in range(strips - 1)]
-    down = [(i + 1, i) for i in range(strips - 1)]
+
+    def both(first):
+        pairs = [(i, i + 1) for i in range(first, strips - 1, 2)]
+        return pairs + [(b, a) for a, b in pairs]
+
     later = [(i, i + 1) for i in range(count - 1)]
 
     rhs_t, guess_t, diff_t = tiles(rhs), tiles(guess), tiles(diffusion)
@@ -476,65 +557,72 @@
         flat = pl.BlockSpec((edge_groups, wide, 128), lambda i: (block, 0, 0))
         return [time, time, flat]
 
-    top, end = kernel_call(
+    g_prev = tiles(lax.ppermute(guess[1], "tm", later))
+    far_args = [pltpu.with_memory_space_constraint(x, pltpu.HBM) for x in (guess_t, rhs_t, diff_t)]
+    facing, backing = kernel_call(
         pack_edges, [shape(5 * HALO, 8, 128)] * 2, specs=edge_specs(0) + edge_specs(far), grid=(1,)
-    )(guess_t, rhs_t, diff_t, guess_t, rhs_t, diff_t)
-    low = lax.ppermute(end, "space", up)
-    high = lax.ppermute(top, "space", down)
-    g_prev = tiles(lax.ppermute(guess[1], "tm", later))
+    )(*far_args, *far_args)
+    facing = lax.ppermute(facing, "space", both(0))
+    backing = lax.ppermute(backing, "space", both(1))
 
     sent = rows + 2 * (HALO - 2) + 2 * (HALO - 1)
-    s_ext, w_ext, send, g0, g1 = kernel_call(
+    s_ext, w_ext, send, g0, g1, low, high = kernel_call(
         first_sweep,
-        [shape(ext, 8, 128), shape(ext, 8, 128), shape(sent, 8, 128), shape(ext, 8, 128), shape(ext, 8, 128)],
+        [kept(ext, 8, 128)] * 2 + [shape(sent, 8, 128)] + [shape(ext, 8, 128)] * 2 + [shape(5 * HALO, 8, 128)] * 2,
         n_in=5,
-    )(guess_t, rhs_t, diff_t, low, high)
+    )(guess_t, rhs_t, diff_t, facing, backing)
     got = lax.ppermute(send, "tm", later)
     part0, left0, left1, v1 = kernel_call(local_parts, [shape(ext, 8, 128)] * 4, n_in=7, flops=10**7)(
         rhs_t, low, high, s_ext, w_ext, g0, g1
     )
-    mine, base0, base1, back, norm0 = kernel_call(
-        functools.partial(join_first, starts, window),
-        [shape(TEAM, window, 8, 128), shape(rows + 2, 8, 128), shape(rows + 2, 8, 128), shape(rows, 8, 128), shape(8, 128)],
+    *mine, base0, base1, back, norm0 = kernel_call(
+        functools.partial(join_first, start_of, window),
+        [shape(window, 8, 128)] * TEAM
+        + [kept(rows + 2, 8, 128), kept(rows + 2, 8, 128), shape(rows, 8, 128), shape(8, 128)],
         scratch=[(ext, 8, 128)] * 2,
         n_in=8,
     )(g_prev, got, s_ext, w_ext, part0, left0, left1, v1)
 
-    teams = [list(range(k, k + TEAM)) for k in range(0, count, TEAM)]
-
-    def exchange(x):
-        return lax.all_to_all(x, "tm", 0, 0, axis_index_groups=teams if len(teams) > 1 else None)
-
-    g_win = exchange(mine)
-    g_win, back = lax.optimization_barrier((g_win, back))
+    def exchange(parts):
+        moved = [parts[0]]
+        for k in range(1, TEAM):
+            moved.append(lax.ppermute(parts[k], "tm", [(i, i ^ k) for i in range(count)]))
+        return moved
+
+    mine = exchange(mine)
+    *mine, back = lax.optimization_barrier((*mine, back))
     back = lax.ppermute(back, "tm", later)
-    place = lax.axis_index("tm") % TEAM
-    if len(teams) == 1:
-        half = [(TEAM >> level, window, 8, 128) for level in range(LEVELS)]
+    if count == TEAM:
+        tall = padded(window)
+        half = [(TEAM >> level, tall, 8, 128) for level in range(LEVELS)]
         bases = []
         for level in range(1, LEVELS - 1):
             bases += [half[level - 1], half[level]]
-        fields, norms = kernel_call(
-            functools.partial(coarse_levels, starts, rows),
-            [shape(TEAM, 2 * piece, 8, 128), shape(LEVELS - 1, 8, 128)],
-            scratch=[(window, 8, 128), (LEVELS - 1, window, 8, 128), half[0], half[0]] + bases,
-            specs=[pl.BlockSpec(memory_space=pltpu.SMEM), vmem(), vmem()],
-        )(place.astype(jnp.int32).reshape(1), g_win, s_ext)
+        *fields, norms = kernel_call(
+            functools.partial(coarse_levels, start_of, rows),
+            [shape(2 * piece, 8, 128)] * TEAM + [shape(LEVELS - 1, 8, 128)],
+            scratch=[(tall, 8, 128), (LEVELS - 1, tall, 8, 128), half[0], half[0], (TEAM + 1, piece, 8, 128)] + bases,
+            n_in=1 + TEAM,
+        )(s_ext, *mine)
     else:
-        start = -EDGE + place * (rows + 2 * EDGE - piece) // (TEAM - 1) - REACH
+        place = place_of()
+        order = place ^ jnp.arange(TEAM)
+        start = start_of(place) - REACH
         s_win = lax.dynamic_slice_in_dim(s_ext, start + HALO, window, axis=0)
         at = start + jnp.arange(window) - place * (rows // TEAM)
         own = (at >= 0) & (at < rows // TEAM)
         jumps = [(i, i + TEAM) for i in range(count - TEAM)]
-        fields, norms = coarse_plain(g_win, s_win, own, lambda v: lax.ppermute(v, "tm", jumps))
+        fields, norms = coarse_plain(jnp.stack(mine)[order], s_win, own, lambda v: lax.ppermute(v, "tm", jumps))
+        fields = list(fields[order])
     fields = exchange(fields)
 
+    s_ext, w_ext, base0, base1 = keep(s_ext, w_ext, base0, base1)
     out, sums = kernel_call(
-        functools.partial(finish, starts, piece),
+        functools.partial(finish, start_of, piece),
         [shape(2, groups, wide, 128), shape(8, 128)],
         scratch=[(rows + 2 * EDGE, 8, 128)] * 2 + [(rows + 2, 8, 128)] * 2,
-        n_in=9,
-    )(fields, rhs_t, s_ext, w_ext, base0, base1, back, norm0, norms)
+        n_in=8 + TEAM,
+    )(rhs_t, s_ext, w_ext, base0, base1, back, norm0, norms, *fields)
 
     every = jnp.broadcast_to(sums[None], (count * strips, 8, 128))
     every = lax.all_to_all(every, ("tm", "space"), 0, 0)
@@ -546,4 +634,5 @@
     in_specs = (P("tm", "space", None), P("tm", "space", None), P("space", None))
     out_specs = (P("tm", "space", None), P())
     step = functools.partial(body, mesh.shape["tm"], mesh.shape["space"])
-    return jax.shard_map(step, mesh=mesh, in_specs=in_specs, out_specs=out_specs, check_vma=False)
+    step = jax.shard_map(step, mesh=mesh, in_specs=in_specs, out_specs=out_specs, check_vma=False)
+    return step

time: 194 us -> 128 us (0.66)
  Pallas kernels: 77.8 us -> 22.9 us
  starting transfers between devices: 32.9 us -> 43.1 us
  waiting for transfers between devices: 53.3 us -> 44.6 us
  blocking collectives: 22.7 us -> 16 us
  local copies, waits for them, and re-layouts: 5.27 us -> 0.09 us
    pallas_call x6, Pallas kernels: 77.8 us -> 22.9 us  [call(): pl.pallas_call(body, out_shape=outs, grid=grid, in_specs=specs or [vmem()...]
    all_to_all x2 -> x0, waiting for transfers between devices: 43.1 us -> none  [exchange(): lax.all_to_all(x, 'tm', 0, 0, axis_index_groups=teams if len(teams) > 1 e...]
    ppermute x2 -> x16, waiting for transfers between devices: 7.78 us -> 44.6 us  [the longest x14 39.8 us: exchange(): lax.ppermute(parts[k], 'tm', [(i, i ^ k) for i in range(count)])]
    ppermute x2 -> x16, starting transfers between devices: 6.38 us -> 35.3 us  [the longest x14 31.5 us: exchange(): lax.ppermute(parts[k], 'tm', [(i, i ^ k) for i in range(count)])]
    all_to_all x2 -> x0, starting transfers between devices: 18.7 us -> none  [exchange(): lax.all_to_all(x, 'tm', 0, 0, axis_index_groups=teams if len(teams) > 1 e...]
    all_to_all x1, blocking collectives: 22.7 us -> 16 us  [body(): every = lax.all_to_all(every, ('tm', 'space'), 0, 0)]
    unnamed x16 -> x6, local copies, waits for them, and re-layouts: 4.48 us -> 0.01 us
    ppermute x1, waiting for transfers between devices: 2.41 us -> 0.01 us  [body(): back = lax.ppermute(back, 'tm', later)]
  transfers between devices with their start and end apart: 7 -> 19, of which waited for: 5 -> 7; matrix products, arithmetic and copies ran while one was open for 0% -> 0% of each run, Pallas kernels for 6% -> 9%
where the time goes in v2:
time: 128 us
  waiting for transfers between devices  44.6 us (35%)
  starting transfers between devices  43.1 us (34%)
  Pallas kernels  22.9 us (18%)
  blocking collectives  16 us (12%)
    ppermute x14, waiting for transfers between devices, exchange(): lax.ppermute(parts[k], 'tm', [(i, i ^ k) for i in range(count)])  39.8 us
    ppermute x14, starting transfers between devices, exchange(): lax.ppermute(parts[k], 'tm', [(i, i ^ k) for i in range(count)])  31.5 us
    pallas_call x6, Pallas kernels, call(): pl.pallas_call(body, out_shape=outs, grid=grid, in_specs=specs or [vmem()...  22.9 us
    all_to_all x1, blocking collectives, body(): every = lax.all_to_all(every, ('tm', 'space'), 0, 0)  16 us
    ppermute x1, waiting for transfers between devices, body(): facing = lax.ppermute(facing, 'space', both(0))  4.84 us
    ppermute x1, starting transfers between devices, body(): g_prev = tiles(lax.ppermute(guess[1], 'tm', later))  4.28 us
    ppermute x1, starting transfers between devices, body(): facing = lax.ppermute(facing, 'space', both(0))  3.12 us
  transfers between devices with their start and end apart: 19, of which 7 were waited for; matrix products, arithmetic and copies ran while one was open for 0% of the time, Pallas kernels for 9%

profile of v2, /device:TPU:0, one launch (start us, length us, event | category | flops | bytes accessed | tf_op | source)
XLA Modules:
  0.0 128.2 jit_solution(252343691520080686)
XLA Ops:
  0.7 1.4 %shard_map.50 = (f32[55,8,128]{2,1,0:T(8,128)S(1)}, f32[55,8,128]{2,1,0:T(8,128)S(1)}) custom-call(f32[2,32,64,128]{3,2,1,0:T(8,128)} %bitcast.32, f32[2,32,64,128]{3,2,1,0:T(8,128)} %bitcast.27, f32[32,64,128]{2,1,0:T(8,128)} %bitcast.35, f32[2,32,64,128]{3,2,1,0:T(8,128)} %bitcast.33, f32[2,32,64,128]{3,2,1,0:T(8,128)} %bitcast.28, f32[32,64,128]{2,1,0:T(8,128)} %bitcast.36), custom_call_target="tpu_custom_call" | custom-call | tf_op jit(solution)/shard_map/pallas_call | solution.py:40
  2.0 3.1 %collective-permute-start = (f32[55,8,128]{2,1,0:T(8,128)S(1)}, f32[55,8,128]{2,1,0:T(8,128)S(1)}, u32[]{:S(2)}, u32[]{:S(2)}) collective-permute-start(f32[55,8,128]{2,1,0:T(8,128)S(1)} %get-tuple-element.47), channel_id=1, source_target_pairs={{0,1},{2,3},{1,0},{3,2},{4,5},{6,7},{5,4},{7,6},{8,9},{10,11},{9,8... | collective-permute-start | bytes 675848 | tf_op jit(solution)/shard_map/ppermute | solution.py:565
  5.2 0.7 collective-permute-start.1
  5.8 4.8 %collective-permute-done.pair = f32[55,8,128]{2,1,0:T(8,128)S(1)} collective-permute-done((f32[55,8,128]{2,1,0:T(8,128)S(1)}, f32[55,8,128]{2,1,0:T(8,128)S(1)}, u32[]{:S(2)}, u32[]{:S(2)}) %collective-permute-start) | collective-permute-done | bytes 225312 | tf_op jit(solution)/shard_map/ppermute | solution.py:565
  10.7 2.2 %shard_map.51 = (f32[278,8,128]{2,1,0:T(8,128)S(1)}, f32[278,8,128]{2,1,0:T(8,128)S(1)}, f32[294,8,128]{2,1,0:T(8,128)S(1)}, f32[278,8,128]{2,1,0:T(8,128)S(1)},...) custom-call(f32[2,32,64,128]{3,2,1,0:T(8,128)S(1)} %bitcast.34, ...), custom_call_target="tpu_custom_call" | custom-call | tf_op jit(solution)/shard_map/pallas_call | solution.py:40
  12.9 1.4 %collective-permute-start.3 = (f32[294,8,128]{2,1,0:T(8,128)S(1)}, f32[294,8,128]{2,1,0:T(8,128)S(1)}, u32[]{:S(2)}, u32[]{:S(2)}) collective-permute-start(f32[294,8,128]{2,1,0:T(8,128)S(1)} %get-tuple-element.51), channel_id=1, source_target_pairs={{0,4},{4,8},{8,12},{12,16},{16,20},{20,24},{24,28},{1,5},{5,9},{9,... | collective-permute-start | bytes 3612680 | tf_op jit(solution)/shard_map/ppermute | solution.py:574
  14.2 0.1 slice_bitcast_fusion
  14.3 4.3 %collective-permute-start.2 = (f32[256,1024]{1,0:T(8,128)S(1)}, f32[256,1024]{1,0:T(8,128)S(1)}, u32[]{:S(2)}, u32[]{:S(2)}) collective-permute-start(f32[256,1024]{1,0:T(8,128)S(1)} %slice_bitcast_fusion), channel_id=1, source_target_pairs={{0,4},{4,8},{8,12},{12,16},{16,20},{20,24},{24,28},{1,5},{5,9},{9,... | collective-permute-start | bytes 3145736 | tf_op jit(solution)/shard_map/ppermute | solution.py:560
  18.6 4.9 %shard_map.52 = (f32[278,8,128]{2,1,0:T(8,128)S(1)}, f32[278,8,128]{2,1,0:T(8,128)S(1)}, f32[278,8,128]{2,1,0:T(8,128)S(1)}, f32[278,8,128]{2,1,0:T(8,128)S(1)}) custom-call(f32[2,32,64,128]{3,2,1,0:T(8,128)S(1)} %bitcast.30, f32[55,8,128]{2,1,0:T(8,128)S(1)} %get-tuple-element.52.low, f32[55,8,128]{2,1,0:T(8,128)S(1)} %get-tuple-element.53.high, ...), custom_call_target="tpu_custom_call" | custom-call | flops 10000000 | bytes 10000000 | tf_op jit(solution)/shard_map/pallas_call | solution.py:40
  23.6 2.0 %shard_map.53 = (f32[47,8,128]{2,1,0:T(8,128)S(1)}, f32[47,8,128]{2,1,0:T(8,128)S(1)}, f32[47,8,128]{2,1,0:T(8,128)S(1)}, f32[47,8,128]{2,1,0:T(8,128)S(1)}, f32...) custom-call(f32[32,64,128]{2,1,0:T(8,128)S(1)} %bitcast.38, ...), custom_call_target="tpu_custom_call" | custom-call | tf_op jit(solution)/shard_map/pallas_call | solution.py:40
  25.6 17.7 %collective-permute-start.4 = (f32[47,8,128]{2,1,0:T(8,128)S(1)}, f32[47,8,128]{2,1,0:T(8,128)S(1)}, u32[]{:S(2)}, u32[]{:S(2)}) collective-permute-start(f32[47,8,128]{2,1,0:T(8,128)S(1)} %get-tuple-element.63), channel_id=1, source_target_pairs={{0,4},{4,0},{8,12},{12,8},{16,20},{20,16},{24,28},{28,24},{1,5},{5... | collective-permute-start | bytes 577544 | tf_op jit(solution)/shard_map/ppermute | solution.py:589
  43.3 2.4 %collective-permute-start.5 = (f32[47,8,128]{2,1,0:T(8,128)S(1)}, f32[47,8,128]{2,1,0:T(8,128)S(1)}, u32[]{:S(2)}, u32[]{:S(2)}) collective-permute-start(f32[47,8,128]{2,1,0:T(8,128)S(1)} %get-tuple-element.64), channel_id=1, source_target_pairs={{0,8},{4,12},{8,0},{12,4},{16,24},{20,28},{24,16},{28,20},{1,9},{5... | collective-permute-start | bytes 577544 | tf_op jit(solution)/shard_map/ppermute | solution.py:589
  45.8 2.7 %collective-permute-start.7 = (f32[47,8,128]{2,1,0:T(8,128)S(1)}, f32[47,8,128]{2,1,0:T(8,128)S(1)}, u32[]{:S(2)}, u32[]{:S(2)}) collective-permute-start(f32[47,8,128]{2,1,0:T(8,128)S(1)} %get-tuple-element.66), channel_id=1, source_target_pairs={{0,16},{4,20},{8,24},{12,28},{16,0},{20,4},{24,8},{28,12},{1,17},{... | collective-permute-start | bytes 577544 | tf_op jit(solution)/shard_map/ppermute | solution.py:589
  48.4 1.7 %collective-permute-start.9 = (f32[47,8,128]{2,1,0:T(8,128)S(1)}, f32[47,8,128]{2,1,0:T(8,128)S(1)}, u32[]{:S(2)}, u32[]{:S(2)}) collective-permute-start(f32[47,8,128]{2,1,0:T(8,128)S(1)} %get-tuple-element.68), channel_id=1, source_target_pairs={{0,24},{4,28},{8,16},{12,20},{16,8},{20,12},{24,0},{28,4},{1,25},{... | collective-permute-start | bytes 577544 | tf_op jit(solution)/shard_map/ppermute | solution.py:589
  50.2 1.2 collective-permute-done.5.refs_2_
  51.4 1.6 %collective-permute-start.10 = (f32[47,8,128]{2,1,0:T(8,128)S(1)}, f32[47,8,128]{2,1,0:T(8,128)S(1)}, u32[]{:S(2)}, u32[]{:S(2)}) collective-permute-start(f32[47,8,128]{2,1,0:T(8,128)S(1)} %get-tuple-element.69), channel_id=1, source_target_pairs={{0,28},{4,24},{8,20},{12,16},{16,12},{20,8},{24,4},{28,0},{1,29},{... | collective-permute-start | bytes 577544 | tf_op jit(solution)/shard_map/ppermute | solution.py:589
  53.0 2.0 %collective-permute-done.6.refs_3_ = f32[47,8,128]{2,1,0:T(8,128)S(1)} collective-permute-done((f32[47,8,128]{2,1,0:T(8,128)S(1)}, f32[47,8,128]{2,1,0:T(8,128)S(1)}, u32[]{:S(2)}, u32[]{:S(2)}) %collective-permute-start.6) | collective-permute-done | bytes 192544 | tf_op jit(solution)/shard_map/ppermute | solution.py:589
  55.0 10.8 %collective-permute-done.8.refs_5_ = f32[47,8,128]{2,1,0:T(8,128)S(1)} collective-permute-done((f32[47,8,128]{2,1,0:T(8,128)S(1)}, f32[47,8,128]{2,1,0:T(8,128)S(1)}, u32[]{:S(2)}, u32[]{:S(2)}) %collective-permute-start.8) | collective-permute-done | bytes 192544 | tf_op jit(solution)/shard_map/ppermute | solution.py:589
  65.8 2.1 %collective-permute-start.11 = (f32[256,8,128]{2,1,0:T(8,128)S(1)}, f32[256,8,128]{2,1,0:T(8,128)S(1)}, u32[]{:S(2)}, u32[]{:S(2)}) collective-permute-start(f32[256,8,128]{2,1,0:T(8,128)S(1)} %get-tuple-element.71), channel_id=1, source_target_pairs={{0,4},{4,8},{8,12},{12,16},{16,20},{20,24},{24,28},{1,5},{5,9},{9,... | collective-permute-start | bytes 3145736 | tf_op jit(solution)/shard_map/ppermute | solution.py:594
  67.9 6.4 %shard_map.54 = (f32[66,8,128]{2,1,0:T(8,128)S(1)}, f32[66,8,128]{2,1,0:T(8,128)S(1)}, f32[66,8,128]{2,1,0:T(8,128)S(1)}, f32[66,8,128]{2,1,0:T(8,128)S(1)}, f32...) custom-call(f32[278,8,128]{2,1,0:T(8,128)S(1)} %get-tuple-element.49, ...), custom_call_target="tpu_custom_call" | custom-call | tf_op jit(solution)/shard_map/pallas_call | solution.py:40
  74.3 0.5 collective-permute-start.12
  74.8 2.4 %collective-permute-start.13 = (f32[66,8,128]{2,1,0:T(8,128)S(1)}, f32[66,8,128]{2,1,0:T(8,128)S(1)}, u32[]{:S(2)}, u32[]{:S(2)}) collective-permute-start(f32[66,8,128]{2,1,0:T(8,128)S(1)} %get-tuple-element.84), channel_id=1, source_target_pairs={{0,8},{4,12},{8,0},{12,4},{16,24},{20,28},{24,16},{28,20},{1,9},{5... | collective-permute-start | bytes 811016 | tf_op jit(solution)/shard_map/ppermute | solution.py:589
  77.2 0.7 collective-permute-start.15
  77.9 0.8 collective-permute-start.16
  78.7 5.9 %collective-permute-done.13.refs_2_ = f32[66,8,128]{2,1,0:T(8,128)S(1)} collective-permute-done((f32[66,8,128]{2,1,0:T(8,128)S(1)}, f32[66,8,128]{2,1,0:T(8,128)S(1)}, u32[]{:S(2)}, u32[]{:S(2)}) %collective-permute-start.13) | collective-permute-done | bytes 270368 | tf_op jit(solution)/shard_map/ppermute | solution.py:589
  84.5 1.0 collective-permute-start.17
  85.5 11.8 %collective-permute-done.14.refs_3_ = f32[66,8,128]{2,1,0:T(8,128)S(1)} collective-permute-done((f32[66,8,128]{2,1,0:T(8,128)S(1)}, f32[66,8,128]{2,1,0:T(8,128)S(1)}, u32[]{:S(2)}, u32[]{:S(2)}) %collective-permute-start.14) | collective-permute-done | bytes 270368 | tf_op jit(solution)/shard_map/ppermute | solution.py:589
  97.3 8.1 %collective-permute-done.16.refs_5_ = f32[66,8,128]{2,1,0:T(8,128)S(1)} collective-permute-done((f32[66,8,128]{2,1,0:T(8,128)S(1)}, f32[66,8,128]{2,1,0:T(8,128)S(1)}, u32[]{:S(2)}, u32[]{:S(2)}) %collective-permute-start.16) | collective-permute-done | bytes 270368 | tf_op jit(solution)/shard_map/ppermute | solution.py:589
  105.4 6.0 %shard_map.55 = (f32[2,32,64,128]{3,2,1,0:T(8,128)}, f32[8,128]{1,0:T(8,128)S(1)}) custom-call(f32[2,32,64,128]{3,2,1,0:T(8,128)S(1)} %bitcast.31, f32[278,8,128]{2,1,0:T(8,128)S(1)} %get-tuple-element.49.s_ext, f32[278,8,128]{2,1,0:T(8,128)S(1)} %get-tuple-element.50.w_ext, f32[258,8,128]{2,1,0:T(8,128)S(1)} %get-tuple-element.60.base0, ...), custom_call_target="tpu_custom_call" | custom-call | tf_op jit(solution)/shard_map/pallas_call | solution.py:40
  111.5 16.0 %all_to_all.5 = f32[32,8,128]{2,1,0:T(8,128)S(1)} all-to-all(f32[32,8,128]{2,1,0:T(8,128)S(1)} %broadcast_in_dim.2), channel_id=1, replica_groups=mesh['tm'=8,'space'=4] {'tm','space'}, dimensions={0} | all-to-all | bytes 262144 | tf_op jit(solution)/shard_map/all_to_all | solution.py:628
  127.5 0.1 reduce_sum.9
  127.6 0.5 multiply_sqrt_fusion
  (23 shorter events, 0.1 us)
Async XLA Ops:
  0.6 10.1 %copy-start = (f32[2,256,1024]{2,1,0:T(8,128)S(1)}, f32[2,256,1024]{2,1,0:T(8,128)}, u32[]{:S(2)}) copy-start(f32[2,256,1024]{2,1,0:T(8,128)} %param.3) | copy-start | bytes 6291460
  0.6 10.0 %copy-start.1 = (f32[2,256,1024]{2,1,0:T(8,128)S(1)}, f32[2,256,1024]{2,1,0:T(8,128)}, u32[]{:S(2)}) copy-start(f32[2,256,1024]{2,1,0:T(8,128)} %param.4) | copy-start | bytes 6291460
  0.6 10.0 %copy-start.2 = (f32[256,1024]{1,0:T(8,128)S(1)}, f32[256,1024]{1,0:T(8,128)}, u32[]{:S(2)}) copy-start(f32[256,1024]{1,0:T(8,128)} %param.5) | copy-start | bytes 3145732
  2.0 8.6 %collective-permute-start = (f32[55,8,128]{2,1,0:T(8,128)S(1)}, f32[55,8,128]{2,1,0:T(8,128)S(1)}, u32[]{:S(2)}, u32[]{:S(2)}) collective-permute-start(f32[55,8,128]{2,1,0:T(8,128)S(1)} %get-tuple-element.47), channel_id=1, source_target_pairs={{0,1},{2,3},{1,0},{3,2},{4,5},{6,7},{5,4},{7,6},{8,9},{10,11},{9,8... | collective-permute-start | bytes 675848 | tf_op jit(solution)/shard_map/ppermute | solution.py:565
  5.2 5.5 %collective-permute-start.1 = (f32[55,8,128]{2,1,0:T(8,128)S(1)}, f32[55,8,128]{2,1,0:T(8,128)S(1)}, u32[]{:S(2)}, u32[]{:S(2)}) collective-permute-start(f32[55,8,128]{2,1,0:T(8,128)S(1)} %get-tuple-element.48), channel_id=1, source_target_pairs={{1,2},{2,1},{5,6},{6,5},{9,10},{10,9},{13,14},{14,13},{17,18},{18,... | collective-permute-start | bytes 675848 | tf_op jit(solution)/shard_map/ppermute | solution.py:566
  12.9 10.7 %collective-permute-start.3 = (f32[294,8,128]{2,1,0:T(8,128)S(1)}, f32[294,8,128]{2,1,0:T(8,128)S(1)}, u32[]{:S(2)}, u32[]{:S(2)}) collective-permute-start(f32[294,8,128]{2,1,0:T(8,128)S(1)} %get-tuple-element.51), channel_id=1, source_target_pairs={{0,4},{4,8},{8,12},{12,16},{16,20},{20,24},{24,28},{1,5},{5,9},{9,... | collective-permute-start | bytes 3612680 | tf_op jit(solution)/shard_map/ppermute | solution.py:574
  14.3 9.2 %collective-permute-start.2 = (f32[256,1024]{1,0:T(8,128)S(1)}, f32[256,1024]{1,0:T(8,128)S(1)}, u32[]{:S(2)}, u32[]{:S(2)}) collective-permute-start(f32[256,1024]{1,0:T(8,128)S(1)} %slice_bitcast_fusion), channel_id=1, source_target_pairs={{0,4},{4,8},{8,12},{12,16},{16,20},{20,24},{24,28},{1,5},{5,9},{9,... | collective-permute-start | bytes 3145736 | tf_op jit(solution)/shard_map/ppermute | solution.py:560
  25.6 22.8 %collective-permute-start.4 = (f32[47,8,128]{2,1,0:T(8,128)S(1)}, f32[47,8,128]{2,1,0:T(8,128)S(1)}, u32[]{:S(2)}, u32[]{:S(2)}) collective-permute-start(f32[47,8,128]{2,1,0:T(8,128)S(1)} %get-tuple-element.63), channel_id=1, source_target_pairs={{0,4},{4,0},{8,12},{12,8},{16,20},{20,16},{24,28},{28,24},{1,5},{5... | collective-permute-start | bytes 577544 | tf_op jit(solution)/shard_map/ppermute | solution.py:589
  43.3 8.1 %collective-permute-start.5 = (f32[47,8,128]{2,1,0:T(8,128)S(1)}, f32[47,8,128]{2,1,0:T(8,128)S(1)}, u32[]{:S(2)}, u32[]{:S(2)}) collective-permute-start(f32[47,8,128]{2,1,0:T(8,128)S(1)} %get-tuple-element.64), channel_id=1, source_target_pairs={{0,8},{4,12},{8,0},{12,4},{16,24},{20,28},{24,16},{28,20},{1,9},{5... | collective-permute-start | bytes 577544 | tf_op jit(solution)/shard_map/ppermute | solution.py:589
  45.7 9.3 %collective-permute-start.6 = (f32[47,8,128]{2,1,0:T(8,128)S(1)}, f32[47,8,128]{2,1,0:T(8,128)S(1)}, u32[]{:S(2)}, u32[]{:S(2)}) collective-permute-start(f32[47,8,128]{2,1,0:T(8,128)S(1)} %get-tuple-element.65), channel_id=1, source_target_pairs={{0,12},{4,8},{8,4},{12,0},{16,28},{20,24},{24,20},{28,16},{1,13},{... | collective-permute-start | bytes 577544 | tf_op jit(solution)/shard_map/ppermute | solution.py:589
  45.8 9.3 %collective-permute-start.7 = (f32[47,8,128]{2,1,0:T(8,128)S(1)}, f32[47,8,128]{2,1,0:T(8,128)S(1)}, u32[]{:S(2)}, u32[]{:S(2)}) collective-permute-start(f32[47,8,128]{2,1,0:T(8,128)S(1)} %get-tuple-element.66), channel_id=1, source_target_pairs={{0,16},{4,20},{8,24},{12,28},{16,0},{20,4},{24,8},{28,12},{1,17},{... | collective-permute-start | bytes 577544 | tf_op jit(solution)/shard_map/ppermute | solution.py:589
  48.4 17.4 %collective-permute-start.8 = (f32[47,8,128]{2,1,0:T(8,128)S(1)}, f32[47,8,128]{2,1,0:T(8,128)S(1)}, u32[]{:S(2)}, u32[]{:S(2)}) collective-permute-start(f32[47,8,128]{2,1,0:T(8,128)S(1)} %get-tuple-element.67), channel_id=1, source_target_pairs={{0,20},{4,16},{8,28},{12,24},{16,4},{20,0},{24,12},{28,8},{1,21},{... | collective-permute-start | bytes 577544 | tf_op jit(solution)/shard_map/ppermute | solution.py:589
  48.4 17.4 %collective-permute-start.9 = (f32[47,8,128]{2,1,0:T(8,128)S(1)}, f32[47,8,128]{2,1,0:T(8,128)S(1)}, u32[]{:S(2)}, u32[]{:S(2)}) collective-permute-start(f32[47,8,128]{2,1,0:T(8,128)S(1)} %get-tuple-element.68), channel_id=1, source_target_pairs={{0,24},{4,28},{8,16},{12,20},{16,8},{20,12},{24,0},{28,4},{1,25},{... | collective-permute-start | bytes 577544 | tf_op jit(solution)/shard_map/ppermute | solution.py:589
  51.4 14.4 %collective-permute-start.10 = (f32[47,8,128]{2,1,0:T(8,128)S(1)}, f32[47,8,128]{2,1,0:T(8,128)S(1)}, u32[]{:S(2)}, u32[]{:S(2)}) collective-permute-start(f32[47,8,128]{2,1,0:T(8,128)S(1)} %get-tuple-element.69), channel_id=1, source_target_pairs={{0,28},{4,24},{8,20},{12,16},{16,12},{20,8},{24,4},{28,0},{1,29},{... | collective-permute-start | bytes 577544 | tf_op jit(solution)/shard_map/ppermute | solution.py:589
  65.8 39.6 %collective-permute-start.11 = (f32[256,8,128]{2,1,0:T(8,128)S(1)}, f32[256,8,128]{2,1,0:T(8,128)S(1)}, u32[]{:S(2)}, u32[]{:S(2)}) collective-permute-start(f32[256,8,128]{2,1,0:T(8,128)S(1)} %get-tuple-element.71), channel_id=1, source_target_pairs={{0,4},{4,8},{8,12},{12,16},{16,20},{20,24},{24,28},{1,5},{5,9},{9,... | collective-permute-start | bytes 3145736 | tf_op jit(solution)/shard_map/ppermute | solution.py:594
  74.3 3.6 %collective-permute-start.12 = (f32[66,8,128]{2,1,0:T(8,128)S(1)}, f32[66,8,128]{2,1,0:T(8,128)S(1)}, u32[]{:S(2)}, u32[]{:S(2)}) collective-permute-start(f32[66,8,128]{2,1,0:T(8,128)S(1)} %get-tuple-element.83), channel_id=1, source_target_pairs={{0,4},{4,0},{8,12},{12,8},{16,20},{20,16},{24,28},{28,24},{1,5},{5... | collective-permute-start | bytes 811016 | tf_op jit(solution)/shard_map/ppermute | solution.py:589
  74.8 9.7 %collective-permute-start.13 = (f32[66,8,128]{2,1,0:T(8,128)S(1)}, f32[66,8,128]{2,1,0:T(8,128)S(1)}, u32[]{:S(2)}, u32[]{:S(2)}) collective-permute-start(f32[66,8,128]{2,1,0:T(8,128)S(1)} %get-tuple-element.84), channel_id=1, source_target_pairs={{0,8},{4,12},{8,0},{12,4},{16,24},{20,28},{24,16},{28,20},{1,9},{5... | collective-permute-start | bytes 811016 | tf_op jit(solution)/shard_map/ppermute | solution.py:589
  77.2 20.1 %collective-permute-start.14 = (f32[66,8,128]{2,1,0:T(8,128)S(1)}, f32[66,8,128]{2,1,0:T(8,128)S(1)}, u32[]{:S(2)}, u32[]{:S(2)}) collective-permute-start(f32[66,8,128]{2,1,0:T(8,128)S(1)} %get-tuple-element.85), channel_id=1, source_target_pairs={{0,12},{4,8},{8,4},{12,0},{16,28},{20,24},{24,20},{28,16},{1,13},{... | collective-permute-start | bytes 811016 | tf_op jit(solution)/shard_map/ppermute | solution.py:589
  77.2 20.1 %collective-permute-start.15 = (f32[66,8,128]{2,1,0:T(8,128)S(1)}, f32[66,8,128]{2,1,0:T(8,128)S(1)}, u32[]{:S(2)}, u32[]{:S(2)}) collective-permute-start(f32[66,8,128]{2,1,0:T(8,128)S(1)} %get-tuple-element.86), channel_id=1, source_target_pairs={{0,16},{4,20},{8,24},{12,28},{16,0},{20,4},{24,8},{28,12},{1,17},{... | collective-permute-start | bytes 811016 | tf_op jit(solution)/shard_map/ppermute | solution.py:589
  77.9 27.5 %collective-permute-start.16 = (f32[66,8,128]{2,1,0:T(8,128)S(1)}, f32[66,8,128]{2,1,0:T(8,128)S(1)}, u32[]{:S(2)}, u32[]{:S(2)}) collective-permute-start(f32[66,8,128]{2,1,0:T(8,128)S(1)} %get-tuple-element.87), channel_id=1, source_target_pairs={{0,20},{4,16},{8,28},{12,24},{16,4},{20,0},{24,12},{28,8},{1,21},{... | collective-permute-start | bytes 811016 | tf_op jit(solution)/shard_map/ppermute | solution.py:589
  84.5 20.9 %collective-permute-start.17 = (f32[66,8,128]{2,1,0:T(8,128)S(1)}, f32[66,8,128]{2,1,0:T(8,128)S(1)}, u32[]{:S(2)}, u32[]{:S(2)}) collective-permute-start(f32[66,8,128]{2,1,0:T(8,128)S(1)} %get-tuple-element.88), channel_id=1, source_target_pairs={{0,24},{4,28},{8,16},{12,20},{16,8},{20,12},{24,0},{28,4},{1,25},{... | collective-permute-start | bytes 811016 | tf_op jit(solution)/shard_map/ppermute | solution.py:589
  97.3 8.1 %collective-permute-start.18 = (f32[66,8,128]{2,1,0:T(8,128)S(1)}, f32[66,8,128]{2,1,0:T(8,128)S(1)}, u32[]{:S(2)}, u32[]{:S(2)}) collective-permute-start(f32[66,8,128]{2,1,0:T(8,128)S(1)} %get-tuple-element.89), channel_id=1, source_target_pairs={{0,28},{4,24},{8,20},{12,16},{16,12},{20,8},{24,4},{28,0},{1,29},{... | collective-permute-start | bytes 811016 | tf_op jit(solution)/shard_map/ppermute | solution.py:589

commit v3 on v2

--- a/solution.py
+++ b/solution.py
@@ -12,7 +12,9 @@
 KEEP = 1.0 - DAMPING
 GROUP = 2 ** (LEVELS - 1)
 TEAM = GROUP // 2
+SWAPS = (2, 6, 4, 3, 7, 5, 1)
 HALO = 2 * LEVELS + 1
+SIDE = HALO - 1
 EDGE = 2
 REACH = 2 * LEVELS - 3
 
@@ -33,7 +35,7 @@
     return [pltpu.with_memory_space_constraint(x, pltpu.VMEM) for x in arrays]
 
 
-def kernel_call(body, outs, scratch=(), flops=0, n_in=0, specs=None, grid=()):
+def kernel_call(body, outs, scratch=(), flops=0, n_in=0, specs=None, grid=(), more=()):
     def call(*args):
         held = sum(math.prod(dims) for dims in scratch)
         held += sum(math.prod(x.shape) for x in list(outs) + list(args))
@@ -43,7 +45,7 @@
             grid=grid,
             in_specs=specs or [vmem() for _ in range(n_in)],
             out_specs=[vmem() for _ in outs],
-            scratch_shapes=[pltpu.VMEM(dims, jnp.float32) for dims in scratch],
+            scratch_shapes=[pltpu.VMEM(dims, jnp.float32) for dims in scratch] + list(more),
             compiler_params=pltpu.CompilerParams(vmem_limit_bytes=4 * held + 2**21),
             cost_estimate=pl.CostEstimate(flops=flops, bytes_accessed=flops, transcendentals=0),
         )(*args)
@@ -101,7 +103,7 @@
     return None if quiet else value
 
 
-BLOCK = 32
+BLOCK = 64
 
 
 def padded(rows):
@@ -130,7 +132,9 @@
     pl.when(jnp.logical_not(flag))(lambda: body(one, two))
 
 
-def pack_edges(g_top, r_top, d_top, g_end, r_end, d_end, pair, other):
+def pack_edges(guess, g_top, r_top, d_top, g_end, r_end, d_end, pair, other, later, done):
+    copy = pltpu.make_async_copy(guess.at[1], later, done)
+    copy.start()
     count = g_top.shape[1] * 8
     refs = [((g_top, (t,)), (g_end, (t,))) for t in range(2)]
     refs += [((r_top, (t,)), (r_end, (t,))) for t in range(2)]
@@ -144,10 +148,33 @@
                 end[i * HALO + k] = strided(b, lead_b, row // 8, row % 8)
 
     either(odd_strip(), fill, pair, other)
-
-
-def first_sweep(guess, rhs, diff, pair, other, s_ext, w_ext, send, g0, g1, low, high):
+    copy.wait()
+
+
+def first_sweep(guess, rhs, diff, send, g1):
     rows = guess.shape[1] * 8
+    m = masks()
+
+    def unpack(g):
+        for k in range(8):
+            i = g * 8 + k
+            g1[1 + i] = strided(guess, (1,), g, k)
+
+    loop(0, rows // 8, unpack, unroll=2)
+
+    def sweep(g):
+        for k in range(8):
+            i = g * 8 + k
+            s = strided(diff, (), g, k)
+            w = DAMPING / (1.0 + 4.0 * s)
+            whole = strided(rhs, (1,), g, k) + s * around(g1, 1 + i, m) + strided(guess, (0,), g, k)
+            send[i] = KEEP * g1[1 + i] + w * whole
+
+    loop(0, rows // 8, sweep, unroll=4)
+
+
+def local_parts(guess, rhs, diff, pair, other, s_ext, w_ext, part0, left0, left1, v1, edges, g0, g1, low, high):
+    rows = rhs.shape[1] * 8
     m = masks()
 
     def unpack(g):
@@ -173,39 +200,11 @@
         for i in (k, HALO + rows + k):
             w_ext[i] = DAMPING / (1.0 + 4.0 * s_ext[i])
 
-    def sweep(i, source):
-        return KEEP * g1[i] + w_ext[i] * (source + s_ext[i] * around(g1, i, m) + g0[i])
-
-    def inner(g):
-        for k in range(8):
-            i = HALO + g * 8 + k
-            send[i - 2] = sweep(i, strided(rhs, (1,), g, k))
-
-    loop(0, rows // 8, inner, unroll=4)
-    for k in range(2, HALO):
-        send[k - 2] = sweep(k, low[3 * HALO + k])
-    for k in range(0, HALO - 2):
-        i = HALO + rows + k
-        send[i - 2] = sweep(i, high[3 * HALO + k])
-    tail = rows + 2 * (HALO - 2)
-    for k in range(HALO - 1):
-        send[tail + k] = g1[1 + k]
-        send[tail + HALO - 1 + k] = g1[HALO + rows + k]
-
-
-def local_parts(rhs, low, high, s_ext, w_ext, g0, g1, part0, left0, left1, v1):
-    rows = rhs.shape[1] * 8
-    m = masks()
-
-    def sweep0(i, source):
-        return KEEP * g0[i] + w_ext[i] * (source + s_ext[i] * around(g0, i, m))
-
-    def sweep1(i, source):
-        return KEEP * g1[i] + w_ext[i] * (source + s_ext[i] * around(g1, i, m) + g0[i])
-
     def fill(i, a, b):
-        part0[i] = sweep0(i, a)
-        v1[i] = sweep1(i, b)
+        s = s_ext[i]
+        w = w_ext[i]
+        part0[i] = KEEP * g0[i] + w * (a + s * around(g0, i, m))
+        v1[i] = KEEP * g1[i] + w * (b + s * around(g1, i, m) + g0[i])
 
     def inner(g):
         for k in range(8):
@@ -216,6 +215,11 @@
         fill(k, low[2 * HALO + k], low[3 * HALO + k])
     for k in range(0, HALO - 1):
         fill(HALO + rows + k, high[2 * HALO + k], high[3 * HALO + k])
+    for k in range(SIDE):
+        edges[k] = v1[2 + k]
+        edges[SIDE + k] = v1[HALO + rows - 1 + k]
+        edges[2 * SIDE + k] = g1[1 + k]
+        edges[3 * SIDE + k] = g1[HALO + rows + k]
 
     def rest(i, a, b):
         s = s_ext[i]
@@ -244,13 +248,12 @@
     return piece, piece + 2 * REACH, start
 
 
-def join_first(start_of, window, g_prev, got, s_ext, w_ext, part0, left0, left1, v1, *refs):
+def join_first(start_of, window, g_prev, got, edges, s_ext, w_ext, part0, left0, left1, v1, *refs):
     outs = refs[:TEAM]
-    base0, base1, back, norm, y, coarse = refs[TEAM:]
+    base0, base1, back1, back2, norm, y, coarse = refs[TEAM:]
     place = place_of()
-    rows = g_prev.shape[0] * 8
+    rows = got.shape[0]
     m = masks()
-    tail = rows + 2 * (HALO - 2)
 
     def inner(g):
         for k in range(8):
@@ -258,20 +261,19 @@
             y[i] = w_ext[i] * strided(g_prev, (), g, k)
 
     loop(0, rows // 8, inner, unroll=2)
-    for k in range(HALO - 1):
-        i = 1 + k
-        y[i] = w_ext[i] * got[tail + k]
+    for k in range(SIDE):
+        y[1 + k] = w_ext[1 + k] * edges[2 * SIDE + k]
         i = HALO + rows + k
-        y[i] = w_ext[i] * got[tail + HALO - 1 + k]
-
-    def resid(i):
+        y[i] = w_ext[i] * edges[3 * SIDE + k]
+
+    def resid(i, swept):
         s = s_ext[i]
         here = y[i]
-        a = left0[i] - (1.0 + 4.0 * s) * here + s * around(y, i, m) + got[i - 2]
+        a = left0[i] - (1.0 + 4.0 * s) * here + s * around(y, i, m) + swept
         return a, left1[i] + here
 
-    def edge(i):
-        a, b = resid(i)
+    def edge(i, swept):
+        a, b = resid(i, swept)
         coarse[i] = a + b
         return a, b
 
@@ -282,17 +284,31 @@
         base1[i - HALO + 1] = value
         return value
 
-    def main(i, acc):
-        a, b = edge(i)
-        back[i - HALO] = based(i, a, b)
-        return acc + (a * a + b * b)
-
-    norm[...] = loop(HALO, HALO + rows, main, jnp.zeros((8, 128), jnp.float32), unroll=32)
-    for i in (HALO - 1, HALO + rows):
-        a, b = edge(i)
-        based(i, a, b)
-    for i in list(range(2, HALO - 1)) + list(range(HALO + rows + 1, 2 * HALO + rows - 2)):
-        edge(i)
+    acc = jnp.zeros((8, 128), jnp.float32)
+    first = HALO
+    for back in (back1, back2):
+
+        def main(i, acc, back=back, first=first):
+            a, b = edge(i, got[i - HALO])
+            back[i - first] = based(i, a, b)
+            return acc + (a * a + b * b)
+
+        low = max(first, HALO + 1)
+        high = min(first + back.shape[0], HALO + rows - 1)
+        acc = loop(low, high, main, acc, unroll=32)
+        first += back.shape[0]
+    for k in range(SIDE):
+        for i, at in ((2 + k, k), (HALO + rows - 1 + k, SIDE + k)):
+            a, b = edge(i, edges[at])
+            if HALO - 1 <= i <= HALO + rows:
+                value = based(i, a, b)
+            if i == HALO:
+                back1[0] = value
+                acc = acc + (a * a + b * b)
+            if i == HALO + rows - 1:
+                back2[back2.shape[0] - 1] = value
+                acc = acc + (a * a + b * b)
+    norm[...] = acc
     for k, out in enumerate(outs):
         low = start_of(place ^ k) - REACH + HALO
 
@@ -437,9 +453,9 @@
         loop(0, piece, copy, unroll=11)
 
 
-def finish(start_of, piece, rhs, s_ext, w_ext, base0, base1, back, norm0, norms, *refs):
+def finish(start_of, piece, rhs, s_ext, w_ext, base0, base1, *refs):
     fields = refs[:TEAM]
-    out, sums, e, before, sol0, sol1 = refs[TEAM:]
+    out, left, norm, e, before, sol0, sol1 = refs[TEAM:]
     rows = rhs.shape[1] * 8
     m = masks()
     place = place_of()
@@ -460,7 +476,7 @@
         sol0[i] = base0[i] + part + w * before[i + 1]
         sol1[i] = base1[i] + part + w * here
 
-    loop(0, rows + 2, correct, unroll=24)
+    loop(0, rows + 2, correct, unroll=43)
 
     def last(g, acc):
         for k in range(8):
@@ -469,18 +485,31 @@
             w = w_ext[i + HALO]
             diag = 1.0 + 4.0 * s
             past = before[i + EDGE]
-            past = back[i] + KEEP * past + w * (s * around(before, i + EDGE, m) + past)
+            past = KEEP * past + w * (s * around(before, i + EDGE, m) + past)
             a = sol0[i + 1]
             b = sol1[i + 1]
-            ra = strided(rhs, (0,), g, k) - diag * a + s * around(sol0, i + 1, m) + past
+            left[i] = strided(rhs, (0,), g, k) - diag * a + s * around(sol0, i + 1, m) + past
             rb = strided(rhs, (1,), g, k) - diag * b + s * around(sol1, i + 1, m) + a
             out[0, g, pl.ds(k, 8, stride=8)] = a
             out[1, g, pl.ds(k, 8, stride=8)] = b
-            acc = acc + (ra * ra + rb * rb)
+            acc = acc + rb * rb
         return acc
 
-    final = loop(0, rows // 8, last, jnp.zeros((8, 128), jnp.float32), unroll=2)
-    parts = [norm0[...]] + [norms[k] for k in range(LEVELS - 1)] + [final]
+    norm[...] = loop(0, rows // 8, last, jnp.zeros((8, 128), jnp.float32), unroll=2)
+
+
+def add_up(left, back1, back2, norm0, norms, norm, sums):
+    acc = norm[...]
+    first = 0
+    for back in (back1, back2):
+
+        def body(i, acc, back=back, first=first):
+            r = left[first + i] + back[i]
+            return acc + r * r
+
+        acc = loop(0, back.shape[0], body, acc, unroll=16)
+        first += back.shape[0]
+    parts = [norm0[...]] + [norms[k] for k in range(LEVELS - 1)] + [acc]
     for k, part in enumerate(parts):
         sums[pl.ds(k, 1)] = jnp.sum(part, axis=0, keepdims=True)
     for k in range(len(parts), 8):
@@ -557,41 +586,48 @@
         flat = pl.BlockSpec((edge_groups, wide, 128), lambda i: (block, 0, 0))
         return [time, time, flat]
 
-    g_prev = tiles(lax.ppermute(guess[1], "tm", later))
     far_args = [pltpu.with_memory_space_constraint(x, pltpu.HBM) for x in (guess_t, rhs_t, diff_t)]
-    facing, backing = kernel_call(
-        pack_edges, [shape(5 * HALO, 8, 128)] * 2, specs=edge_specs(0) + edge_specs(far), grid=(1,)
-    )(*far_args, *far_args)
+    facing, backing, g_prev = kernel_call(
+        pack_edges,
+        [shape(5 * HALO, 8, 128), shape(5 * HALO, 8, 128), shape(groups, wide, 128)],
+        specs=[pl.BlockSpec(memory_space=pl.ANY)] + edge_specs(0) + edge_specs(far),
+        grid=(1,),
+        more=[pltpu.SemaphoreType.DMA(())],
+    )(far_args[0], *far_args, *far_args)
+    g_prev = lax.ppermute(g_prev, "tm", later)
     facing = lax.ppermute(facing, "space", both(0))
     backing = lax.ppermute(backing, "space", both(1))
-
-    sent = rows + 2 * (HALO - 2) + 2 * (HALO - 1)
-    s_ext, w_ext, send, g0, g1, low, high = kernel_call(
-        first_sweep,
-        [kept(ext, 8, 128)] * 2 + [shape(sent, 8, 128)] + [shape(ext, 8, 128)] * 2 + [shape(5 * HALO, 8, 128)] * 2,
+    (send,) = kernel_call(first_sweep, [shape(rows, 8, 128)], scratch=[(rows + 2, 8, 128)], n_in=3)(
+        guess_t, rhs_t, diff_t
+    )
+    got = lax.ppermute(send, "tm", later)
+    s_ext, w_ext, part0, left0, left1, v1, edges = kernel_call(
+        local_parts,
+        [kept(ext, 8, 128)] * 2 + [shape(ext, 8, 128)] * 4 + [shape(4 * SIDE, 8, 128)],
+        scratch=[(ext, 8, 128)] * 2 + [(5 * HALO, 8, 128)] * 2,
         n_in=5,
     )(guess_t, rhs_t, diff_t, facing, backing)
-    got = lax.ppermute(send, "tm", later)
-    part0, left0, left1, v1 = kernel_call(local_parts, [shape(ext, 8, 128)] * 4, n_in=7, flops=10**7)(
-        rhs_t, low, high, s_ext, w_ext, g0, g1
-    )
-    *mine, base0, base1, back, norm0 = kernel_call(
+    edges = lax.ppermute(edges, "tm", later)
+    one = rows * 5 // 80 * 10
+    *mine, base0, base1, back1, back2, norm0 = kernel_call(
         functools.partial(join_first, start_of, window),
         [shape(window, 8, 128)] * TEAM
-        + [kept(rows + 2, 8, 128), kept(rows + 2, 8, 128), shape(rows, 8, 128), shape(8, 128)],
+        + [kept(rows + 2, 8, 128)] * 2
+        + [shape(one, 8, 128), shape(rows - one, 8, 128), shape(8, 128)],
         scratch=[(ext, 8, 128)] * 2,
-        n_in=8,
-    )(g_prev, got, s_ext, w_ext, part0, left0, left1, v1)
+        n_in=9,
+    )(g_prev, got, edges, s_ext, w_ext, part0, left0, left1, v1)
 
     def exchange(parts):
-        moved = [parts[0]]
-        for k in range(1, TEAM):
-            moved.append(lax.ppermute(parts[k], "tm", [(i, i ^ k) for i in range(count)]))
+        moved = list(parts)
+        for k in SWAPS:
+            moved[k] = lax.ppermute(parts[k], "tm", [(i, i ^ k) for i in range(count)])
         return moved
 
     mine = exchange(mine)
-    *mine, back = lax.optimization_barrier((*mine, back))
-    back = lax.ppermute(back, "tm", later)
+    *mine, back1 = lax.optimization_barrier((*mine, back1))
+    back1 = lax.ppermute(back1, "tm", later)
+    back2 = lax.ppermute(back2, "tm", later)
     if count == TEAM:
         tall = padded(window)
         half = [(TEAM >> level, tall, 8, 128) for level in range(LEVELS)]
@@ -617,12 +653,13 @@
     fields = exchange(fields)
 
     s_ext, w_ext, base0, base1 = keep(s_ext, w_ext, base0, base1)
-    out, sums = kernel_call(
+    out, left, norm = kernel_call(
         functools.partial(finish, start_of, piece),
-        [shape(2, groups, wide, 128), shape(8, 128)],
+        [shape(2, groups, wide, 128), shape(rows, 8, 128), shape(8, 128)],
         scratch=[(rows + 2 * EDGE, 8, 128)] * 2 + [(rows + 2, 8, 128)] * 2,
-        n_in=8 + TEAM,
-    )(rhs_t, s_ext, w_ext, base0, base1, back, norm0, norms, *fields)
+        n_in=5 + TEAM,
+    )(rhs_t, s_ext, w_ext, base0, base1, *fields)
+    (sums,) = kernel_call(add_up, [shape(8, 128)], n_in=6)(left, back1, back2, norm0, norms, norm)
 
     every = jnp.broadcast_to(sums[None], (count * strips, 8, 128))
     every = lax.all_to_all(every, ("tm", "space"), 0, 0)

time: 128 us -> 131 us (1.023)
  local copies, waits for them, and re-layouts: 0.09 us -> 4.43 us
  starting transfers between devices: 43.1 us -> 40.6 us
    unnamed x6 -> x12, local copies, waits for them, and re-layouts: 0.01 us -> 4.42 us
    ppermute x16 -> x18, starting transfers between devices: 37.9 us -> 35.7 us  [the longest x14 25.9 us: exchange(): moved[k] = lax.ppermute(parts[k], 'tm', [(i, i ^ k) for i in range(count)])]
    ppermute x1, starting transfers between devices: 3.12 us -> 1.64 us  [body(): facing = lax.ppermute(facing, 'space', both(0))]
    pallas_call x6 -> x7, Pallas kernels: 22.9 us -> 23.4 us  [call(): pl.pallas_call(body, out_shape=outs, grid=grid, in_specs=specs or [vmem()...]
    ppermute x16 -> x18, waiting for transfers between devices: 39.8 us -> 40.1 us  [the longest x14 39.1 us: exchange(): moved[k] = lax.ppermute(parts[k], 'tm', [(i, i ^ k) for i in range(count)])]
  transfers between devices with their start and end apart: 19 -> 21, of which waited for: 7 -> 8; matrix products, arithmetic and copies ran while one was open for 0% -> 0% of each run, Pallas kernels for 9% -> 11%
where the time goes in v3:
time: 131 us
  waiting for transfers between devices  45.2 us (35%)
  starting transfers between devices  40.6 us (31%)
  Pallas kernels  23.4 us (18%)
  blocking collectives  15.8 us (12%)
  local copies, waits for them, and re-layouts  4.43 us (3%)
    ppermute x14, waiting for transfers between devices, exchange(): moved[k] = lax.ppermute(parts[k], 'tm', [(i, i ^ k) for i in range(count)])  39.1 us
    ppermute x14, starting transfers between devices, exchange(): moved[k] = lax.ppermute(parts[k], 'tm', [(i, i ^ k) for i in range(count)])  25.9 us
    pallas_call x7, Pallas kernels, call(): pl.pallas_call(body, out_shape=outs, grid=grid, in_specs=specs or [vmem()...  23.4 us
    all_to_all x1, blocking collectives, body(): every = lax.all_to_all(every, ('tm', 'space'), 0, 0)  15.8 us
    ppermute x1, waiting for transfers between devices, body(): facing = lax.ppermute(facing, 'space', both(0))  5.12 us
    ppermute x1, starting transfers between devices, body(): g_prev = lax.ppermute(g_prev, 'tm', later)  4.5 us
    unnamed x12, local copies, waits for them, and re-layouts  4.42 us
  transfers between devices with their start and end apart: 21, of which 8 were waited for; matrix products, arithmetic and copies ran while one was open for 0% of the time, Pallas kernels for 11%

profile of v3, /device:TPU:0, one launch (start us, length us, event | category | flops | bytes accessed | tf_op | source)
XLA Modules:
  0.0 130.9 jit_solution(11368401032208799322)
XLA Ops:
  0.6 1.6 %copy-done = f32[2,256,1024]{2,1,0:T(8,128)S(1)} copy-done((f32[2,256,1024]{2,1,0:T(8,128)S(1)}, f32[2,256,1024]{2,1,0:T(8,128)}, u32[]{:S(2)}) %copy-start) | copy-done | bytes 2097176
  2.2 1.6 %copy-done.2 = f32[2,256,1024]{2,1,0:T(8,128)S(1)} copy-done((f32[2,256,1024]{2,1,0:T(8,128)S(1)}, f32[2,256,1024]{2,1,0:T(8,128)}, u32[]{:S(2)}) %copy-start.2) | copy-done | bytes 2097176
  3.8 1.2 copy-done.4
  5.0 1.5 %shard_map.52 = f32[256,8,128]{2,1,0:T(8,128)S(1)} custom-call(f32[2,32,64,128]{3,2,1,0:T(8,128)S(1)} %bitcast.23, f32[2,32,64,128]{3,2,1,0:T(8,128)S(1)} %bitcast.27, f32[32,64,128]{2,1,0:T(8,128)S(1)} %bitcast.32), custom_call_target="tpu_custom_call" | custom-call | tf_op jit(solution)/shard_map/pallas_call | solution.py:42
  6.6 2.6 %collective-permute-start.3 = (f32[256,8,128]{2,1,0:T(8,128)S(1)}, f32[256,8,128]{2,1,0:T(8,128)S(1)}, u32[]{:S(2)}, u32[]{:S(2)}) collective-permute-start(f32[256,8,128]{2,1,0:T(8,128)S(1)} %shard_map.52), channel_id=1, source_target_pairs={{0,4},{4,8},{8,12},{12,16},{16,20},{20,24},{24,28},{1,5},{5,9},{9,... | collective-permute-start | bytes 3145736 | tf_op jit(solution)/shard_map/ppermute | solution.py:603
  9.2 2.8 %shard_map.50 = (f32[55,8,128]{2,1,0:T(8,128)S(1)}, f32[55,8,128]{2,1,0:T(8,128)S(1)}, f32[32,64,128]{2,1,0:T(8,128)S(1)}) custom-call(f32[2,32,64,128]{3,2,1,0:T(8,128)} %bitcast.20, f32[2,32,64,128]{3,2,1,0:T(8,128)} %bitcast.21, f32[2,32,64,128]{3,2,1,0:T(8,128)} %bitcast.25, f32[32,64,128]{2,1,0:T(8,128)} %bitcast.30, f32[2,32,64,128]{3,2,1,0:T(8,128)} %bitcast.22, ...), custom_call_target="tpu_custom_call" | custom-call | tf_op jit(solution)/shard_map/pallas_call | solution.py:42
  12.0 4.5 %collective-permute-start.2 = (f32[32,64,128]{2,1,0:T(8,128)S(1)}, f32[32,64,128]{2,1,0:T(8,128)S(1)}, u32[]{:S(2)}, u32[]{:S(2)}) collective-permute-start(f32[32,64,128]{2,1,0:T(8,128)S(1)} %get-tuple-element.50), channel_id=1, source_target_pairs={{0,4},{4,8},{8,12},{12,16},{16,20},{20,24},{24,28},{1,5},{5,9},{9,... | collective-permute-start | bytes 3145736 | tf_op jit(solution)/shard_map/ppermute | solution.py:597
  16.5 1.6 %collective-permute-start = (f32[55,8,128]{2,1,0:T(8,128)S(1)}, f32[55,8,128]{2,1,0:T(8,128)S(1)}, u32[]{:S(2)}, u32[]{:S(2)}) collective-permute-start(f32[55,8,128]{2,1,0:T(8,128)S(1)} %get-tuple-element.46), channel_id=1, source_target_pairs={{0,1},{2,3},{1,0},{3,2},{4,5},{6,7},{5,4},{7,6},{8,9},{10,11},{9,8... | collective-permute-start | bytes 675848 | tf_op jit(solution)/shard_map/ppermute | solution.py:598
  18.8 5.1 %collective-permute-done.pair = f32[55,8,128]{2,1,0:T(8,128)S(1)} collective-permute-done((f32[55,8,128]{2,1,0:T(8,128)S(1)}, f32[55,8,128]{2,1,0:T(8,128)S(1)}, u32[]{:S(2)}, u32[]{:S(2)}) %collective-permute-start) | collective-permute-done | bytes 225312 | tf_op jit(solution)/shard_map/ppermute | solution.py:598
  24.0 5.8 %shard_map.51 = (f32[278,8,128]{2,1,0:T(8,128)S(1)}, f32[278,8,128]{2,1,0:T(8,128)S(1)}, f32[278,8,128]{2,1,0:T(8,128)S(1)}, f32[278,8,128]{2,1,0:T(8,128)S(1)},...) custom-call(f32[2,32,64,128]{3,2,1,0:T(8,128)S(1)} %bitcast.24, ...), custom_call_target="tpu_custom_call" | custom-call | tf_op jit(solution)/shard_map/pallas_call | solution.py:42
  29.8 1.3 collective-permute-start.4
  31.1 1.0 collective-permute-done.4.edges
  32.1 2.0 %shard_map.53 = (f32[47,8,128]{2,1,0:T(8,128)S(1)}, f32[47,8,128]{2,1,0:T(8,128)S(1)}, f32[47,8,128]{2,1,0:T(8,128)S(1)}, f32[47,8,128]{2,1,0:T(8,128)S(1)}, f32...) custom-call(f32[32,64,128]{2,1,0:T(8,128)S(1)} %collective-permute-d, ...), custom_call_target="tpu_custom_call" | custom-call | tf_op jit(solution)/shard_map/pallas_call | solution.py:42
  34.0 4.4 %collective-permute-start.5 = (f32[47,8,128]{2,1,0:T(8,128)S(1)}, f32[47,8,128]{2,1,0:T(8,128)S(1)}, u32[]{:S(2)}, u32[]{:S(2)}) collective-permute-start(f32[47,8,128]{2,1,0:T(8,128)S(1)} %get-tuple-element.59), channel_id=1, source_target_pairs={{0,4},{4,0},{8,12},{12,8},{16,20},{20,16},{24,28},{28,24},{1,5},{5... | collective-permute-start | bytes 577544 | tf_op jit(solution)/shard_map/ppermute | solution.py:624
  38.5 2.4 %collective-permute-start.6 = (f32[47,8,128]{2,1,0:T(8,128)S(1)}, f32[47,8,128]{2,1,0:T(8,128)S(1)}, u32[]{:S(2)}, u32[]{:S(2)}) collective-permute-start(f32[47,8,128]{2,1,0:T(8,128)S(1)} %get-tuple-element.60), channel_id=1, source_target_pairs={{0,8},{4,12},{8,0},{12,4},{16,24},{20,28},{24,16},{28,20},{1,9},{5... | collective-permute-start | bytes 577544 | tf_op jit(solution)/shard_map/ppermute | solution.py:624
  40.9 2.7 %collective-permute-start.8 = (f32[47,8,128]{2,1,0:T(8,128)S(1)}, f32[47,8,128]{2,1,0:T(8,128)S(1)}, u32[]{:S(2)}, u32[]{:S(2)}) collective-permute-start(f32[47,8,128]{2,1,0:T(8,128)S(1)} %get-tuple-element.62), channel_id=1, source_target_pairs={{0,16},{4,20},{8,24},{12,28},{16,0},{20,4},{24,8},{28,12},{1,17},{... | collective-permute-start | bytes 577544 | tf_op jit(solution)/shard_map/ppermute | solution.py:624
  43.6 1.7 %collective-permute-start.10 = (f32[47,8,128]{2,1,0:T(8,128)S(1)}, f32[47,8,128]{2,1,0:T(8,128)S(1)}, u32[]{:S(2)}, u32[]{:S(2)}) collective-permute-start(f32[47,8,128]{2,1,0:T(8,128)S(1)} %get-tuple-element.64), channel_id=1, source_target_pairs={{0,24},{4,28},{8,16},{12,20},{16,8},{20,12},{24,0},{28,4},{1,25},{... | collective-permute-start | bytes 577544 | tf_op jit(solution)/shard_map/ppermute | solution.py:624
  45.4 1.2 collective-permute-done.6.refs_2_
  46.6 1.6 %collective-permute-start.11 = (f32[47,8,128]{2,1,0:T(8,128)S(1)}, f32[47,8,128]{2,1,0:T(8,128)S(1)}, u32[]{:S(2)}, u32[]{:S(2)}) collective-permute-start(f32[47,8,128]{2,1,0:T(8,128)S(1)} %get-tuple-element.65), channel_id=1, source_target_pairs={{0,28},{4,24},{8,20},{12,16},{16,12},{20,8},{24,4},{28,0},{1,29},{... | collective-permute-start | bytes 577544 | tf_op jit(solution)/shard_map/ppermute | solution.py:624
  48.2 2.0 %collective-permute-done.7.refs_3_ = f32[47,8,128]{2,1,0:T(8,128)S(1)} collective-permute-done((f32[47,8,128]{2,1,0:T(8,128)S(1)}, f32[47,8,128]{2,1,0:T(8,128)S(1)}, u32[]{:S(2)}, u32[]{:S(2)}) %collective-permute-start.7) | collective-permute-done | bytes 192544 | tf_op jit(solution)/shard_map/ppermute | solution.py:624
  50.2 10.8 %collective-permute-done.9.refs_5_ = f32[47,8,128]{2,1,0:T(8,128)S(1)} collective-permute-done((f32[47,8,128]{2,1,0:T(8,128)S(1)}, f32[47,8,128]{2,1,0:T(8,128)S(1)}, u32[]{:S(2)}, u32[]{:S(2)}) %collective-permute-start.9) | collective-permute-done | bytes 192544 | tf_op jit(solution)/shard_map/ppermute | solution.py:624
  61.0 5.4 %shard_map.54 = (f32[66,8,128]{2,1,0:T(8,128)S(1)}, f32[66,8,128]{2,1,0:T(8,128)S(1)}, f32[66,8,128]{2,1,0:T(8,128)S(1)}, f32[66,8,128]{2,1,0:T(8,128)S(1)}, f32...) custom-call(f32[278,8,128]{2,1,0:T(8,128)S(1)} %get-tuple-element.48, ...), custom_call_target="tpu_custom_call" | custom-call | tf_op jit(solution)/shard_map/pallas_call | solution.py:42
  66.6 2.3 %collective-permute-start.19 = (f32[160,8,128]{2,1,0:T(8,128)S(1)}, f32[160,8,128]{2,1,0:T(8,128)S(1)}, u32[]{:S(2)}, u32[]{:S(2)}) collective-permute-start(f32[160,8,128]{2,1,0:T(8,128)S(1)} %get-tuple-element.85), channel_id=1, source_target_pairs={{0,4},{4,8},{8,12},{12,16},{16,20},{20,24},{24,28},{1,5},{5,9},{9,... | collective-permute-start | bytes 1966088 | tf_op jit(solution)/shard_map/ppermute | solution.py:629
  69.5 2.1 %collective-permute-start.14 = (f32[66,8,128]{2,1,0:T(8,128)S(1)}, f32[66,8,128]{2,1,0:T(8,128)S(1)}, u32[]{:S(2)}, u32[]{:S(2)}) collective-permute-start(f32[66,8,128]{2,1,0:T(8,128)S(1)} %get-tuple-element.78), channel_id=1, source_target_pairs={{0,12},{4,8},{8,4},{12,0},{16,28},{20,24},{24,20},{28,16},{1,13},{... | collective-permute-start | bytes 811016 | tf_op jit(solution)/shard_map/ppermute | solution.py:624
  71.6 0.8 collective-permute-start.15
  72.4 1.8 %collective-permute-start.20 = (f32[96,8,128]{2,1,0:T(8,128)S(1)}, f32[96,8,128]{2,1,0:T(8,128)S(1)}, u32[]{:S(2)}, u32[]{:S(2)}) collective-permute-start(f32[96,8,128]{2,1,0:T(8,128)S(1)} %get-tuple-element.86), channel_id=1, source_target_pairs={{0,4},{4,8},{8,12},{12,16},{16,20},{20,24},{24,28},{1,5},{5,9},{9,... | collective-permute-start | bytes 1179656 | tf_op jit(solution)/shard_map/ppermute | solution.py:630
  74.2 4.0 %collective-permute-done.13.refs_2_ = f32[66,8,128]{2,1,0:T(8,128)S(1)} collective-permute-done((f32[66,8,128]{2,1,0:T(8,128)S(1)}, f32[66,8,128]{2,1,0:T(8,128)S(1)}, u32[]{:S(2)}, u32[]{:S(2)}) %collective-permute-start.13) | collective-permute-done | bytes 270368 | tf_op jit(solution)/shard_map/ppermute | solution.py:624
  78.2 8.6 %collective-permute-start.16 = (f32[66,8,128]{2,1,0:T(8,128)S(1)}, f32[66,8,128]{2,1,0:T(8,128)S(1)}, u32[]{:S(2)}, u32[]{:S(2)}) collective-permute-start(f32[66,8,128]{2,1,0:T(8,128)S(1)} %get-tuple-element.80), channel_id=1, source_target_pairs={{0,20},{4,16},{8,28},{12,24},{16,4},{20,0},{24,12},{28,8},{1,21},{... | collective-permute-start | bytes 811016 | tf_op jit(solution)/shard_map/ppermute | solution.py:624
  86.8 4.4 %collective-permute-done.14.refs_3_ = f32[66,8,128]{2,1,0:T(8,128)S(1)} collective-permute-done((f32[66,8,128]{2,1,0:T(8,128)S(1)}, f32[66,8,128]{2,1,0:T(8,128)S(1)}, u32[]{:S(2)}, u32[]{:S(2)}) %collective-permute-start.14) | collective-permute-done | bytes 270368 | tf_op jit(solution)/shard_map/ppermute | solution.py:624
  91.9 16.6 %collective-permute-done.16.refs_5_ = f32[66,8,128]{2,1,0:T(8,128)S(1)} collective-permute-done((f32[66,8,128]{2,1,0:T(8,128)S(1)}, f32[66,8,128]{2,1,0:T(8,128)S(1)}, u32[]{:S(2)}, u32[]{:S(2)}) %collective-permute-start.16) | collective-permute-done | bytes 270368 | tf_op jit(solution)/shard_map/ppermute | solution.py:624
  108.5 5.6 %shard_map.55 = (f32[2,32,64,128]{3,2,1,0:T(8,128)}, f32[256,8,128]{2,1,0:T(8,128)S(1)}, f32[8,128]{1,0:T(8,128)S(1)}) custom-call(f32[2,32,64,128]{3,2,1,0:T(8,128)S(1)} %bitcast.29, f32[278,8,128]{2,1,0:T(8,128)S(1)} %get-tuple-element.48.s_ext, f32[278,8,128]{2,1,0:T(8,128)S(1)} %get-tuple-element.49.w_ext, f32[258,8,128]{2,1,0:T(8,128)S(1)} %get-tuple-element.56.base0, ...), custom_call_target="tpu_custom_call" | custom-call | tf_op jit(solution)/shard_map/pallas_call | solution.py:42
  114.5 15.8 %all_to_all.5 = f32[32,8,128]{2,1,0:T(8,128)S(1)} all-to-all(f32[32,8,128]{2,1,0:T(8,128)S(1)} %broadcast_in_dim.2), channel_id=1, replica_groups=mesh['tm'=8,'space'=4] {'tm','space'}, dimensions={0} | all-to-all | bytes 262144 | tf_op jit(solution)/shard_map/all_to_all | solution.py:665
  (33 shorter events, 3.2 us)
Async XLA Ops:
  0.6 1.6 %copy-start = (f32[2,256,1024]{2,1,0:T(8,128)S(1)}, f32[2,256,1024]{2,1,0:T(8,128)}, u32[]{:S(2)}) copy-start(f32[2,256,1024]{2,1,0:T(8,128)} %param.4) | copy-start | bytes 6291460
  2.2 1.6 %copy-start.2 = (f32[2,256,1024]{2,1,0:T(8,128)S(1)}, f32[2,256,1024]{2,1,0:T(8,128)}, u32[]{:S(2)}) copy-start(f32[2,256,1024]{2,1,0:T(8,128)} %param.3) | copy-start | bytes 6291460
  3.8 1.2 copy-start.4
  6.6 17.4 %copy-start.5 = (f32[256,1024]{1,0:T(8,128)S(1)}, f32[256,1024]{1,0:T(8,128)}, u32[]{:S(2)}) copy-start(f32[256,1024]{1,0:T(8,128)} %param.5) | copy-start | bytes 3145732
  6.6 25.5 %collective-permute-start.3 = (f32[256,8,128]{2,1,0:T(8,128)S(1)}, f32[256,8,128]{2,1,0:T(8,128)S(1)}, u32[]{:S(2)}, u32[]{:S(2)}) collective-permute-start(f32[256,8,128]{2,1,0:T(8,128)S(1)} %shard_map.52), channel_id=1, source_target_pairs={{0,4},{4,8},{8,12},{12,16},{16,20},{20,24},{24,28},{1,5},{5,9},{9,... | collective-permute-start | bytes 3145736 | tf_op jit(solution)/shard_map/ppermute | solution.py:603
  9.2 14.8 %copy-start.1 = (f32[2,256,1024]{2,1,0:T(8,128)S(1)}, f32[2,256,1024]{2,1,0:T(8,128)}, u32[]{:S(2)}) copy-start(f32[2,256,1024]{2,1,0:T(8,128)} %param.4) | copy-start | bytes 6291460
  9.2 14.8 %copy-start.3 = (f32[2,256,1024]{2,1,0:T(8,128)S(1)}, f32[2,256,1024]{2,1,0:T(8,128)}, u32[]{:S(2)}) copy-start(f32[2,256,1024]{2,1,0:T(8,128)} %param.3) | copy-start | bytes 6291460
  12.0 20.1 %collective-permute-start.2 = (f32[32,64,128]{2,1,0:T(8,128)S(1)}, f32[32,64,128]{2,1,0:T(8,128)S(1)}, u32[]{:S(2)}, u32[]{:S(2)}) collective-permute-start(f32[32,64,128]{2,1,0:T(8,128)S(1)} %get-tuple-element.50), channel_id=1, source_target_pairs={{0,4},{4,8},{8,12},{12,16},{16,20},{20,24},{24,28},{1,5},{5,9},{9,... | collective-permute-start | bytes 3145736 | tf_op jit(solution)/shard_map/ppermute | solution.py:597
  16.5 7.4 %collective-permute-start = (f32[55,8,128]{2,1,0:T(8,128)S(1)}, f32[55,8,128]{2,1,0:T(8,128)S(1)}, u32[]{:S(2)}, u32[]{:S(2)}) collective-permute-start(f32[55,8,128]{2,1,0:T(8,128)S(1)} %get-tuple-element.46), channel_id=1, source_target_pairs={{0,1},{2,3},{1,0},{3,2},{4,5},{6,7},{5,4},{7,6},{8,9},{10,11},{9,8... | collective-permute-start | bytes 675848 | tf_op jit(solution)/shard_map/ppermute | solution.py:598
  18.1 5.8 %collective-permute-start.1 = (f32[55,8,128]{2,1,0:T(8,128)S(1)}, f32[55,8,128]{2,1,0:T(8,128)S(1)}, u32[]{:S(2)}, u32[]{:S(2)}) collective-permute-start(f32[55,8,128]{2,1,0:T(8,128)S(1)} %get-tuple-element.47), channel_id=1, source_target_pairs={{1,2},{2,1},{5,6},{6,5},{9,10},{10,9},{13,14},{14,13},{17,18},{18,... | collective-permute-start | bytes 675848 | tf_op jit(solution)/shard_map/ppermute | solution.py:599
  29.8 2.3 %collective-permute-start.4 = (f32[40,8,128]{2,1,0:T(8,128)S(1)}, f32[40,8,128]{2,1,0:T(8,128)S(1)}, u32[]{:S(2)}, u32[]{:S(2)}) collective-permute-start(f32[40,8,128]{2,1,0:T(8,128)S(1)} %get-tuple-element.51), channel_id=1, source_target_pairs={{0,4},{4,8},{8,12},{12,16},{16,20},{20,24},{24,28},{1,5},{5,9},{9,... | collective-permute-start | bytes 491528 | tf_op jit(solution)/shard_map/ppermute | solution.py:610
  34.0 9.6 %collective-permute-start.5 = (f32[47,8,128]{2,1,0:T(8,128)S(1)}, f32[47,8,128]{2,1,0:T(8,128)S(1)}, u32[]{:S(2)}, u32[]{:S(2)}) collective-permute-start(f32[47,8,128]{2,1,0:T(8,128)S(1)} %get-tuple-element.59), channel_id=1, source_target_pairs={{0,4},{4,0},{8,12},{12,8},{16,20},{20,16},{24,28},{28,24},{1,5},{5... | collective-permute-start | bytes 577544 | tf_op jit(solution)/shard_map/ppermute | solution.py:624
  38.5 8.1 %collective-permute-start.6 = (f32[47,8,128]{2,1,0:T(8,128)S(1)}, f32[47,8,128]{2,1,0:T(8,128)S(1)}, u32[]{:S(2)}, u32[]{:S(2)}) collective-permute-start(f32[47,8,128]{2,1,0:T(8,128)S(1)} %get-tuple-element.60), channel_id=1, source_target_pairs={{0,8},{4,12},{8,0},{12,4},{16,24},{20,28},{24,16},{28,20},{1,9},{5... | collective-permute-start | bytes 577544 | tf_op jit(solution)/shard_map/ppermute | solution.py:624
  40.9 9.3 %collective-permute-start.7 = (f32[47,8,128]{2,1,0:T(8,128)S(1)}, f32[47,8,128]{2,1,0:T(8,128)S(1)}, u32[]{:S(2)}, u32[]{:S(2)}) collective-permute-start(f32[47,8,128]{2,1,0:T(8,128)S(1)} %get-tuple-element.61), channel_id=1, source_target_pairs={{0,12},{4,8},{8,4},{12,0},{16,28},{20,24},{24,20},{28,16},{1,13},{... | collective-permute-start | bytes 577544 | tf_op jit(solution)/shard_map/ppermute | solution.py:624
  40.9 9.3 %collective-permute-start.8 = (f32[47,8,128]{2,1,0:T(8,128)S(1)}, f32[47,8,128]{2,1,0:T(8,128)S(1)}, u32[]{:S(2)}, u32[]{:S(2)}) collective-permute-start(f32[47,8,128]{2,1,0:T(8,128)S(1)} %get-tuple-element.62), channel_id=1, source_target_pairs={{0,16},{4,20},{8,24},{12,28},{16,0},{20,4},{24,8},{28,12},{1,17},{... | collective-permute-start | bytes 577544 | tf_op jit(solution)/shard_map/ppermute | solution.py:624
  43.6 17.4 %collective-permute-start.9 = (f32[47,8,128]{2,1,0:T(8,128)S(1)}, f32[47,8,128]{2,1,0:T(8,128)S(1)}, u32[]{:S(2)}, u32[]{:S(2)}) collective-permute-start(f32[47,8,128]{2,1,0:T(8,128)S(1)} %get-tuple-element.63), channel_id=1, source_target_pairs={{0,20},{4,16},{8,28},{12,24},{16,4},{20,0},{24,12},{28,8},{1,21},{... | collective-permute-start | bytes 577544 | tf_op jit(solution)/shard_map/ppermute | solution.py:624
  43.6 17.4 %collective-permute-start.10 = (f32[47,8,128]{2,1,0:T(8,128)S(1)}, f32[47,8,128]{2,1,0:T(8,128)S(1)}, u32[]{:S(2)}, u32[]{:S(2)}) collective-permute-start(f32[47,8,128]{2,1,0:T(8,128)S(1)} %get-tuple-element.64), channel_id=1, source_target_pairs={{0,24},{4,28},{8,16},{12,20},{16,8},{20,12},{24,0},{28,4},{1,25},{... | collective-permute-start | bytes 577544 | tf_op jit(solution)/shard_map/ppermute | solution.py:624
  46.6 14.4 %collective-permute-start.11 = (f32[47,8,128]{2,1,0:T(8,128)S(1)}, f32[47,8,128]{2,1,0:T(8,128)S(1)}, u32[]{:S(2)}, u32[]{:S(2)}) collective-permute-start(f32[47,8,128]{2,1,0:T(8,128)S(1)} %get-tuple-element.65), channel_id=1, source_target_pairs={{0,28},{4,24},{8,20},{12,16},{16,12},{20,8},{24,4},{28,0},{1,29},{... | collective-permute-start | bytes 577544 | tf_op jit(solution)/shard_map/ppermute | solution.py:624
  66.4 6.0 %collective-permute-start.12 = (f32[66,8,128]{2,1,0:T(8,128)S(1)}, f32[66,8,128]{2,1,0:T(8,128)S(1)}, u32[]{:S(2)}, u32[]{:S(2)}) collective-permute-start(f32[66,8,128]{2,1,0:T(8,128)S(1)} %get-tuple-element.76), channel_id=1, source_target_pairs={{0,4},{4,0},{8,12},{12,8},{16,20},{20,16},{24,28},{28,24},{1,5},{5... | collective-permute-start | bytes 811016 | tf_op jit(solution)/shard_map/ppermute | solution.py:624
  66.6 47.5 %collective-permute-start.19 = (f32[160,8,128]{2,1,0:T(8,128)S(1)}, f32[160,8,128]{2,1,0:T(8,128)S(1)}, u32[]{:S(2)}, u32[]{:S(2)}) collective-permute-start(f32[160,8,128]{2,1,0:T(8,128)S(1)} %get-tuple-element.85), channel_id=1, source_target_pairs={{0,4},{4,8},{8,12},{12,16},{16,20},{20,24},{24,28},{1,5},{5,9},{9,... | collective-permute-start | bytes 1966088 | tf_op jit(solution)/shard_map/ppermute | solution.py:629
  68.9 9.3 %collective-permute-start.13 = (f32[66,8,128]{2,1,0:T(8,128)S(1)}, f32[66,8,128]{2,1,0:T(8,128)S(1)}, u32[]{:S(2)}, u32[]{:S(2)}) collective-permute-start(f32[66,8,128]{2,1,0:T(8,128)S(1)} %get-tuple-element.77), channel_id=1, source_target_pairs={{0,8},{4,12},{8,0},{12,4},{16,24},{20,28},{24,16},{28,20},{1,9},{5... | collective-permute-start | bytes 811016 | tf_op jit(solution)/shard_map/ppermute | solution.py:624
  69.5 21.7 %collective-permute-start.14 = (f32[66,8,128]{2,1,0:T(8,128)S(1)}, f32[66,8,128]{2,1,0:T(8,128)S(1)}, u32[]{:S(2)}, u32[]{:S(2)}) collective-permute-start(f32[66,8,128]{2,1,0:T(8,128)S(1)} %get-tuple-element.78), channel_id=1, source_target_pairs={{0,12},{4,8},{8,4},{12,0},{16,28},{20,24},{24,20},{28,16},{1,13},{... | collective-permute-start | bytes 811016 | tf_op jit(solution)/shard_map/ppermute | solution.py:624
  71.6 20.3 %collective-permute-start.15 = (f32[66,8,128]{2,1,0:T(8,128)S(1)}, f32[66,8,128]{2,1,0:T(8,128)S(1)}, u32[]{:S(2)}, u32[]{:S(2)}) collective-permute-start(f32[66,8,128]{2,1,0:T(8,128)S(1)} %get-tuple-element.79), channel_id=1, source_target_pairs={{0,16},{4,20},{8,24},{12,28},{16,0},{20,4},{24,8},{28,12},{1,17},{... | collective-permute-start | bytes 811016 | tf_op jit(solution)/shard_map/ppermute | solution.py:624
  72.4 41.7 %collective-permute-start.20 = (f32[96,8,128]{2,1,0:T(8,128)S(1)}, f32[96,8,128]{2,1,0:T(8,128)S(1)}, u32[]{:S(2)}, u32[]{:S(2)}) collective-permute-start(f32[96,8,128]{2,1,0:T(8,128)S(1)} %get-tuple-element.86), channel_id=1, source_target_pairs={{0,4},{4,8},{8,12},{12,16},{16,20},{20,24},{24,28},{1,5},{5,9},{9,... | collective-permute-start | bytes 1179656 | tf_op jit(solution)/shard_map/ppermute | solution.py:630
  78.2 30.3 %collective-permute-start.16 = (f32[66,8,128]{2,1,0:T(8,128)S(1)}, f32[66,8,128]{2,1,0:T(8,128)S(1)}, u32[]{:S(2)}, u32[]{:S(2)}) collective-permute-start(f32[66,8,128]{2,1,0:T(8,128)S(1)} %get-tuple-element.80), channel_id=1, source_target_pairs={{0,20},{4,16},{8,28},{12,24},{16,4},{20,0},{24,12},{28,8},{1,21},{... | collective-permute-start | bytes 811016 | tf_op jit(solution)/shard_map/ppermute | solution.py:624
  91.2 17.3 %collective-permute-start.17 = (f32[66,8,128]{2,1,0:T(8,128)S(1)}, f32[66,8,128]{2,1,0:T(8,128)S(1)}, u32[]{:S(2)}, u32[]{:S(2)}) collective-permute-start(f32[66,8,128]{2,1,0:T(8,128)S(1)} %get-tuple-element.81), channel_id=1, source_target_pairs={{0,24},{4,28},{8,16},{12,20},{16,8},{20,12},{24,0},{28,4},{1,25},{... | collective-permute-start | bytes 811016 | tf_op jit(solution)/shard_map/ppermute | solution.py:624
  91.8 16.6 %collective-permute-start.18 = (f32[66,8,128]{2,1,0:T(8,128)S(1)}, f32[66,8,128]{2,1,0:T(8,128)S(1)}, u32[]{:S(2)}, u32[]{:S(2)}) collective-permute-start(f32[66,8,128]{2,1,0:T(8,128)S(1)} %get-tuple-element.82), channel_id=1, source_target_pairs={{0,28},{4,24},{8,20},{12,16},{16,12},{20,8},{24,4},{28,0},{1,29},{... | collective-permute-start | bytes 811016 | tf_op jit(solution)/shard_map/ppermute | solution.py:624

commit v4 on v3

--- a/solution.py
+++ b/solution.py
@@ -12,7 +12,8 @@
 KEEP = 1.0 - DAMPING
 GROUP = 2 ** (LEVELS - 1)
 TEAM = GROUP // 2
-SWAPS = (2, 6, 4, 3, 7, 5, 1)
+DOWN = (2, 6, 4, 3, 7, 5, 1)
+UP = (2, 6, 4, 3, 7, 5, 1)
 HALO = 2 * LEVELS + 1
 SIDE = HALO - 1
 EDGE = 2
@@ -248,9 +249,9 @@
     return piece, piece + 2 * REACH, start
 
 
-def join_first(start_of, window, g_prev, got, edges, s_ext, w_ext, part0, left0, left1, v1, *refs):
+def join_first(start_of, window, g_prev, got, edges, s_ext, w_ext, left0, left1, *refs):
     outs = refs[:TEAM]
-    base0, base1, back1, back2, norm, y, coarse = refs[TEAM:]
+    y, resid0, coarse = refs[TEAM:]
     place = place_of()
     rows = got.shape[0]
     m = masks()
@@ -270,52 +271,42 @@
         s = s_ext[i]
         here = y[i]
         a = left0[i] - (1.0 + 4.0 * s) * here + s * around(y, i, m) + swept
-        return a, left1[i] + here
-
-    def edge(i, swept):
-        a, b = resid(i, swept)
-        coarse[i] = a + b
-        return a, b
-
-    def based(i, a, b):
+        resid0[i] = a
+        coarse[i] = a + left1[i] + here
+
+    loop(HALO + 1, HALO + rows - 1, lambda i: resid(i, got[i - HALO]), unroll=32)
+    for k in range(SIDE):
+        resid(2 + k, edges[k])
+        resid(HALO + rows - 1 + k, edges[SIDE + k])
+    for k, out in enumerate(outs):
+        low = start_of(place ^ k) - REACH + HALO
+
+        def copy(i, out=out, low=low):
+            out[i] = coarse[low + i]
+
+        loop(0, window, copy, unroll=16)
+
+
+def join_rest(w_ext, part0, left1, v1, y, resid0, base0, base1, back, norm):
+    rows = back.shape[0]
+
+    def based(i):
         w = w_ext[i]
+        a = resid0[i]
+        b = left1[i] + y[i]
         base0[i - HALO + 1] = part0[i] + y[i] + w * a
         value = v1[i] + w * b
         base1[i - HALO + 1] = value
-        return value
-
-    acc = jnp.zeros((8, 128), jnp.float32)
-    first = HALO
-    for back in (back1, back2):
-
-        def main(i, acc, back=back, first=first):
-            a, b = edge(i, got[i - HALO])
-            back[i - first] = based(i, a, b)
-            return acc + (a * a + b * b)
-
-        low = max(first, HALO + 1)
-        high = min(first + back.shape[0], HALO + rows - 1)
-        acc = loop(low, high, main, acc, unroll=32)
-        first += back.shape[0]
-    for k in range(SIDE):
-        for i, at in ((2 + k, k), (HALO + rows - 1 + k, SIDE + k)):
-            a, b = edge(i, edges[at])
-            if HALO - 1 <= i <= HALO + rows:
-                value = based(i, a, b)
-            if i == HALO:
-                back1[0] = value
-                acc = acc + (a * a + b * b)
-            if i == HALO + rows - 1:
-                back2[back2.shape[0] - 1] = value
-                acc = acc + (a * a + b * b)
-    norm[...] = acc
-    for k, out in enumerate(outs):
-        low = start_of(place ^ k) - REACH + HALO
-
-        def copy(i, out=out, low=low):
-            out[i] = coarse[low + i]
-
-        loop(0, window, copy, unroll=16)
+        return a, b, value
+
+    def main(i, acc):
+        a, b, value = based(i)
+        back[i - HALO] = value
+        return acc + (a * a + b * b)
+
+    norm[...] = loop(HALO, HALO + rows, main, jnp.zeros((8, 128), jnp.float32), unroll=8)
+    based(HALO - 1)
+    based(HALO + rows)
 
 
 def coarse_levels(start_of, rows, s_ext, *refs):
@@ -446,69 +437,122 @@
     loop(0, piece, blank, unroll=11)
     for k, out in enumerate(outs):
 
-        def copy(i, k=k, out=out):
-            out[i] = final[(place ^ k) + 1, i]
-            out[piece + i] = final[place ^ k, i]
+        target = place ^ k
+        odd = lax.rem(target, 2)
+        half = out.shape[0] - piece
+
+        def copy(i, out=out, at=target + odd):
+            out[i] = final[at, i]
+
+        def copy_half(i, out=out, at=target - odd + 1, skip=odd * (piece - half), half=half):
+            out[piece + i] = final[at, skip + i]
 
         loop(0, piece, copy, unroll=11)
-
-
-def finish(start_of, piece, rhs, s_ext, w_ext, base0, base1, *refs):
-    fields = refs[:TEAM]
-    out, left, norm, e, before, sol0, sol1 = refs[TEAM:]
-    rows = rhs.shape[1] * 8
+        loop(0, half, copy_half, unroll=17)
+
+
+def odd_place():
+    return lax.rem(lax.axis_index("tm"), 2)
+
+
+def pick_halves(piece, *refs):
+    fields, (out,) = refs[:TEAM], refs[TEAM:]
+    half = fields[0].shape[0] - piece
+    place = place_of()
+    for k, got in enumerate(fields):
+        first = (place ^ k) * half
+
+        def copy(i, got=got, first=first):
+            out[first + i] = got[piece + i]
+
+        loop(0, half, copy, unroll=17)
+
+
+def spread(field, s_ext, w_ext, out):
     m = masks()
+
+    def body(i):
+        s = s_ext[i + HALO - 1]
+        out[i] = KEEP * field[i + 1] + w_ext[i + HALO - 1] * (s * around(field, i + 1, m))
+
+    loop(0, out.shape[0], body, unroll=43)
+
+
+def spread_own(start_of, piece, s_ext, w_ext, *refs):
+    fields, (own, out) = refs[:TEAM], refs[TEAM:]
     place = place_of()
     for k, got in enumerate(fields):
         start = start_of(place ^ k) + EDGE
 
         def copy(i, got=got, start=start):
-            e[start + i] = got[i]
-            before[start + i] = got[piece + i]
+            own[start + i] = got[i]
 
         loop(0, piece, copy, unroll=11)
-
-    def correct(i):
-        s = s_ext[i + HALO - 1]
-        w = w_ext[i + HALO - 1]
-        here = e[i + 1]
-        part = KEEP * here + w * (s * around(e, i + 1, m))
-        sol0[i] = base0[i] + part + w * before[i + 1]
-        sol1[i] = base1[i] + part + w * here
-
-    loop(0, rows + 2, correct, unroll=43)
-
-    def last(g, acc):
-        for k in range(8):
-            i = g * 8 + k
-            s = s_ext[i + HALO]
-            w = w_ext[i + HALO]
-            diag = 1.0 + 4.0 * s
-            past = before[i + EDGE]
-            past = KEEP * past + w * (s * around(before, i + EDGE, m) + past)
-            a = sol0[i + 1]
-            b = sol1[i + 1]
-            left[i] = strided(rhs, (0,), g, k) - diag * a + s * around(sol0, i + 1, m) + past
-            rb = strided(rhs, (1,), g, k) - diag * b + s * around(sol1, i + 1, m) + a
-            out[0, g, pl.ds(k, 8, stride=8)] = a
-            out[1, g, pl.ds(k, 8, stride=8)] = b
-            acc = acc + rb * rb
-        return acc
-
-    norm[...] = loop(0, rows // 8, last, jnp.zeros((8, 128), jnp.float32), unroll=2)
-
-
-def add_up(left, back1, back2, norm0, norms, norm, sums):
-    acc = norm[...]
-    first = 0
-    for back in (back1, back2):
-
-        def body(i, acc, back=back, first=first):
-            r = left[first + i] + back[i]
-            return acc + r * r
-
-        acc = loop(0, back.shape[0], body, acc, unroll=16)
-        first += back.shape[0]
+    spread(own, s_ext, w_ext, out)
+
+
+def finish(start_of, piece, rhs, s_ext, w_ext, base0, base1, own, own_spread, halves, *refs):
+    fields = refs[:TEAM]
+    out, left, norm, shared, shared_spread, sol0, sol1 = refs[TEAM:]
+    rows = rhs.shape[1] * 8
+    half = fields[0].shape[0] - piece
+    m = masks()
+    place = place_of()
+    odd = odd_place()
+    skip = odd * (piece - half)
+    for k, got in enumerate(fields):
+        start = start_of(place ^ k) + EDGE + skip
+
+        def copy(i, got=got, start=start):
+            shared[start + i] = got[piece + i]
+
+        loop(0, half, copy, unroll=17)
+    for j in range(TEAM):
+        start = start_of(j) + EDGE + (piece - half) - skip
+
+        def copy(i, j=j, start=start):
+            shared[start + i] = halves[j * half + i]
+
+        loop(0, half, copy, unroll=17)
+    spread(shared, s_ext, w_ext, shared_spread)
+
+    def solve(now, before):
+        e, part = now
+        past, past_part = before
+
+        def correct(i):
+            w = w_ext[i + HALO - 1]
+            sol0[i] = base0[i] + part[i] + w * past[i + 1]
+            sol1[i] = base1[i] + part[i] + w * e[i + 1]
+
+        loop(0, rows + 2, correct, unroll=16)
+
+        def last(g, acc):
+            for k in range(8):
+                i = g * 8 + k
+                s = s_ext[i + HALO]
+                diag = 1.0 + 4.0 * s
+                older = past_part[i + 1] + w_ext[i + HALO] * past[i + EDGE]
+                a = sol0[i + 1]
+                b = sol1[i + 1]
+                left[i] = strided(rhs, (0,), g, k) - diag * a + s * around(sol0, i + 1, m) + older
+                rb = strided(rhs, (1,), g, k) - diag * b + s * around(sol1, i + 1, m) + a
+                out[0, g, pl.ds(k, 8, stride=8)] = a
+                out[1, g, pl.ds(k, 8, stride=8)] = b
+                acc = acc + rb * rb
+            return acc
+
+        norm[...] = loop(0, rows // 8, last, jnp.zeros((8, 128), jnp.float32), unroll=2)
+
+    either(odd == 1, solve, (shared, shared_spread), (own, own_spread))
+
+
+def add_up(left, back, norm0, norms, norm, sums):
+    def body(i, acc):
+        r = left[i] + back[i]
+        return acc + r * r
+
+    acc = loop(0, back.shape[0], body, norm[...], unroll=16)
     parts = [norm0[...]] + [norms[k] for k in range(LEVELS - 1)] + [acc]
     for k, part in enumerate(parts):
         sums[pl.ds(k, 1)] = jnp.sum(part, axis=0, keepdims=True)
@@ -555,8 +599,11 @@
         field = fields[level - 1] + jnp.repeat(field, 2, axis=0)
         field = field + w * resid(field, sources[level - 1], s, earlier(field[-1:]))
     past = jnp.concatenate([earlier(field[-1:]), field[:-1]], axis=0)
-    both = [x[:, REACH : x.shape[1] - REACH] for x in (field, past)]
-    both = jnp.concatenate(both, axis=1)
+    field, past = [x[:, REACH : x.shape[1] - REACH] for x in (field, past)]
+    half = -(-field.shape[1] // 2)
+    even = jnp.concatenate([past, field[:, :half]], axis=1)
+    odd = jnp.concatenate([field, past[:, -half:]], axis=1)
+    both = jnp.where((jnp.arange(TEAM) % 2 == 1)[:, None, None], odd, even)
     return both.reshape(*both.shape[:2], 8, 128), jnp.stack(norms)
 
 
@@ -567,6 +614,7 @@
     total_cells = rows * strips * cells
     groups = rows // 8
     piece, window, start_of = windows_of(rows)
+    half_piece = -(-piece // 2)
     wide = cells // 16
     ext = rows + 2 * HALO
 
@@ -608,26 +656,26 @@
         n_in=5,
     )(guess_t, rhs_t, diff_t, facing, backing)
     edges = lax.ppermute(edges, "tm", later)
-    one = rows * 5 // 80 * 10
-    *mine, base0, base1, back1, back2, norm0 = kernel_call(
+    *mine, y, resid0 = kernel_call(
         functools.partial(join_first, start_of, window),
-        [shape(window, 8, 128)] * TEAM
-        + [kept(rows + 2, 8, 128)] * 2
-        + [shape(one, 8, 128), shape(rows - one, 8, 128), shape(8, 128)],
-        scratch=[(ext, 8, 128)] * 2,
-        n_in=9,
-    )(g_prev, got, edges, s_ext, w_ext, part0, left0, left1, v1)
-
-    def exchange(parts):
+        [shape(window, 8, 128)] * TEAM + [shape(ext, 8, 128)] * 2,
+        scratch=[(ext, 8, 128)],
+        n_in=7,
+    )(g_prev, got, edges, s_ext, w_ext, left0, left1)
+
+    def exchange(order, parts):
         moved = list(parts)
-        for k in SWAPS:
+        for k in order:
             moved[k] = lax.ppermute(parts[k], "tm", [(i, i ^ k) for i in range(count)])
         return moved
 
-    mine = exchange(mine)
-    *mine, back1 = lax.optimization_barrier((*mine, back1))
-    back1 = lax.ppermute(back1, "tm", later)
-    back2 = lax.ppermute(back2, "tm", later)
+    mine = exchange(DOWN, mine)
+    base0, base1, back, norm0 = kernel_call(
+        join_rest,
+        [kept(rows + 2, 8, 128)] * 2 + [shape(rows, 8, 128), shape(8, 128)],
+        n_in=6,
+    )(w_ext, part0, left1, v1, y, resid0)
+    back = lax.ppermute(back, "tm", later)
     if count == TEAM:
         tall = padded(window)
         half = [(TEAM >> level, tall, 8, 128) for level in range(LEVELS)]
@@ -636,7 +684,7 @@
             bases += [half[level - 1], half[level]]
         *fields, norms = kernel_call(
             functools.partial(coarse_levels, start_of, rows),
-            [shape(2 * piece, 8, 128)] * TEAM + [shape(LEVELS - 1, 8, 128)],
+            [shape(piece + half_piece, 8, 128)] * TEAM + [shape(LEVELS - 1, 8, 128)],
             scratch=[(tall, 8, 128), (LEVELS - 1, tall, 8, 128), half[0], half[0], (TEAM + 1, piece, 8, 128)] + bases,
             n_in=1 + TEAM,
         )(s_ext, *mine)
@@ -650,16 +698,25 @@
         jumps = [(i, i + TEAM) for i in range(count - TEAM)]
         fields, norms = coarse_plain(jnp.stack(mine)[order], s_win, own, lambda v: lax.ppermute(v, "tm", jumps))
         fields = list(fields[order])
-    fields = exchange(fields)
+    fields = exchange(UP, fields)
 
     s_ext, w_ext, base0, base1 = keep(s_ext, w_ext, base0, base1)
+    (halves,) = kernel_call(
+        functools.partial(pick_halves, piece), [shape(TEAM * half_piece, 8, 128)], n_in=TEAM
+    )(*fields)
+    halves = lax.ppermute(halves, "tm", [(i, i ^ 1) for i in range(count)])
+    own, own_spread = kernel_call(
+        functools.partial(spread_own, start_of, piece),
+        [shape(rows + 2 * EDGE, 8, 128), shape(rows + 2, 8, 128)],
+        n_in=2 + TEAM,
+    )(s_ext, w_ext, *fields)
     out, left, norm = kernel_call(
         functools.partial(finish, start_of, piece),
         [shape(2, groups, wide, 128), shape(rows, 8, 128), shape(8, 128)],
-        scratch=[(rows + 2 * EDGE, 8, 128)] * 2 + [(rows + 2, 8, 128)] * 2,
-        n_in=5 + TEAM,
-    )(rhs_t, s_ext, w_ext, base0, base1, *fields)
-    (sums,) = kernel_call(add_up, [shape(8, 128)], n_in=6)(left, back1, back2, norm0, norms, norm)
+        scratch=[(rows + 2 * EDGE, 8, 128)] + [(rows + 2, 8, 128)] * 3,
+        n_in=8 + TEAM,
+    )(rhs_t, s_ext, w_ext, base0, base1, own, own_spread, halves, *fields)
+    (sums,) = kernel_call(add_up, [shape(8, 128)], n_in=5)(left, back, norm0, norms, norm)
 
     every = jnp.broadcast_to(sums[None], (count * strips, 8, 128))
     every = lax.all_to_all(every, ("tm", "space"), 0, 0)

time: 131 us -> 123 us (0.939)
  starting transfers between devices: 40.6 us -> 34.5 us
  waiting for transfers between devices: 45.2 us -> 43 us
  Pallas kernels: 23.4 us -> 24.9 us
    ppermute x14, starting transfers between devices: 25.9 us -> 21.1 us  [exchange(): moved[k] = lax.ppermute(parts[k], 'tm', [(i, i ^ k) for i in range(count)])]
    ppermute x14, waiting for transfers between devices: 39.1 us -> 36.2 us  [exchange(): moved[k] = lax.ppermute(parts[k], 'tm', [(i, i ^ k) for i in range(count)])]
    pallas_call x7 -> x10, Pallas kernels: 23.4 us -> 24.9 us  [call(): pl.pallas_call(body, out_shape=outs, grid=grid, in_specs=specs or [vmem()...]
    ppermute x2, starting transfers between devices: 4.08 us -> 2.71 us  [the longest x1 2.53 us: body(): back = lax.ppermute(back, 'tm', later)]
  transfers between devices with their start and end apart: 21 -> 21, of which waited for: 8 -> 9; matrix products, arithmetic and copies ran while one was open for 0% -> 0% of each run, Pallas kernels for 11% -> 17%
where the time goes in v4:
time: 123 us
  waiting for transfers between devices  43 us (35%)
  starting transfers between devices  34.5 us (28%)
  Pallas kernels  24.9 us (20%)
  blocking collectives  14.5 us (12%)
  local copies, waits for them, and re-layouts  4.43 us (4%)
    ppermute x14, waiting for transfers between devices, exchange(): moved[k] = lax.ppermute(parts[k], 'tm', [(i, i ^ k) for i in range(count)])  36.2 us
    pallas_call x10, Pallas kernels, call(): pl.pallas_call(body, out_shape=outs, grid=grid, in_specs=specs or [vmem()...  24.9 us
    ppermute x14, starting transfers between devices, exchange(): moved[k] = lax.ppermute(parts[k], 'tm', [(i, i ^ k) for i in range(count)])  21.1 us
    all_to_all x1, blocking collectives, body(): every = lax.all_to_all(every, ('tm', 'space'), 0, 0)  14.5 us
    ppermute x1, waiting for transfers between devices, body(): facing = lax.ppermute(facing, 'space', both(0))  5.12 us
    ppermute x1, starting transfers between devices, body(): g_prev = lax.ppermute(g_prev, 'tm', later)  4.5 us
    unnamed x12, local copies, waits for them, and re-layouts  4.42 us
    ppermute x1, starting transfers between devices, body(): got = lax.ppermute(send, 'tm', later)  2.59 us
  transfers between devices with their start and end apart: 21, of which 9 were waited for; matrix products, arithmetic and copies ran while one was open for 0% of the time, Pallas kernels for 17%

profile of v4, /device:TPU:0, one launch (start us, length us, event | category | flops | bytes accessed | tf_op | source)
XLA Modules:
  0.0 122.8 jit_solution(4780460957056761314)
XLA Ops:
  0.6 1.6 %copy-done = f32[2,256,1024]{2,1,0:T(8,128)S(1)} copy-done((f32[2,256,1024]{2,1,0:T(8,128)S(1)}, f32[2,256,1024]{2,1,0:T(8,128)}, u32[]{:S(2)}) %copy-start) | copy-done | bytes 2097176
  2.2 1.6 %copy-done.2 = f32[2,256,1024]{2,1,0:T(8,128)S(1)} copy-done((f32[2,256,1024]{2,1,0:T(8,128)S(1)}, f32[2,256,1024]{2,1,0:T(8,128)}, u32[]{:S(2)}) %copy-start.2) | copy-done | bytes 2097176
  3.8 1.2 copy-done.4
  5.0 1.5 %shard_map.52 = f32[256,8,128]{2,1,0:T(8,128)S(1)} custom-call(f32[2,32,64,128]{3,2,1,0:T(8,128)S(1)} %bitcast.23, f32[2,32,64,128]{3,2,1,0:T(8,128)S(1)} %bitcast.27, f32[32,64,128]{2,1,0:T(8,128)S(1)} %bitcast.32), custom_call_target="tpu_custom_call" | custom-call | tf_op jit(solution)/shard_map/pallas_call | solution.py:43
  6.6 2.6 %collective-permute-start.3 = (f32[256,8,128]{2,1,0:T(8,128)S(1)}, f32[256,8,128]{2,1,0:T(8,128)S(1)}, u32[]{:S(2)}, u32[]{:S(2)}) collective-permute-start(f32[256,8,128]{2,1,0:T(8,128)S(1)} %shard_map.52), channel_id=1, source_target_pairs={{0,4},{4,8},{8,12},{12,16},{16,20},{20,24},{24,28},{1,5},{5,9},{9,... | collective-permute-start | bytes 3145736 | tf_op jit(solution)/shard_map/ppermute | solution.py:651
  9.2 2.8 %shard_map.50 = (f32[55,8,128]{2,1,0:T(8,128)S(1)}, f32[55,8,128]{2,1,0:T(8,128)S(1)}, f32[32,64,128]{2,1,0:T(8,128)S(1)}) custom-call(f32[2,32,64,128]{3,2,1,0:T(8,128)} %bitcast.20, f32[2,32,64,128]{3,2,1,0:T(8,128)} %bitcast.21, f32[2,32,64,128]{3,2,1,0:T(8,128)} %bitcast.25, f32[32,64,128]{2,1,0:T(8,128)} %bitcast.30, f32[2,32,64,128]{3,2,1,0:T(8,128)} %bitcast.22, ...), custom_call_target="tpu_custom_call" | custom-call | tf_op jit(solution)/shard_map/pallas_call | solution.py:43
  12.0 4.5 %collective-permute-start.2 = (f32[32,64,128]{2,1,0:T(8,128)S(1)}, f32[32,64,128]{2,1,0:T(8,128)S(1)}, u32[]{:S(2)}, u32[]{:S(2)}) collective-permute-start(f32[32,64,128]{2,1,0:T(8,128)S(1)} %get-tuple-element.47), channel_id=1, source_target_pairs={{0,4},{4,8},{8,12},{12,16},{16,20},{20,24},{24,28},{1,5},{5,9},{9,... | collective-permute-start | bytes 3145736 | tf_op jit(solution)/shard_map/ppermute | solution.py:645
  16.5 1.6 %collective-permute-start = (f32[55,8,128]{2,1,0:T(8,128)S(1)}, f32[55,8,128]{2,1,0:T(8,128)S(1)}, u32[]{:S(2)}, u32[]{:S(2)}) collective-permute-start(f32[55,8,128]{2,1,0:T(8,128)S(1)} %get-tuple-element.40), channel_id=1, source_target_pairs={{0,1},{2,3},{1,0},{3,2},{4,5},{6,7},{5,4},{7,6},{8,9},{10,11},{9,8... | collective-permute-start | bytes 675848 | tf_op jit(solution)/shard_map/ppermute | solution.py:646
  18.8 5.1 %collective-permute-done.pair = f32[55,8,128]{2,1,0:T(8,128)S(1)} collective-permute-done((f32[55,8,128]{2,1,0:T(8,128)S(1)}, f32[55,8,128]{2,1,0:T(8,128)S(1)}, u32[]{:S(2)}, u32[]{:S(2)}) %collective-permute-start) | collective-permute-done | bytes 225312 | tf_op jit(solution)/shard_map/ppermute | solution.py:646
  24.0 5.8 %shard_map.51 = (f32[278,8,128]{2,1,0:T(8,128)S(1)}, f32[278,8,128]{2,1,0:T(8,128)S(1)}, f32[278,8,128]{2,1,0:T(8,128)S(1)}, f32[278,8,128]{2,1,0:T(8,128)S(1)},...) custom-call(f32[2,32,64,128]{3,2,1,0:T(8,128)S(1)} %bitcast.24, ...), custom_call_target="tpu_custom_call" | custom-call | tf_op jit(solution)/shard_map/pallas_call | solution.py:43
  29.8 1.3 %collective-permute-start.4 = (f32[40,8,128]{2,1,0:T(8,128)S(1)}, f32[40,8,128]{2,1,0:T(8,128)S(1)}, u32[]{:S(2)}, u32[]{:S(2)}) collective-permute-start(f32[40,8,128]{2,1,0:T(8,128)S(1)} %get-tuple-element.48), channel_id=1, source_target_pairs={{0,4},{4,8},{8,12},{12,16},{16,20},{20,24},{24,28},{1,5},{5,9},{9,... | collective-permute-start | bytes 491528 | tf_op jit(solution)/shard_map/ppermute | solution.py:658
  32.1 1.8 %shard_map.53 = (f32[47,8,128]{2,1,0:T(8,128)S(1)}, f32[47,8,128]{2,1,0:T(8,128)S(1)}, f32[47,8,128]{2,1,0:T(8,128)S(1)}, f32[47,8,128]{2,1,0:T(8,128)S(1)}, f32...) custom-call(f32[32,64,128]{2,1,0:T(8,128)S(1)} %collective-permute-d, ...), custom_call_target="tpu_custom_call" | custom-call | tf_op jit(solution)/shard_map/pallas_call | solution.py:43
  33.9 4.4 %collective-permute-start.5 = (f32[47,8,128]{2,1,0:T(8,128)S(1)}, f32[47,8,128]{2,1,0:T(8,128)S(1)}, u32[]{:S(2)}, u32[]{:S(2)}) collective-permute-start(f32[47,8,128]{2,1,0:T(8,128)S(1)} %get-tuple-element.55), channel_id=1, source_target_pairs={{0,4},{4,0},{8,12},{12,8},{16,20},{20,16},{24,28},{28,24},{1,5},{5... | collective-permute-start | bytes 577544 | tf_op jit(solution)/shard_map/ppermute | solution.py:669
  38.3 2.4 %collective-permute-start.6 = (f32[47,8,128]{2,1,0:T(8,128)S(1)}, f32[47,8,128]{2,1,0:T(8,128)S(1)}, u32[]{:S(2)}, u32[]{:S(2)}) collective-permute-start(f32[47,8,128]{2,1,0:T(8,128)S(1)} %get-tuple-element.56), channel_id=1, source_target_pairs={{0,8},{4,12},{8,0},{12,4},{16,24},{20,28},{24,16},{28,20},{1,9},{5... | collective-permute-start | bytes 577544 | tf_op jit(solution)/shard_map/ppermute | solution.py:669
  40.7 2.7 %collective-permute-start.8 = (f32[47,8,128]{2,1,0:T(8,128)S(1)}, f32[47,8,128]{2,1,0:T(8,128)S(1)}, u32[]{:S(2)}, u32[]{:S(2)}) collective-permute-start(f32[47,8,128]{2,1,0:T(8,128)S(1)} %get-tuple-element.58), channel_id=1, source_target_pairs={{0,16},{4,20},{8,24},{12,28},{16,0},{20,4},{24,8},{28,12},{1,17},{... | collective-permute-start | bytes 577544 | tf_op jit(solution)/shard_map/ppermute | solution.py:669
  43.4 1.7 %collective-permute-start.10 = (f32[47,8,128]{2,1,0:T(8,128)S(1)}, f32[47,8,128]{2,1,0:T(8,128)S(1)}, u32[]{:S(2)}, u32[]{:S(2)}) collective-permute-start(f32[47,8,128]{2,1,0:T(8,128)S(1)} %get-tuple-element.60), channel_id=1, source_target_pairs={{0,24},{4,28},{8,16},{12,20},{16,8},{20,12},{24,0},{28,4},{1,25},{... | collective-permute-start | bytes 577544 | tf_op jit(solution)/shard_map/ppermute | solution.py:669
  45.2 1.2 collective-permute-done.6.refs_2_
  46.4 1.6 %collective-permute-start.11 = (f32[47,8,128]{2,1,0:T(8,128)S(1)}, f32[47,8,128]{2,1,0:T(8,128)S(1)}, u32[]{:S(2)}, u32[]{:S(2)}) collective-permute-start(f32[47,8,128]{2,1,0:T(8,128)S(1)} %get-tuple-element.61), channel_id=1, source_target_pairs={{0,28},{4,24},{8,20},{12,16},{16,12},{20,8},{24,4},{28,0},{1,29},{... | collective-permute-start | bytes 577544 | tf_op jit(solution)/shard_map/ppermute | solution.py:669
  48.6 1.4 %collective-permute-done.7.refs_3_ = f32[47,8,128]{2,1,0:T(8,128)S(1)} collective-permute-done((f32[47,8,128]{2,1,0:T(8,128)S(1)}, f32[47,8,128]{2,1,0:T(8,128)S(1)}, u32[]{:S(2)}, u32[]{:S(2)}) %collective-permute-start.7) | collective-permute-done | bytes 192544 | tf_op jit(solution)/shard_map/ppermute | solution.py:669
  50.0 2.5 %collective-permute-start.20 = (f32[256,8,128]{2,1,0:T(8,128)S(1)}, f32[256,8,128]{2,1,0:T(8,128)S(1)}, u32[]{:S(2)}, u32[]{:S(2)}) collective-permute-start(f32[256,8,128]{2,1,0:T(8,128)S(1)} %get-tuple-element.74), channel_id=1, source_target_pairs={{0,4},{4,8},{8,12},{12,16},{16,20},{20,24},{24,28},{1,5},{5,9},{9,... | collective-permute-start | bytes 3145736 | tf_op jit(solution)/shard_map/ppermute | solution.py:678
  52.6 19.0 %collective-permute-done.9.refs_5_ = f32[47,8,128]{2,1,0:T(8,128)S(1)} collective-permute-done((f32[47,8,128]{2,1,0:T(8,128)S(1)}, f32[47,8,128]{2,1,0:T(8,128)S(1)}, u32[]{:S(2)}, u32[]{:S(2)}) %collective-permute-start.9) | collective-permute-done | bytes 192544 | tf_op jit(solution)/shard_map/ppermute | solution.py:669
  71.6 5.3 %shard_map.55 = (f32[50,8,128]{2,1,0:T(8,128)S(1)}, f32[50,8,128]{2,1,0:T(8,128)S(1)}, f32[50,8,128]{2,1,0:T(8,128)S(1)}, f32[50,8,128]{2,1,0:T(8,128)S(1)}, f32...) custom-call(f32[278,8,128]{2,1,0:T(8,128)S(1)} %get-tuple-element.42, ...), custom_call_target="tpu_custom_call" | custom-call | tf_op jit(solution)/shard_map/pallas_call | solution.py:43
  77.1 1.8 %collective-permute-start.14 = (f32[50,8,128]{2,1,0:T(8,128)S(1)}, f32[50,8,128]{2,1,0:T(8,128)S(1)}, u32[]{:S(2)}, u32[]{:S(2)}) collective-permute-start(f32[50,8,128]{2,1,0:T(8,128)S(1)} %get-tuple-element.65), channel_id=1, source_target_pairs={{0,12},{4,8},{8,4},{12,0},{16,28},{20,24},{24,20},{28,16},{1,13},{... | collective-permute-start | bytes 614408 | tf_op jit(solution)/shard_map/ppermute | solution.py:669
  78.9 1.9 %collective-permute-start.15 = (f32[50,8,128]{2,1,0:T(8,128)S(1)}, f32[50,8,128]{2,1,0:T(8,128)S(1)}, u32[]{:S(2)}, u32[]{:S(2)}) collective-permute-start(f32[50,8,128]{2,1,0:T(8,128)S(1)} %get-tuple-element.66), channel_id=1, source_target_pairs={{0,16},{4,20},{8,24},{12,28},{16,0},{20,4},{24,8},{28,12},{1,17},{... | collective-permute-start | bytes 614408 | tf_op jit(solution)/shard_map/ppermute | solution.py:669
  81.1 4.0 %collective-permute-done.13.refs_2_ = f32[50,8,128]{2,1,0:T(8,128)S(1)} collective-permute-done((f32[50,8,128]{2,1,0:T(8,128)S(1)}, f32[50,8,128]{2,1,0:T(8,128)S(1)}, u32[]{:S(2)}, u32[]{:S(2)}) %collective-permute-start.13) | collective-permute-done | bytes 204832 | tf_op jit(solution)/shard_map/ppermute | solution.py:669
  85.1 1.7 %collective-permute-start.17 = (f32[50,8,128]{2,1,0:T(8,128)S(1)}, f32[50,8,128]{2,1,0:T(8,128)S(1)}, u32[]{:S(2)}, u32[]{:S(2)}) collective-permute-start(f32[50,8,128]{2,1,0:T(8,128)S(1)} %get-tuple-element.68), channel_id=1, source_target_pairs={{0,24},{4,28},{8,16},{12,20},{16,8},{20,12},{24,0},{28,4},{1,25},{... | collective-permute-start | bytes 614408 | tf_op jit(solution)/shard_map/ppermute | solution.py:669
  86.7 1.6 %collective-permute-done.14.refs_3_ = f32[50,8,128]{2,1,0:T(8,128)S(1)} collective-permute-done((f32[50,8,128]{2,1,0:T(8,128)S(1)}, f32[50,8,128]{2,1,0:T(8,128)S(1)}, u32[]{:S(2)}, u32[]{:S(2)}) %collective-permute-start.14) | collective-permute-done | bytes 204832 | tf_op jit(solution)/shard_map/ppermute | solution.py:669
  88.4 2.5 %collective-permute-start.18 = (f32[50,8,128]{2,1,0:T(8,128)S(1)}, f32[50,8,128]{2,1,0:T(8,128)S(1)}, u32[]{:S(2)}, u32[]{:S(2)}) collective-permute-start(f32[50,8,128]{2,1,0:T(8,128)S(1)} %get-tuple-element.69), channel_id=1, source_target_pairs={{0,28},{4,24},{8,20},{12,16},{16,12},{20,8},{24,4},{28,0},{1,29},{... | collective-permute-start | bytes 614408 | tf_op jit(solution)/shard_map/ppermute | solution.py:669
  90.8 8.9 %collective-permute-done.16.refs_5_ = f32[50,8,128]{2,1,0:T(8,128)S(1)} collective-permute-done((f32[50,8,128]{2,1,0:T(8,128)S(1)}, f32[50,8,128]{2,1,0:T(8,128)S(1)}, u32[]{:S(2)}, u32[]{:S(2)}) %collective-permute-start.16) | collective-permute-done | bytes 204832 | tf_op jit(solution)/shard_map/ppermute | solution.py:669
  100.0 1.2 shard_map.56
  101.8 5.5 %shard_map.58 = (f32[2,32,64,128]{3,2,1,0:T(8,128)}, f32[256,8,128]{2,1,0:T(8,128)S(1)}, f32[8,128]{1,0:T(8,128)S(1)}) custom-call(f32[2,32,64,128]{3,2,1,0:T(8,128)S(1)} %bitcast.29, f32[278,8,128]{2,1,0:T(8,128)S(1)} %get-tuple-element.42.s_ext, f32[278,8,128]{2,1,0:T(8,128)S(1)} %get-tuple-element.43.w_ext, f32[258,8,128]{2,1,0:T(8,128)S(1)} %get-tuple-element.52.base0, ...), custom_call_target="tpu_custom_call" | custom-call | tf_op jit(solution)/shard_map/pallas_call | solution.py:43
  107.7 14.5 %all_to_all.5 = f32[32,8,128]{2,1,0:T(8,128)S(1)} all-to-all(f32[32,8,128]{2,1,0:T(8,128)S(1)} %broadcast_in_dim.2), channel_id=1, replica_groups=mesh['tm'=8,'space'=4] {'tm','space'}, dimensions={0} | all-to-all | bytes 262144 | tf_op jit(solution)/shard_map/all_to_all | solution.py:722
  (36 shorter events, 4.7 us)
Async XLA Ops:
  0.6 1.6 %copy-start = (f32[2,256,1024]{2,1,0:T(8,128)S(1)}, f32[2,256,1024]{2,1,0:T(8,128)}, u32[]{:S(2)}) copy-start(f32[2,256,1024]{2,1,0:T(8,128)} %param.4) | copy-start | bytes 6291460
  2.2 1.6 %copy-start.2 = (f32[2,256,1024]{2,1,0:T(8,128)S(1)}, f32[2,256,1024]{2,1,0:T(8,128)}, u32[]{:S(2)}) copy-start(f32[2,256,1024]{2,1,0:T(8,128)} %param.3) | copy-start | bytes 6291460
  3.8 1.2 copy-start.4
  6.6 17.4 %copy-start.5 = (f32[256,1024]{1,0:T(8,128)S(1)}, f32[256,1024]{1,0:T(8,128)}, u32[]{:S(2)}) copy-start(f32[256,1024]{1,0:T(8,128)} %param.5) | copy-start | bytes 3145732
  6.6 25.5 %collective-permute-start.3 = (f32[256,8,128]{2,1,0:T(8,128)S(1)}, f32[256,8,128]{2,1,0:T(8,128)S(1)}, u32[]{:S(2)}, u32[]{:S(2)}) collective-permute-start(f32[256,8,128]{2,1,0:T(8,128)S(1)} %shard_map.52), channel_id=1, source_target_pairs={{0,4},{4,8},{8,12},{12,16},{16,20},{20,24},{24,28},{1,5},{5,9},{9,... | collective-permute-start | bytes 3145736 | tf_op jit(solution)/shard_map/ppermute | solution.py:651
  9.2 14.8 %copy-start.1 = (f32[2,256,1024]{2,1,0:T(8,128)S(1)}, f32[2,256,1024]{2,1,0:T(8,128)}, u32[]{:S(2)}) copy-start(f32[2,256,1024]{2,1,0:T(8,128)} %param.4) | copy-start | bytes 6291460
  9.2 14.8 %copy-start.3 = (f32[2,256,1024]{2,1,0:T(8,128)S(1)}, f32[2,256,1024]{2,1,0:T(8,128)}, u32[]{:S(2)}) copy-start(f32[2,256,1024]{2,1,0:T(8,128)} %param.3) | copy-start | bytes 6291460
  12.0 20.1 %collective-permute-start.2 = (f32[32,64,128]{2,1,0:T(8,128)S(1)}, f32[32,64,128]{2,1,0:T(8,128)S(1)}, u32[]{:S(2)}, u32[]{:S(2)}) collective-permute-start(f32[32,64,128]{2,1,0:T(8,128)S(1)} %get-tuple-element.47), channel_id=1, source_target_pairs={{0,4},{4,8},{8,12},{12,16},{16,20},{20,24},{24,28},{1,5},{5,9},{9,... | collective-permute-start | bytes 3145736 | tf_op jit(solution)/shard_map/ppermute | solution.py:645
  16.5 7.4 %collective-permute-start = (f32[55,8,128]{2,1,0:T(8,128)S(1)}, f32[55,8,128]{2,1,0:T(8,128)S(1)}, u32[]{:S(2)}, u32[]{:S(2)}) collective-permute-start(f32[55,8,128]{2,1,0:T(8,128)S(1)} %get-tuple-element.40), channel_id=1, source_target_pairs={{0,1},{2,3},{1,0},{3,2},{4,5},{6,7},{5,4},{7,6},{8,9},{10,11},{9,8... | collective-permute-start | bytes 675848 | tf_op jit(solution)/shard_map/ppermute | solution.py:646
  18.1 5.8 %collective-permute-start.1 = (f32[55,8,128]{2,1,0:T(8,128)S(1)}, f32[55,8,128]{2,1,0:T(8,128)S(1)}, u32[]{:S(2)}, u32[]{:S(2)}) collective-permute-start(f32[55,8,128]{2,1,0:T(8,128)S(1)} %get-tuple-element.41), channel_id=1, source_target_pairs={{1,2},{2,1},{5,6},{6,5},{9,10},{10,9},{13,14},{14,13},{17,18},{18,... | collective-permute-start | bytes 675848 | tf_op jit(solution)/shard_map/ppermute | solution.py:647
  29.8 2.3 %collective-permute-start.4 = (f32[40,8,128]{2,1,0:T(8,128)S(1)}, f32[40,8,128]{2,1,0:T(8,128)S(1)}, u32[]{:S(2)}, u32[]{:S(2)}) collective-permute-start(f32[40,8,128]{2,1,0:T(8,128)S(1)} %get-tuple-element.48), channel_id=1, source_target_pairs={{0,4},{4,8},{8,12},{12,16},{16,20},{20,24},{24,28},{1,5},{5,9},{9,... | collective-permute-start | bytes 491528 | tf_op jit(solution)/shard_map/ppermute | solution.py:658
  33.9 9.6 %collective-permute-start.5 = (f32[47,8,128]{2,1,0:T(8,128)S(1)}, f32[47,8,128]{2,1,0:T(8,128)S(1)}, u32[]{:S(2)}, u32[]{:S(2)}) collective-permute-start(f32[47,8,128]{2,1,0:T(8,128)S(1)} %get-tuple-element.55), channel_id=1, source_target_pairs={{0,4},{4,0},{8,12},{12,8},{16,20},{20,16},{24,28},{28,24},{1,5},{5... | collective-permute-start | bytes 577544 | tf_op jit(solution)/shard_map/ppermute | solution.py:669
  38.3 8.1 %collective-permute-start.6 = (f32[47,8,128]{2,1,0:T(8,128)S(1)}, f32[47,8,128]{2,1,0:T(8,128)S(1)}, u32[]{:S(2)}, u32[]{:S(2)}) collective-permute-start(f32[47,8,128]{2,1,0:T(8,128)S(1)} %get-tuple-element.56), channel_id=1, source_target_pairs={{0,8},{4,12},{8,0},{12,4},{16,24},{20,28},{24,16},{28,20},{1,9},{5... | collective-permute-start | bytes 577544 | tf_op jit(solution)/shard_map/ppermute | solution.py:669
  40.7 9.3 %collective-permute-start.7 = (f32[47,8,128]{2,1,0:T(8,128)S(1)}, f32[47,8,128]{2,1,0:T(8,128)S(1)}, u32[]{:S(2)}, u32[]{:S(2)}) collective-permute-start(f32[47,8,128]{2,1,0:T(8,128)S(1)} %get-tuple-element.57), channel_id=1, source_target_pairs={{0,12},{4,8},{8,4},{12,0},{16,28},{20,24},{24,20},{28,16},{1,13},{... | collective-permute-start | bytes 577544 | tf_op jit(solution)/shard_map/ppermute | solution.py:669
  40.7 11.8 %collective-permute-start.8 = (f32[47,8,128]{2,1,0:T(8,128)S(1)}, f32[47,8,128]{2,1,0:T(8,128)S(1)}, u32[]{:S(2)}, u32[]{:S(2)}) collective-permute-start(f32[47,8,128]{2,1,0:T(8,128)S(1)} %get-tuple-element.58), channel_id=1, source_target_pairs={{0,16},{4,20},{8,24},{12,28},{16,0},{20,4},{24,8},{28,12},{1,17},{... | collective-permute-start | bytes 577544 | tf_op jit(solution)/shard_map/ppermute | solution.py:669
  43.4 28.2 %collective-permute-start.9 = (f32[47,8,128]{2,1,0:T(8,128)S(1)}, f32[47,8,128]{2,1,0:T(8,128)S(1)}, u32[]{:S(2)}, u32[]{:S(2)}) collective-permute-start(f32[47,8,128]{2,1,0:T(8,128)S(1)} %get-tuple-element.59), channel_id=1, source_target_pairs={{0,20},{4,16},{8,28},{12,24},{16,4},{20,0},{24,12},{28,8},{1,21},{... | collective-permute-start | bytes 577544 | tf_op jit(solution)/shard_map/ppermute | solution.py:669
  43.4 28.2 %collective-permute-start.10 = (f32[47,8,128]{2,1,0:T(8,128)S(1)}, f32[47,8,128]{2,1,0:T(8,128)S(1)}, u32[]{:S(2)}, u32[]{:S(2)}) collective-permute-start(f32[47,8,128]{2,1,0:T(8,128)S(1)} %get-tuple-element.60), channel_id=1, source_target_pairs={{0,24},{4,28},{8,16},{12,20},{16,8},{20,12},{24,0},{28,4},{1,25},{... | collective-permute-start | bytes 577544 | tf_op jit(solution)/shard_map/ppermute | solution.py:669
  46.4 25.3 %collective-permute-start.11 = (f32[47,8,128]{2,1,0:T(8,128)S(1)}, f32[47,8,128]{2,1,0:T(8,128)S(1)}, u32[]{:S(2)}, u32[]{:S(2)}) collective-permute-start(f32[47,8,128]{2,1,0:T(8,128)S(1)} %get-tuple-element.61), channel_id=1, source_target_pairs={{0,28},{4,24},{8,20},{12,16},{16,12},{20,8},{24,4},{28,0},{1,29},{... | collective-permute-start | bytes 577544 | tf_op jit(solution)/shard_map/ppermute | solution.py:669
  50.0 57.3 %collective-permute-start.20 = (f32[256,8,128]{2,1,0:T(8,128)S(1)}, f32[256,8,128]{2,1,0:T(8,128)S(1)}, u32[]{:S(2)}, u32[]{:S(2)}) collective-permute-start(f32[256,8,128]{2,1,0:T(8,128)S(1)} %get-tuple-element.74), channel_id=1, source_target_pairs={{0,4},{4,8},{8,12},{12,16},{16,20},{20,24},{24,28},{1,5},{5,9},{9,... | collective-permute-start | bytes 3145736 | tf_op jit(solution)/shard_map/ppermute | solution.py:678
  77.0 3.8 %collective-permute-start.12 = (f32[50,8,128]{2,1,0:T(8,128)S(1)}, f32[50,8,128]{2,1,0:T(8,128)S(1)}, u32[]{:S(2)}, u32[]{:S(2)}) collective-permute-start(f32[50,8,128]{2,1,0:T(8,128)S(1)} %get-tuple-element.63), channel_id=1, source_target_pairs={{0,4},{4,0},{8,12},{12,8},{16,20},{20,16},{24,28},{28,24},{1,5},{5... | collective-permute-start | bytes 614408 | tf_op jit(solution)/shard_map/ppermute | solution.py:669
  77.0 8.0 %collective-permute-start.13 = (f32[50,8,128]{2,1,0:T(8,128)S(1)}, f32[50,8,128]{2,1,0:T(8,128)S(1)}, u32[]{:S(2)}, u32[]{:S(2)}) collective-permute-start(f32[50,8,128]{2,1,0:T(8,128)S(1)} %get-tuple-element.64), channel_id=1, source_target_pairs={{0,8},{4,12},{8,0},{12,4},{16,24},{20,28},{24,16},{28,20},{1,9},{5... | collective-permute-start | bytes 614408 | tf_op jit(solution)/shard_map/ppermute | solution.py:669
  77.1 11.2 %collective-permute-start.14 = (f32[50,8,128]{2,1,0:T(8,128)S(1)}, f32[50,8,128]{2,1,0:T(8,128)S(1)}, u32[]{:S(2)}, u32[]{:S(2)}) collective-permute-start(f32[50,8,128]{2,1,0:T(8,128)S(1)} %get-tuple-element.65), channel_id=1, source_target_pairs={{0,12},{4,8},{8,4},{12,0},{16,28},{20,24},{24,20},{28,16},{1,13},{... | collective-permute-start | bytes 614408 | tf_op jit(solution)/shard_map/ppermute | solution.py:669
  78.9 11.9 %collective-permute-start.15 = (f32[50,8,128]{2,1,0:T(8,128)S(1)}, f32[50,8,128]{2,1,0:T(8,128)S(1)}, u32[]{:S(2)}, u32[]{:S(2)}) collective-permute-start(f32[50,8,128]{2,1,0:T(8,128)S(1)} %get-tuple-element.66), channel_id=1, source_target_pairs={{0,16},{4,20},{8,24},{12,28},{16,0},{20,4},{24,8},{28,12},{1,17},{... | collective-permute-start | bytes 614408 | tf_op jit(solution)/shard_map/ppermute | solution.py:669
  80.8 19.0 %collective-permute-start.16 = (f32[50,8,128]{2,1,0:T(8,128)S(1)}, f32[50,8,128]{2,1,0:T(8,128)S(1)}, u32[]{:S(2)}, u32[]{:S(2)}) collective-permute-start(f32[50,8,128]{2,1,0:T(8,128)S(1)} %get-tuple-element.67), channel_id=1, source_target_pairs={{0,20},{4,16},{8,28},{12,24},{16,4},{20,0},{24,12},{28,8},{1,21},{... | collective-permute-start | bytes 614408 | tf_op jit(solution)/shard_map/ppermute | solution.py:669
  85.1 14.7 %collective-permute-start.17 = (f32[50,8,128]{2,1,0:T(8,128)S(1)}, f32[50,8,128]{2,1,0:T(8,128)S(1)}, u32[]{:S(2)}, u32[]{:S(2)}) collective-permute-start(f32[50,8,128]{2,1,0:T(8,128)S(1)} %get-tuple-element.68), channel_id=1, source_target_pairs={{0,24},{4,28},{8,16},{12,20},{16,8},{20,12},{24,0},{28,4},{1,25},{... | collective-permute-start | bytes 614408 | tf_op jit(solution)/shard_map/ppermute | solution.py:669
  88.4 11.4 %collective-permute-start.18 = (f32[50,8,128]{2,1,0:T(8,128)S(1)}, f32[50,8,128]{2,1,0:T(8,128)S(1)}, u32[]{:S(2)}, u32[]{:S(2)}) collective-permute-start(f32[50,8,128]{2,1,0:T(8,128)S(1)} %get-tuple-element.69), channel_id=1, source_target_pairs={{0,28},{4,24},{8,20},{12,16},{16,12},{20,8},{24,4},{28,0},{1,29},{... | collective-permute-start | bytes 614408 | tf_op jit(solution)/shard_map/ppermute | solution.py:669
  99.8 2.0 %collective-permute-start.19 = (f32[136,8,128]{2,1,0:T(8,128)S(1)}, f32[136,8,128]{2,1,0:T(8,128)S(1)}, u32[]{:S(2)}, u32[]{:S(2)}) collective-permute-start(f32[136,8,128]{2,1,0:T(8,128)S(1)} %shard_map.57), channel_id=1, source_target_pairs={{0,4},{4,0},{8,12},{12,8},{16,20},{20,16},{24,28},{28,24},{1,5},{5... | collective-permute-start | bytes 1671176 | tf_op jit(solution)/shard_map/ppermute | solution.py:707

commit v5 on v4

--- a/solution.py
+++ b/solution.py
@@ -36,7 +36,7 @@
     return [pltpu.with_memory_space_constraint(x, pltpu.VMEM) for x in arrays]
 
 
-def kernel_call(body, outs, scratch=(), flops=0, n_in=0, specs=None, grid=(), more=()):
+def kernel_call(body, outs, scratch=(), flops=0, n_in=0, specs=None, grid=(), more=(), out_specs=None):
     def call(*args):
         held = sum(math.prod(dims) for dims in scratch)
         held += sum(math.prod(x.shape) for x in list(outs) + list(args))
@@ -45,7 +45,7 @@
             out_shape=outs,
             grid=grid,
             in_specs=specs or [vmem() for _ in range(n_in)],
-            out_specs=[vmem() for _ in outs],
+            out_specs=out_specs or [vmem() for _ in outs],
             scratch_shapes=[pltpu.VMEM(dims, jnp.float32) for dims in scratch] + list(more),
             compiler_params=pltpu.CompilerParams(vmem_limit_bytes=4 * held + 2**21),
             cost_estimate=pl.CostEstimate(flops=flops, bytes_accessed=flops, transcendentals=0),
@@ -133,9 +133,19 @@
     pl.when(jnp.logical_not(flag))(lambda: body(one, two))
 
 
-def pack_edges(guess, g_top, r_top, d_top, g_end, r_end, d_end, pair, other, later, done):
-    copy = pltpu.make_async_copy(guess.at[1], later, done)
-    copy.start()
+def take_later(guess, out, *done):
+    part = out.shape[0] // len(done)
+    copies = []
+    for k, sem in enumerate(done):
+        at = pl.ds(k * part, part)
+        copies.append(pltpu.make_async_copy(guess.at[1, at], out.at[at], sem))
+    for copy in copies:
+        copy.start()
+    for copy in copies:
+        copy.wait()
+
+
+def pack_edges(g_top, r_top, d_top, g_end, r_end, d_end, pair, other):
     count = g_top.shape[1] * 8
     refs = [((g_top, (t,)), (g_end, (t,))) for t in range(2)]
     refs += [((r_top, (t,)), (r_end, (t,))) for t in range(2)]
@@ -149,7 +159,6 @@
                 end[i * HALO + k] = strided(b, lead_b, row // 8, row % 8)
 
     either(odd_strip(), fill, pair, other)
-    copy.wait()
 
 
 def first_sweep(guess, rhs, diff, send, g1):
@@ -426,7 +435,7 @@
 
         span = BLOCK // points * 2
         if level == 1:
-            loop(lost, window - lost, ascend, unroll=min(8, span))
+            loop(lost, window - lost, ascend, unroll=11)
         else:
             block_loop(1, window - 1, ascend, None, span)
         field, other = other, field
@@ -493,7 +502,9 @@
 
 def finish(start_of, piece, rhs, s_ext, w_ext, base0, base1, own, own_spread, halves, *refs):
     fields = refs[:TEAM]
-    out, left, norm, shared, shared_spread, sol0, sol1 = refs[TEAM:]
+    whole, left, norm, shared, shared_spread, sol0, sol1, out, *done = refs[TEAM:]
+    groups = rhs.shape[1]
+    share = groups // len(done)
     rows = rhs.shape[1] * 8
     half = fields[0].shape[0] - piece
     m = masks()
@@ -542,7 +553,16 @@
                 acc = acc + rb * rb
             return acc
 
-        norm[...] = loop(0, rows // 8, last, jnp.zeros((8, 128), jnp.float32), unroll=2)
+        acc = jnp.zeros((8, 128), jnp.float32)
+        copies = []
+        for n, sem in enumerate(done):
+            acc = loop(n * share, (n + 1) * share, last, acc, unroll=4)
+            at = pl.ds(n * share, share)
+            copies.append(pltpu.make_async_copy(out.at[:, at], whole.at[:, at], sem))
+            copies[-1].start()
+        norm[...] = acc
+        for copy in copies:
+            copy.wait()
 
     either(odd == 1, solve, (shared, shared_spread), (own, own_spread))
 
@@ -635,14 +655,16 @@
         return [time, time, flat]
 
     far_args = [pltpu.with_memory_space_constraint(x, pltpu.HBM) for x in (guess_t, rhs_t, diff_t)]
-    facing, backing, g_prev = kernel_call(
-        pack_edges,
-        [shape(5 * HALO, 8, 128), shape(5 * HALO, 8, 128), shape(groups, wide, 128)],
-        specs=[pl.BlockSpec(memory_space=pl.ANY)] + edge_specs(0) + edge_specs(far),
-        grid=(1,),
-        more=[pltpu.SemaphoreType.DMA(())],
-    )(far_args[0], *far_args, *far_args)
+    (g_prev,) = kernel_call(
+        take_later,
+        [shape(groups, wide, 128)],
+        specs=[pl.BlockSpec(memory_space=pl.ANY)],
+        more=[pltpu.SemaphoreType.DMA(())] * 4,
+    )(far_args[0])
     g_prev = lax.ppermute(g_prev, "tm", later)
+    facing, backing = kernel_call(
+        pack_edges, [shape(5 * HALO, 8, 128)] * 2, specs=edge_specs(0) + edge_specs(far), grid=(1,)
+    )(*far_args, *far_args)
     facing = lax.ppermute(facing, "space", both(0))
     backing = lax.ppermute(backing, "space", both(1))
     (send,) = kernel_call(first_sweep, [shape(rows, 8, 128)], scratch=[(rows + 2, 8, 128)], n_in=3)(
@@ -713,7 +735,9 @@
     out, left, norm = kernel_call(
         functools.partial(finish, start_of, piece),
         [shape(2, groups, wide, 128), shape(rows, 8, 128), shape(8, 128)],
-        scratch=[(rows + 2 * EDGE, 8, 128)] + [(rows + 2, 8, 128)] * 3,
+        scratch=[(rows + 2 * EDGE, 8, 128)] + [(rows + 2, 8, 128)] * 3 + [(2, groups, wide, 128)],
+        more=[pltpu.SemaphoreType.DMA(())] * 4,
+        out_specs=[pl.BlockSpec(memory_space=pl.ANY), vmem(), vmem()],
         n_in=8 + TEAM,
     )(rhs_t, s_ext, w_ext, base0, base1, own, own_spread, halves, *fields)
     (sums,) = kernel_call(add_up, [shape(8, 128)], n_in=5)(left, back, norm0, norms, norm)

time: 123 us -> 119 us (0.967)
  local copies, waits for them, and re-layouts: 4.43 us -> 1.63 us
  starting transfers between devices: 34.5 us -> 33.1 us
  Pallas kernels: 24.9 us -> 23.6 us
    unnamed x12, local copies, waits for them, and re-layouts: 4.42 us -> 1.62 us
    ppermute x1, starting transfers between devices: 2.59 us -> 4.63 us  [body(): got = lax.ppermute(send, 'tm', later)]
    ppermute x1, starting transfers between devices: 4.5 us -> 2.46 us  [body(): g_prev = lax.ppermute(g_prev, 'tm', later)]
    ppermute x14, starting transfers between devices: 21.1 us -> 19.7 us  [exchange(): moved[k] = lax.ppermute(parts[k], 'tm', [(i, i ^ k) for i in range(count)])]
    pallas_call x10 -> x11, Pallas kernels: 24.9 us -> 23.6 us  [call(): pl.pallas_call(body, out_shape=outs, grid=grid, in_specs=specs or [vmem()...]
where the time goes in v5:
time: 119 us
  waiting for transfers between devices  43.6 us (37%)
  starting transfers between devices  33.1 us (28%)
  Pallas kernels  23.6 us (20%)
  blocking collectives  15.4 us (13%)
  local copies, waits for them, and re-layouts  1.63 us (1%)
    ppermute x14, waiting for transfers between devices, exchange(): moved[k] = lax.ppermute(parts[k], 'tm', [(i, i ^ k) for i in range(count)])  36.8 us
    pallas_call x11, Pallas kernels, call(): pl.pallas_call(body, out_shape=outs, grid=grid, in_specs=specs or [vmem()...  23.6 us
    ppermute x14, starting transfers between devices, exchange(): moved[k] = lax.ppermute(parts[k], 'tm', [(i, i ^ k) for i in range(count)])  19.7 us
    all_to_all x1, blocking collectives, body(): every = lax.all_to_all(every, ('tm', 'space'), 0, 0)  15.4 us
    ppermute x1, waiting for transfers between devices, body(): facing = lax.ppermute(facing, 'space', both(0))  5.12 us
    ppermute x1, starting transfers between devices, body(): got = lax.ppermute(send, 'tm', later)  4.63 us
    ppermute x1, starting transfers between devices, body(): back = lax.ppermute(back, 'tm', later)  2.53 us
    ppermute x1, starting transfers between devices, body(): g_prev = lax.ppermute(g_prev, 'tm', later)  2.46 us
  transfers between devices with their start and end apart: 21, of which 9 were waited for; matrix products, arithmetic and copies ran while one was open for 0% of the time, Pallas kernels for 17%

profile of v5, /device:TPU:0, one launch (start us, length us, event | category | flops | bytes accessed | tf_op | source)
XLA Modules:
  0.0 118.9 jit_solution(11469794305866972557)
XLA Ops:
  0.7 1.4 %shard_map.52 = f32[32,64,128]{2,1,0:T(8,128)S(1)} custom-call(f32[2,32,64,128]{3,2,1,0:T(8,128)} %bitcast.20), custom_call_target="tpu_custom_call" | custom-call | tf_op jit(solution)/shard_map/pallas_call | solution.py:43
  2.0 2.5 %collective-permute-start.2 = (f32[32,64,128]{2,1,0:T(8,128)S(1)}, f32[32,64,128]{2,1,0:T(8,128)S(1)}, u32[]{:S(2)}, u32[]{:S(2)}) collective-permute-start(f32[32,64,128]{2,1,0:T(8,128)S(1)} %shard_map.52), channel_id=1, source_target_pairs={{0,4},{4,8},{8,12},{12,16},{16,20},{20,24},{24,28},{1,5},{5,9},{9,... | collective-permute-start | bytes 3145736 | tf_op jit(solution)/shard_map/ppermute | solution.py:664
  4.5 1.6 %copy-done.2 = f32[2,256,1024]{2,1,0:T(8,128)S(1)} copy-done((f32[2,256,1024]{2,1,0:T(8,128)S(1)}, f32[2,256,1024]{2,1,0:T(8,128)}, u32[]{:S(2)}) %copy-start.2) | copy-done | bytes 2097176
  6.1 1.5 %shard_map.53 = f32[256,8,128]{2,1,0:T(8,128)S(1)} custom-call(f32[2,32,64,128]{3,2,1,0:T(8,128)S(1)} %bitcast.23, f32[2,32,64,128]{3,2,1,0:T(8,128)S(1)} %bitcast.27, f32[32,64,128]{2,1,0:T(8,128)S(1)} %bitcast.32), custom_call_target="tpu_custom_call" | custom-call | tf_op jit(solution)/shard_map/pallas_call | solution.py:43
  7.7 4.6 %collective-permute-start.3 = (f32[256,8,128]{2,1,0:T(8,128)S(1)}, f32[256,8,128]{2,1,0:T(8,128)S(1)}, u32[]{:S(2)}, u32[]{:S(2)}) collective-permute-start(f32[256,8,128]{2,1,0:T(8,128)S(1)} %shard_map.53), channel_id=1, source_target_pairs={{0,4},{4,8},{8,12},{12,16},{16,20},{20,24},{24,28},{1,5},{5,9},{9,... | collective-permute-start | bytes 3145736 | tf_op jit(solution)/shard_map/ppermute | solution.py:673
  12.3 1.4 %shard_map.50 = (f32[55,8,128]{2,1,0:T(8,128)S(1)}, f32[55,8,128]{2,1,0:T(8,128)S(1)}) custom-call(f32[2,32,64,128]{3,2,1,0:T(8,128)} %bitcast.21, f32[2,32,64,128]{3,2,1,0:T(8,128)} %bitcast.25, f32[32,64,128]{2,1,0:T(8,128)} %bitcast.30, f32[2,32,64,128]{3,2,1,0:T(8,128)} %bitcast.22, f32[2,32,64,128]{3,2,1,0:T(8,128)} %bitcast.26, f32[32,64,128]{2,1,0:T(8,128)} %bitcast.31), custom_call_target="tpu_custom_call" | custom-call | tf_op jit(solution)/shard_map/pallas_call | solution.py:43
  13.7 1.6 %collective-permute-start = (f32[55,8,128]{2,1,0:T(8,128)S(1)}, f32[55,8,128]{2,1,0:T(8,128)S(1)}, u32[]{:S(2)}, u32[]{:S(2)}) collective-permute-start(f32[55,8,128]{2,1,0:T(8,128)S(1)} %get-tuple-element.39), channel_id=1, source_target_pairs={{0,1},{2,3},{1,0},{3,2},{4,5},{6,7},{5,4},{7,6},{8,9},{10,11},{9,8... | collective-permute-start | bytes 675848 | tf_op jit(solution)/shard_map/ppermute | solution.py:668
  16.0 5.1 %collective-permute-done.pair = f32[55,8,128]{2,1,0:T(8,128)S(1)} collective-permute-done((f32[55,8,128]{2,1,0:T(8,128)S(1)}, f32[55,8,128]{2,1,0:T(8,128)S(1)}, u32[]{:S(2)}, u32[]{:S(2)}) %collective-permute-start) | collective-permute-done | bytes 225312 | tf_op jit(solution)/shard_map/ppermute | solution.py:668
  21.2 5.8 %shard_map.51 = (f32[278,8,128]{2,1,0:T(8,128)S(1)}, f32[278,8,128]{2,1,0:T(8,128)S(1)}, f32[278,8,128]{2,1,0:T(8,128)S(1)}, f32[278,8,128]{2,1,0:T(8,128)S(1)},...) custom-call(f32[2,32,64,128]{3,2,1,0:T(8,128)S(1)} %bitcast.24, ...), custom_call_target="tpu_custom_call" | custom-call | tf_op jit(solution)/shard_map/pallas_call | solution.py:43
  27.0 1.3 %collective-permute-start.4 = (f32[40,8,128]{2,1,0:T(8,128)S(1)}, f32[40,8,128]{2,1,0:T(8,128)S(1)}, u32[]{:S(2)}, u32[]{:S(2)}) collective-permute-start(f32[40,8,128]{2,1,0:T(8,128)S(1)} %get-tuple-element.46), channel_id=1, source_target_pairs={{0,4},{4,8},{8,12},{12,16},{16,20},{20,24},{24,28},{1,5},{5,9},{9,... | collective-permute-start | bytes 491528 | tf_op jit(solution)/shard_map/ppermute | solution.py:680
  28.3 1.0 collective-permute-done.4.edges
  29.3 1.7 %shard_map.54 = (f32[47,8,128]{2,1,0:T(8,128)S(1)}, f32[47,8,128]{2,1,0:T(8,128)S(1)}, f32[47,8,128]{2,1,0:T(8,128)S(1)}, f32[47,8,128]{2,1,0:T(8,128)S(1)}, f32...) custom-call(f32[32,64,128]{2,1,0:T(8,128)S(1)} %collective-permute-d, ...), custom_call_target="tpu_custom_call" | custom-call | tf_op jit(solution)/shard_map/pallas_call | solution.py:43
  31.1 3.5 %collective-permute-start.5 = (f32[47,8,128]{2,1,0:T(8,128)S(1)}, f32[47,8,128]{2,1,0:T(8,128)S(1)}, u32[]{:S(2)}, u32[]{:S(2)}) collective-permute-start(f32[47,8,128]{2,1,0:T(8,128)S(1)} %get-tuple-element.53), channel_id=1, source_target_pairs={{0,4},{4,0},{8,12},{12,8},{16,20},{20,16},{24,28},{28,24},{1,5},{5... | collective-permute-start | bytes 577544 | tf_op jit(solution)/shard_map/ppermute | solution.py:691
  34.6 2.4 %collective-permute-start.6 = (f32[47,8,128]{2,1,0:T(8,128)S(1)}, f32[47,8,128]{2,1,0:T(8,128)S(1)}, u32[]{:S(2)}, u32[]{:S(2)}) collective-permute-start(f32[47,8,128]{2,1,0:T(8,128)S(1)} %get-tuple-element.54), channel_id=1, source_target_pairs={{0,8},{4,12},{8,0},{12,4},{16,24},{20,28},{24,16},{28,20},{1,9},{5... | collective-permute-start | bytes 577544 | tf_op jit(solution)/shard_map/ppermute | solution.py:691
  37.1 2.7 %collective-permute-start.8 = (f32[47,8,128]{2,1,0:T(8,128)S(1)}, f32[47,8,128]{2,1,0:T(8,128)S(1)}, u32[]{:S(2)}, u32[]{:S(2)}) collective-permute-start(f32[47,8,128]{2,1,0:T(8,128)S(1)} %get-tuple-element.56), channel_id=1, source_target_pairs={{0,16},{4,20},{8,24},{12,28},{16,0},{20,4},{24,8},{28,12},{1,17},{... | collective-permute-start | bytes 577544 | tf_op jit(solution)/shard_map/ppermute | solution.py:691
  39.8 1.2 %collective-permute-start.10 = (f32[47,8,128]{2,1,0:T(8,128)S(1)}, f32[47,8,128]{2,1,0:T(8,128)S(1)}, u32[]{:S(2)}, u32[]{:S(2)}) collective-permute-start(f32[47,8,128]{2,1,0:T(8,128)S(1)} %get-tuple-element.58), channel_id=1, source_target_pairs={{0,24},{4,28},{8,16},{12,20},{16,8},{20,12},{24,0},{28,4},{1,25},{... | collective-permute-start | bytes 577544 | tf_op jit(solution)/shard_map/ppermute | solution.py:691
  41.0 1.7 %collective-permute-done.6.refs_2_ = f32[47,8,128]{2,1,0:T(8,128)S(1)} collective-permute-done((f32[47,8,128]{2,1,0:T(8,128)S(1)}, f32[47,8,128]{2,1,0:T(8,128)S(1)}, u32[]{:S(2)}, u32[]{:S(2)}) %collective-permute-start.6) | collective-permute-done | bytes 192544 | tf_op jit(solution)/shard_map/ppermute | solution.py:691
  42.7 1.6 %collective-permute-start.11 = (f32[47,8,128]{2,1,0:T(8,128)S(1)}, f32[47,8,128]{2,1,0:T(8,128)S(1)}, u32[]{:S(2)}, u32[]{:S(2)}) collective-permute-start(f32[47,8,128]{2,1,0:T(8,128)S(1)} %get-tuple-element.59), channel_id=1, source_target_pairs={{0,28},{4,24},{8,20},{12,16},{16,12},{20,8},{24,4},{28,0},{1,29},{... | collective-permute-start | bytes 577544 | tf_op jit(solution)/shard_map/ppermute | solution.py:691
  44.9 1.5 %collective-permute-done.7.refs_3_ = f32[47,8,128]{2,1,0:T(8,128)S(1)} collective-permute-done((f32[47,8,128]{2,1,0:T(8,128)S(1)}, f32[47,8,128]{2,1,0:T(8,128)S(1)}, u32[]{:S(2)}, u32[]{:S(2)}) %collective-permute-start.7) | collective-permute-done | bytes 192544 | tf_op jit(solution)/shard_map/ppermute | solution.py:691
  46.4 2.5 %collective-permute-start.20 = (f32[256,8,128]{2,1,0:T(8,128)S(1)}, f32[256,8,128]{2,1,0:T(8,128)S(1)}, u32[]{:S(2)}, u32[]{:S(2)}) collective-permute-start(f32[256,8,128]{2,1,0:T(8,128)S(1)} %get-tuple-element.72), channel_id=1, source_target_pairs={{0,4},{4,8},{8,12},{12,16},{16,20},{20,24},{24,28},{1,5},{5,9},{9,... | collective-permute-start | bytes 3145736 | tf_op jit(solution)/shard_map/ppermute | solution.py:700
  48.9 19.0 %collective-permute-done.9.refs_5_ = f32[47,8,128]{2,1,0:T(8,128)S(1)} collective-permute-done((f32[47,8,128]{2,1,0:T(8,128)S(1)}, f32[47,8,128]{2,1,0:T(8,128)S(1)}, u32[]{:S(2)}, u32[]{:S(2)}) %collective-permute-start.9) | collective-permute-done | bytes 192544 | tf_op jit(solution)/shard_map/ppermute | solution.py:691
  68.0 5.2 %shard_map.56 = (f32[50,8,128]{2,1,0:T(8,128)S(1)}, f32[50,8,128]{2,1,0:T(8,128)S(1)}, f32[50,8,128]{2,1,0:T(8,128)S(1)}, f32[50,8,128]{2,1,0:T(8,128)S(1)}, f32...) custom-call(f32[278,8,128]{2,1,0:T(8,128)S(1)} %get-tuple-element.41, ...), custom_call_target="tpu_custom_call" | custom-call | tf_op jit(solution)/shard_map/pallas_call | solution.py:43
  73.3 1.8 %collective-permute-start.14 = (f32[50,8,128]{2,1,0:T(8,128)S(1)}, f32[50,8,128]{2,1,0:T(8,128)S(1)}, u32[]{:S(2)}, u32[]{:S(2)}) collective-permute-start(f32[50,8,128]{2,1,0:T(8,128)S(1)} %get-tuple-element.63), channel_id=1, source_target_pairs={{0,12},{4,8},{8,4},{12,0},{16,28},{20,24},{24,20},{28,16},{1,13},{... | collective-permute-start | bytes 614408 | tf_op jit(solution)/shard_map/ppermute | solution.py:691
  75.1 1.9 %collective-permute-start.15 = (f32[50,8,128]{2,1,0:T(8,128)S(1)}, f32[50,8,128]{2,1,0:T(8,128)S(1)}, u32[]{:S(2)}, u32[]{:S(2)}) collective-permute-start(f32[50,8,128]{2,1,0:T(8,128)S(1)} %get-tuple-element.64), channel_id=1, source_target_pairs={{0,16},{4,20},{8,24},{12,28},{16,0},{20,4},{24,8},{28,12},{1,17},{... | collective-permute-start | bytes 614408 | tf_op jit(solution)/shard_map/ppermute | solution.py:691
  77.3 4.0 %collective-permute-done.13.refs_2_ = f32[50,8,128]{2,1,0:T(8,128)S(1)} collective-permute-done((f32[50,8,128]{2,1,0:T(8,128)S(1)}, f32[50,8,128]{2,1,0:T(8,128)S(1)}, u32[]{:S(2)}, u32[]{:S(2)}) %collective-permute-start.13) | collective-permute-done | bytes 204832 | tf_op jit(solution)/shard_map/ppermute | solution.py:691
  81.3 1.7 %collective-permute-start.17 = (f32[50,8,128]{2,1,0:T(8,128)S(1)}, f32[50,8,128]{2,1,0:T(8,128)S(1)}, u32[]{:S(2)}, u32[]{:S(2)}) collective-permute-start(f32[50,8,128]{2,1,0:T(8,128)S(1)} %get-tuple-element.66), channel_id=1, source_target_pairs={{0,24},{4,28},{8,16},{12,20},{16,8},{20,12},{24,0},{28,4},{1,25},{... | collective-permute-start | bytes 614408 | tf_op jit(solution)/shard_map/ppermute | solution.py:691
  82.9 1.6 %collective-permute-done.14.refs_3_ = f32[50,8,128]{2,1,0:T(8,128)S(1)} collective-permute-done((f32[50,8,128]{2,1,0:T(8,128)S(1)}, f32[50,8,128]{2,1,0:T(8,128)S(1)}, u32[]{:S(2)}, u32[]{:S(2)}) %collective-permute-start.14) | collective-permute-done | bytes 204832 | tf_op jit(solution)/shard_map/ppermute | solution.py:691
  84.6 2.5 %collective-permute-start.18 = (f32[50,8,128]{2,1,0:T(8,128)S(1)}, f32[50,8,128]{2,1,0:T(8,128)S(1)}, u32[]{:S(2)}, u32[]{:S(2)}) collective-permute-start(f32[50,8,128]{2,1,0:T(8,128)S(1)} %get-tuple-element.67), channel_id=1, source_target_pairs={{0,28},{4,24},{8,20},{12,16},{16,12},{20,8},{24,4},{28,0},{1,29},{... | collective-permute-start | bytes 614408 | tf_op jit(solution)/shard_map/ppermute | solution.py:691
  87.0 8.9 %collective-permute-done.16.refs_5_ = f32[50,8,128]{2,1,0:T(8,128)S(1)} collective-permute-done((f32[50,8,128]{2,1,0:T(8,128)S(1)}, f32[50,8,128]{2,1,0:T(8,128)S(1)}, u32[]{:S(2)}, u32[]{:S(2)}) %collective-permute-start.16) | collective-permute-done | bytes 204832 | tf_op jit(solution)/shard_map/ppermute | solution.py:691
  96.2 1.2 shard_map.57
  98.0 4.4 %shard_map.59 = (f32[2,32,64,128]{3,2,1,0:T(8,128)}, f32[256,8,128]{2,1,0:T(8,128)S(1)}, f32[8,128]{1,0:T(8,128)S(1)}) custom-call(f32[2,32,64,128]{3,2,1,0:T(8,128)S(1)} %bitcast.29, f32[278,8,128]{2,1,0:T(8,128)S(1)} %get-tuple-element.41.s_ext, f32[278,8,128]{2,1,0:T(8,128)S(1)} %get-tuple-element.42.w_ext, f32[258,8,128]{2,1,0:T(8,128)S(1)} %get-tuple-element.50.base0, ...), custom_call_target="tpu_custom_call" | custom-call | tf_op jit(solution)/shard_map/pallas_call | solution.py:43
  102.8 15.4 %all_to_all.5 = f32[32,8,128]{2,1,0:T(8,128)S(1)} all-to-all(f32[32,8,128]{2,1,0:T(8,128)S(1)} %broadcast_in_dim.2), channel_id=1, replica_groups=mesh['tm'=8,'space'=4] {'tm','space'}, dimensions={0} | all-to-all | bytes 262144 | tf_op jit(solution)/shard_map/all_to_all | solution.py:746
  (37 shorter events, 3.7 us)
Async XLA Ops:
  0.6 3.9 %copy-start = (f32[2,256,1024]{2,1,0:T(8,128)S(1)}, f32[2,256,1024]{2,1,0:T(8,128)}, u32[]{:S(2)}) copy-start(f32[2,256,1024]{2,1,0:T(8,128)} %param.4) | copy-start | bytes 6291460
  0.6 3.9 %copy-start.4 = (f32[256,1024]{1,0:T(8,128)S(1)}, f32[256,1024]{1,0:T(8,128)}, u32[]{:S(2)}) copy-start(f32[256,1024]{1,0:T(8,128)} %param.5) | copy-start | bytes 3145732
  2.0 27.3 %collective-permute-start.2 = (f32[32,64,128]{2,1,0:T(8,128)S(1)}, f32[32,64,128]{2,1,0:T(8,128)S(1)}, u32[]{:S(2)}, u32[]{:S(2)}) collective-permute-start(f32[32,64,128]{2,1,0:T(8,128)S(1)} %shard_map.52), channel_id=1, source_target_pairs={{0,4},{4,8},{8,12},{12,16},{16,20},{20,24},{24,28},{1,5},{5,9},{9,... | collective-permute-start | bytes 3145736 | tf_op jit(solution)/shard_map/ppermute | solution.py:664
  4.5 1.6 %copy-start.2 = (f32[2,256,1024]{2,1,0:T(8,128)S(1)}, f32[2,256,1024]{2,1,0:T(8,128)}, u32[]{:S(2)}) copy-start(f32[2,256,1024]{2,1,0:T(8,128)} %param.3) | copy-start | bytes 6291460
  7.7 13.5 %copy-start.5 = (f32[256,1024]{1,0:T(8,128)S(1)}, f32[256,1024]{1,0:T(8,128)}, u32[]{:S(2)}) copy-start(f32[256,1024]{1,0:T(8,128)} %param.5) | copy-start | bytes 3145732
  7.7 21.7 %collective-permute-start.3 = (f32[256,8,128]{2,1,0:T(8,128)S(1)}, f32[256,8,128]{2,1,0:T(8,128)S(1)}, u32[]{:S(2)}, u32[]{:S(2)}) collective-permute-start(f32[256,8,128]{2,1,0:T(8,128)S(1)} %shard_map.53), channel_id=1, source_target_pairs={{0,4},{4,8},{8,12},{12,16},{16,20},{20,24},{24,28},{1,5},{5,9},{9,... | collective-permute-start | bytes 3145736 | tf_op jit(solution)/shard_map/ppermute | solution.py:673
  12.3 8.8 %copy-start.1 = (f32[2,256,1024]{2,1,0:T(8,128)S(1)}, f32[2,256,1024]{2,1,0:T(8,128)}, u32[]{:S(2)}) copy-start(f32[2,256,1024]{2,1,0:T(8,128)} %param.4) | copy-start | bytes 6291460
  12.3 8.8 %copy-start.3 = (f32[2,256,1024]{2,1,0:T(8,128)S(1)}, f32[2,256,1024]{2,1,0:T(8,128)}, u32[]{:S(2)}) copy-start(f32[2,256,1024]{2,1,0:T(8,128)} %param.3) | copy-start | bytes 6291460
  13.7 7.4 %collective-permute-start = (f32[55,8,128]{2,1,0:T(8,128)S(1)}, f32[55,8,128]{2,1,0:T(8,128)S(1)}, u32[]{:S(2)}, u32[]{:S(2)}) collective-permute-start(f32[55,8,128]{2,1,0:T(8,128)S(1)} %get-tuple-element.39), channel_id=1, source_target_pairs={{0,1},{2,3},{1,0},{3,2},{4,5},{6,7},{5,4},{7,6},{8,9},{10,11},{9,8... | collective-permute-start | bytes 675848 | tf_op jit(solution)/shard_map/ppermute | solution.py:668
  15.4 5.8 %collective-permute-start.1 = (f32[55,8,128]{2,1,0:T(8,128)S(1)}, f32[55,8,128]{2,1,0:T(8,128)S(1)}, u32[]{:S(2)}, u32[]{:S(2)}) collective-permute-start(f32[55,8,128]{2,1,0:T(8,128)S(1)} %get-tuple-element.40), channel_id=1, source_target_pairs={{1,2},{2,1},{5,6},{6,5},{9,10},{10,9},{13,14},{14,13},{17,18},{18,... | collective-permute-start | bytes 675848 | tf_op jit(solution)/shard_map/ppermute | solution.py:669
  27.0 2.3 %collective-permute-start.4 = (f32[40,8,128]{2,1,0:T(8,128)S(1)}, f32[40,8,128]{2,1,0:T(8,128)S(1)}, u32[]{:S(2)}, u32[]{:S(2)}) collective-permute-start(f32[40,8,128]{2,1,0:T(8,128)S(1)} %get-tuple-element.46), channel_id=1, source_target_pairs={{0,4},{4,8},{8,12},{12,16},{16,20},{20,24},{24,28},{1,5},{5,9},{9,... | collective-permute-start | bytes 491528 | tf_op jit(solution)/shard_map/ppermute | solution.py:680
  31.1 8.7 %collective-permute-start.5 = (f32[47,8,128]{2,1,0:T(8,128)S(1)}, f32[47,8,128]{2,1,0:T(8,128)S(1)}, u32[]{:S(2)}, u32[]{:S(2)}) collective-permute-start(f32[47,8,128]{2,1,0:T(8,128)S(1)} %get-tuple-element.53), channel_id=1, source_target_pairs={{0,4},{4,0},{8,12},{12,8},{16,20},{20,16},{24,28},{28,24},{1,5},{5... | collective-permute-start | bytes 577544 | tf_op jit(solution)/shard_map/ppermute | solution.py:691
  34.6 8.1 %collective-permute-start.6 = (f32[47,8,128]{2,1,0:T(8,128)S(1)}, f32[47,8,128]{2,1,0:T(8,128)S(1)}, u32[]{:S(2)}, u32[]{:S(2)}) collective-permute-start(f32[47,8,128]{2,1,0:T(8,128)S(1)} %get-tuple-element.54), channel_id=1, source_target_pairs={{0,8},{4,12},{8,0},{12,4},{16,24},{20,28},{24,16},{28,20},{1,9},{5... | collective-permute-start | bytes 577544 | tf_op jit(solution)/shard_map/ppermute | solution.py:691
  37.0 9.3 %collective-permute-start.7 = (f32[47,8,128]{2,1,0:T(8,128)S(1)}, f32[47,8,128]{2,1,0:T(8,128)S(1)}, u32[]{:S(2)}, u32[]{:S(2)}) collective-permute-start(f32[47,8,128]{2,1,0:T(8,128)S(1)} %get-tuple-element.55), channel_id=1, source_target_pairs={{0,12},{4,8},{8,4},{12,0},{16,28},{20,24},{24,20},{28,16},{1,13},{... | collective-permute-start | bytes 577544 | tf_op jit(solution)/shard_map/ppermute | solution.py:691
  37.1 11.8 %collective-permute-start.8 = (f32[47,8,128]{2,1,0:T(8,128)S(1)}, f32[47,8,128]{2,1,0:T(8,128)S(1)}, u32[]{:S(2)}, u32[]{:S(2)}) collective-permute-start(f32[47,8,128]{2,1,0:T(8,128)S(1)} %get-tuple-element.56), channel_id=1, source_target_pairs={{0,16},{4,20},{8,24},{12,28},{16,0},{20,4},{24,8},{28,12},{1,17},{... | collective-permute-start | bytes 577544 | tf_op jit(solution)/shard_map/ppermute | solution.py:691
  39.7 28.2 %collective-permute-start.9 = (f32[47,8,128]{2,1,0:T(8,128)S(1)}, f32[47,8,128]{2,1,0:T(8,128)S(1)}, u32[]{:S(2)}, u32[]{:S(2)}) collective-permute-start(f32[47,8,128]{2,1,0:T(8,128)S(1)} %get-tuple-element.57), channel_id=1, source_target_pairs={{0,20},{4,16},{8,28},{12,24},{16,4},{20,0},{24,12},{28,8},{1,21},{... | collective-permute-start | bytes 577544 | tf_op jit(solution)/shard_map/ppermute | solution.py:691
  39.8 28.2 %collective-permute-start.10 = (f32[47,8,128]{2,1,0:T(8,128)S(1)}, f32[47,8,128]{2,1,0:T(8,128)S(1)}, u32[]{:S(2)}, u32[]{:S(2)}) collective-permute-start(f32[47,8,128]{2,1,0:T(8,128)S(1)} %get-tuple-element.58), channel_id=1, source_target_pairs={{0,24},{4,28},{8,16},{12,20},{16,8},{20,12},{24,0},{28,4},{1,25},{... | collective-permute-start | bytes 577544 | tf_op jit(solution)/shard_map/ppermute | solution.py:691
  42.7 25.3 %collective-permute-start.11 = (f32[47,8,128]{2,1,0:T(8,128)S(1)}, f32[47,8,128]{2,1,0:T(8,128)S(1)}, u32[]{:S(2)}, u32[]{:S(2)}) collective-permute-start(f32[47,8,128]{2,1,0:T(8,128)S(1)} %get-tuple-element.59), channel_id=1, source_target_pairs={{0,28},{4,24},{8,20},{12,16},{16,12},{20,8},{24,4},{28,0},{1,29},{... | collective-permute-start | bytes 577544 | tf_op jit(solution)/shard_map/ppermute | solution.py:691
  46.4 56.1 %collective-permute-start.20 = (f32[256,8,128]{2,1,0:T(8,128)S(1)}, f32[256,8,128]{2,1,0:T(8,128)S(1)}, u32[]{:S(2)}, u32[]{:S(2)}) collective-permute-start(f32[256,8,128]{2,1,0:T(8,128)S(1)} %get-tuple-element.72), channel_id=1, source_target_pairs={{0,4},{4,8},{8,12},{12,16},{16,20},{20,24},{24,28},{1,5},{5,9},{9,... | collective-permute-start | bytes 3145736 | tf_op jit(solution)/shard_map/ppermute | solution.py:700
  73.2 3.8 %collective-permute-start.12 = (f32[50,8,128]{2,1,0:T(8,128)S(1)}, f32[50,8,128]{2,1,0:T(8,128)S(1)}, u32[]{:S(2)}, u32[]{:S(2)}) collective-permute-start(f32[50,8,128]{2,1,0:T(8,128)S(1)} %get-tuple-element.61), channel_id=1, source_target_pairs={{0,4},{4,0},{8,12},{12,8},{16,20},{20,16},{24,28},{28,24},{1,5},{5... | collective-permute-start | bytes 614408 | tf_op jit(solution)/shard_map/ppermute | solution.py:691
  73.2 8.0 %collective-permute-start.13 = (f32[50,8,128]{2,1,0:T(8,128)S(1)}, f32[50,8,128]{2,1,0:T(8,128)S(1)}, u32[]{:S(2)}, u32[]{:S(2)}) collective-permute-start(f32[50,8,128]{2,1,0:T(8,128)S(1)} %get-tuple-element.62), channel_id=1, source_target_pairs={{0,8},{4,12},{8,0},{12,4},{16,24},{20,28},{24,16},{28,20},{1,9},{5... | collective-permute-start | bytes 614408 | tf_op jit(solution)/shard_map/ppermute | solution.py:691
  73.3 11.2 %collective-permute-start.14 = (f32[50,8,128]{2,1,0:T(8,128)S(1)}, f32[50,8,128]{2,1,0:T(8,128)S(1)}, u32[]{:S(2)}, u32[]{:S(2)}) collective-permute-start(f32[50,8,128]{2,1,0:T(8,128)S(1)} %get-tuple-element.63), channel_id=1, source_target_pairs={{0,12},{4,8},{8,4},{12,0},{16,28},{20,24},{24,20},{28,16},{1,13},{... | collective-permute-start | bytes 614408 | tf_op jit(solution)/shard_map/ppermute | solution.py:691
  75.1 11.9 %collective-permute-start.15 = (f32[50,8,128]{2,1,0:T(8,128)S(1)}, f32[50,8,128]{2,1,0:T(8,128)S(1)}, u32[]{:S(2)}, u32[]{:S(2)}) collective-permute-start(f32[50,8,128]{2,1,0:T(8,128)S(1)} %get-tuple-element.64), channel_id=1, source_target_pairs={{0,16},{4,20},{8,24},{12,28},{16,0},{20,4},{24,8},{28,12},{1,17},{... | collective-permute-start | bytes 614408 | tf_op jit(solution)/shard_map/ppermute | solution.py:691
  77.0 19.0 %collective-permute-start.16 = (f32[50,8,128]{2,1,0:T(8,128)S(1)}, f32[50,8,128]{2,1,0:T(8,128)S(1)}, u32[]{:S(2)}, u32[]{:S(2)}) collective-permute-start(f32[50,8,128]{2,1,0:T(8,128)S(1)} %get-tuple-element.65), channel_id=1, source_target_pairs={{0,20},{4,16},{8,28},{12,24},{16,4},{20,0},{24,12},{28,8},{1,21},{... | collective-permute-start | bytes 614408 | tf_op jit(solution)/shard_map/ppermute | solution.py:691
  81.3 14.7 %collective-permute-start.17 = (f32[50,8,128]{2,1,0:T(8,128)S(1)}, f32[50,8,128]{2,1,0:T(8,128)S(1)}, u32[]{:S(2)}, u32[]{:S(2)}) collective-permute-start(f32[50,8,128]{2,1,0:T(8,128)S(1)} %get-tuple-element.66), channel_id=1, source_target_pairs={{0,24},{4,28},{8,16},{12,20},{16,8},{20,12},{24,0},{28,4},{1,25},{... | collective-permute-start | bytes 614408 | tf_op jit(solution)/shard_map/ppermute | solution.py:691
  84.6 11.4 %collective-permute-start.18 = (f32[50,8,128]{2,1,0:T(8,128)S(1)}, f32[50,8,128]{2,1,0:T(8,128)S(1)}, u32[]{:S(2)}, u32[]{:S(2)}) collective-permute-start(f32[50,8,128]{2,1,0:T(8,128)S(1)} %get-tuple-element.67), channel_id=1, source_target_pairs={{0,28},{4,24},{8,20},{12,16},{16,12},{20,8},{24,4},{28,0},{1,29},{... | collective-permute-start | bytes 614408 | tf_op jit(solution)/shard_map/ppermute | solution.py:691
  96.0 2.0 %collective-permute-start.19 = (f32[136,8,128]{2,1,0:T(8,128)S(1)}, f32[136,8,128]{2,1,0:T(8,128)S(1)}, u32[]{:S(2)}, u32[]{:S(2)}) collective-permute-start(f32[136,8,128]{2,1,0:T(8,128)S(1)} %shard_map.58), channel_id=1, source_target_pairs={{0,4},{4,0},{8,12},{12,8},{16,20},{20,16},{24,28},{28,24},{1,5},{5... | collective-permute-start | bytes 1671176 | tf_op jit(solution)/shard_map/ppermute | solution.py:729

commit v6 on v5

--- a/solution.py
+++ b/solution.py
@@ -183,7 +183,7 @@
     loop(0, rows // 8, sweep, unroll=4)
 
 
-def local_parts(guess, rhs, diff, pair, other, s_ext, w_ext, part0, left0, left1, v1, edges, g0, g1, low, high):
+def local_parts(guess, rhs, diff, pair, other, s_ext, w_ext, part0, left0, left1, v1, edges, g0, g1, low, high, drift):
     rows = rhs.shape[1] * 8
     m = masks()
 
@@ -225,11 +225,21 @@
         fill(k, low[2 * HALO + k], low[3 * HALO + k])
     for k in range(0, HALO - 1):
         fill(HALO + rows + k, high[2 * HALO + k], high[3 * HALO + k])
-    for k in range(SIDE):
-        edges[k] = v1[2 + k]
-        edges[SIDE + k] = v1[HALO + rows - 1 + k]
-        edges[2 * SIDE + k] = g1[1 + k]
-        edges[3 * SIDE + k] = g1[HALO + rows + k]
+    ends = [(2, HALO - 1), (HALO + rows, 2 * HALO + rows - 3)]
+    for n, (first, final) in enumerate(ends):
+        for i in range(first - 1, final + 2):
+            drift[n * (SIDE + 1) + i - first + 1] = w_ext[i] * g1[i]
+    for n, (first, final) in enumerate(ends):
+        for i in range(first, final + 1):
+            at = n * (SIDE + 1) + i - first + 1
+            s = s_ext[i]
+            here = drift[at]
+            edges[n * (SIDE - 1) + i - first] = v1[i] - 4.0 * s * here + s * around(drift, at, m)
+    low_at = 2 * (SIDE - 1)
+    edges[low_at] = w_ext[HALO - 1] * g1[HALO - 1]
+    edges[low_at + 1] = w_ext[HALO + rows] * g1[HALO + rows]
+    edges[low_at + 2] = v1[HALO]
+    edges[low_at + 3] = v1[HALO + rows - 1]
 
     def rest(i, a, b):
         s = s_ext[i]
@@ -271,10 +281,9 @@
             y[i] = w_ext[i] * strided(g_prev, (), g, k)
 
     loop(0, rows // 8, inner, unroll=2)
-    for k in range(SIDE):
-        y[1 + k] = w_ext[1 + k] * edges[2 * SIDE + k]
-        i = HALO + rows + k
-        y[i] = w_ext[i] * edges[3 * SIDE + k]
+    single = 2 * (SIDE - 1)
+    y[HALO - 1] = edges[single]
+    y[HALO + rows] = edges[single + 1]
 
     def resid(i, swept):
         s = s_ext[i]
@@ -284,9 +293,14 @@
         coarse[i] = a + left1[i] + here
 
     loop(HALO + 1, HALO + rows - 1, lambda i: resid(i, got[i - HALO]), unroll=32)
-    for k in range(SIDE):
-        resid(2 + k, edges[k])
-        resid(HALO + rows - 1 + k, edges[SIDE + k])
+    resid(HALO, edges[single + 2])
+    resid(HALO + rows - 1, edges[single + 3])
+    for k in range(SIDE - 1):
+        for i, at in ((2 + k, k), (HALO + rows + k, SIDE - 1 + k)):
+            taken = left0[i] + edges[at]
+            coarse[i] = taken + left1[i]
+            if i in (HALO - 1, HALO + rows):
+                resid0[i] = taken - y[i]
     for k, out in enumerate(outs):
         low = start_of(place ^ k) - REACH + HALO
 
@@ -673,8 +687,8 @@
     got = lax.ppermute(send, "tm", later)
     s_ext, w_ext, part0, left0, left1, v1, edges = kernel_call(
         local_parts,
-        [kept(ext, 8, 128)] * 2 + [shape(ext, 8, 128)] * 4 + [shape(4 * SIDE, 8, 128)],
-        scratch=[(ext, 8, 128)] * 2 + [(5 * HALO, 8, 128)] * 2,
+        [kept(ext, 8, 128)] * 2 + [shape(ext, 8, 128)] * 4 + [shape(2 * SIDE + 2, 8, 128)],
+        scratch=[(ext, 8, 128)] * 2 + [(5 * HALO, 8, 128)] * 2 + [(2 * (SIDE + 1), 8, 128)],
         n_in=5,
     )(guess_t, rhs_t, diff_t, facing, backing)
     edges = lax.ppermute(edges, "tm", later)

time: 119 us -> 118 us (level)
  no operation moved by 1% of the time
where the time goes in v6:
time: 118 us
  waiting for transfers between devices  43.5 us (37%)
  starting transfers between devices  32.4 us (27%)
  Pallas kernels  23.5 us (20%)
  blocking collectives  15.4 us (13%)
  local copies, waits for them, and re-layouts  1.63 us (1%)
    ppermute x14, waiting for transfers between devices, exchange(): moved[k] = lax.ppermute(parts[k], 'tm', [(i, i ^ k) for i in range(count)])  36.8 us
    pallas_call x11, Pallas kernels, call(): pl.pallas_call(body, out_shape=outs, grid=grid, in_specs=specs or [vmem()...  23.5 us
    ppermute x14, starting transfers between devices, exchange(): moved[k] = lax.ppermute(parts[k], 'tm', [(i, i ^ k) for i in range(count)])  19 us
    all_to_all x1, blocking collectives, body(): every = lax.all_to_all(every, ('tm', 'space'), 0, 0)  15.4 us
    ppermute x1, waiting for transfers between devices, body(): facing = lax.ppermute(facing, 'space', both(0))  5.12 us
    ppermute x1, starting transfers between devices, body(): got = lax.ppermute(send, 'tm', later)  4.63 us
    ppermute x1, starting transfers between devices, body(): back = lax.ppermute(back, 'tm', later)  2.53 us
    ppermute x1, starting transfers between devices, body(): g_prev = lax.ppermute(g_prev, 'tm', later)  2.46 us
  transfers between devices with their start and end apart: 21, of which 9 were waited for; matrix products, arithmetic and copies ran while one was open for 0% of the time, Pallas kernels for 17%

profile of v6, /device:TPU:0, one launch (start us, length us, event | category | flops | bytes accessed | tf_op | source)
XLA Modules:
  0.0 118.0 jit_solution(4474599863294683142)
XLA Ops:
  0.7 1.4 %shard_map.52 = f32[32,64,128]{2,1,0:T(8,128)S(1)} custom-call(f32[2,32,64,128]{3,2,1,0:T(8,128)} %bitcast.20), custom_call_target="tpu_custom_call" | custom-call | tf_op jit(solution)/shard_map/pallas_call | solution.py:43
  2.0 2.5 %collective-permute-start.2 = (f32[32,64,128]{2,1,0:T(8,128)S(1)}, f32[32,64,128]{2,1,0:T(8,128)S(1)}, u32[]{:S(2)}, u32[]{:S(2)}) collective-permute-start(f32[32,64,128]{2,1,0:T(8,128)S(1)} %shard_map.52), channel_id=1, source_target_pairs={{0,4},{4,8},{8,12},{12,16},{16,20},{20,24},{24,28},{1,5},{5,9},{9,... | collective-permute-start | bytes 3145736 | tf_op jit(solution)/shard_map/ppermute | solution.py:678
  4.5 1.6 %copy-done.2 = f32[2,256,1024]{2,1,0:T(8,128)S(1)} copy-done((f32[2,256,1024]{2,1,0:T(8,128)S(1)}, f32[2,256,1024]{2,1,0:T(8,128)}, u32[]{:S(2)}) %copy-start.2) | copy-done | bytes 2097176
  6.1 1.5 %shard_map.53 = f32[256,8,128]{2,1,0:T(8,128)S(1)} custom-call(f32[2,32,64,128]{3,2,1,0:T(8,128)S(1)} %bitcast.23, f32[2,32,64,128]{3,2,1,0:T(8,128)S(1)} %bitcast.27, f32[32,64,128]{2,1,0:T(8,128)S(1)} %bitcast.32), custom_call_target="tpu_custom_call" | custom-call | tf_op jit(solution)/shard_map/pallas_call | solution.py:43
  7.7 4.6 %collective-permute-start.3 = (f32[256,8,128]{2,1,0:T(8,128)S(1)}, f32[256,8,128]{2,1,0:T(8,128)S(1)}, u32[]{:S(2)}, u32[]{:S(2)}) collective-permute-start(f32[256,8,128]{2,1,0:T(8,128)S(1)} %shard_map.53), channel_id=1, source_target_pairs={{0,4},{4,8},{8,12},{12,16},{16,20},{20,24},{24,28},{1,5},{5,9},{9,... | collective-permute-start | bytes 3145736 | tf_op jit(solution)/shard_map/ppermute | solution.py:687
  12.3 1.4 %shard_map.50 = (f32[55,8,128]{2,1,0:T(8,128)S(1)}, f32[55,8,128]{2,1,0:T(8,128)S(1)}) custom-call(f32[2,32,64,128]{3,2,1,0:T(8,128)} %bitcast.21, f32[2,32,64,128]{3,2,1,0:T(8,128)} %bitcast.25, f32[32,64,128]{2,1,0:T(8,128)} %bitcast.30, f32[2,32,64,128]{3,2,1,0:T(8,128)} %bitcast.22, f32[2,32,64,128]{3,2,1,0:T(8,128)} %bitcast.26, f32[32,64,128]{2,1,0:T(8,128)} %bitcast.31), custom_call_target="tpu_custom_call" | custom-call | tf_op jit(solution)/shard_map/pallas_call | solution.py:43
  13.7 1.6 %collective-permute-start = (f32[55,8,128]{2,1,0:T(8,128)S(1)}, f32[55,8,128]{2,1,0:T(8,128)S(1)}, u32[]{:S(2)}, u32[]{:S(2)}) collective-permute-start(f32[55,8,128]{2,1,0:T(8,128)S(1)} %get-tuple-element.39), channel_id=1, source_target_pairs={{0,1},{2,3},{1,0},{3,2},{4,5},{6,7},{5,4},{7,6},{8,9},{10,11},{9,8... | collective-permute-start | bytes 675848 | tf_op jit(solution)/shard_map/ppermute | solution.py:682
  16.0 5.1 %collective-permute-done.pair = f32[55,8,128]{2,1,0:T(8,128)S(1)} collective-permute-done((f32[55,8,128]{2,1,0:T(8,128)S(1)}, f32[55,8,128]{2,1,0:T(8,128)S(1)}, u32[]{:S(2)}, u32[]{:S(2)}) %collective-permute-start) | collective-permute-done | bytes 225312 | tf_op jit(solution)/shard_map/ppermute | solution.py:682
  21.2 5.9 %shard_map.51 = (f32[278,8,128]{2,1,0:T(8,128)S(1)}, f32[278,8,128]{2,1,0:T(8,128)S(1)}, f32[278,8,128]{2,1,0:T(8,128)S(1)}, f32[278,8,128]{2,1,0:T(8,128)S(1)},...) custom-call(f32[2,32,64,128]{3,2,1,0:T(8,128)S(1)} %bitcast.24, ...), custom_call_target="tpu_custom_call" | custom-call | tf_op jit(solution)/shard_map/pallas_call | solution.py:43
  27.0 1.3 %collective-permute-start.4 = (f32[22,8,128]{2,1,0:T(8,128)S(1)}, f32[22,8,128]{2,1,0:T(8,128)S(1)}, u32[]{:S(2)}, u32[]{:S(2)}) collective-permute-start(f32[22,8,128]{2,1,0:T(8,128)S(1)} %get-tuple-element.46), channel_id=1, source_target_pairs={{0,4},{4,8},{8,12},{12,16},{16,20},{20,24},{24,28},{1,5},{5,9},{9,... | collective-permute-start | bytes 270344 | tf_op jit(solution)/shard_map/ppermute | solution.py:694
  28.3 0.9 collective-permute-done.4.edges
  29.3 1.7 %shard_map.54 = (f32[47,8,128]{2,1,0:T(8,128)S(1)}, f32[47,8,128]{2,1,0:T(8,128)S(1)}, f32[47,8,128]{2,1,0:T(8,128)S(1)}, f32[47,8,128]{2,1,0:T(8,128)S(1)}, f32...) custom-call(f32[32,64,128]{2,1,0:T(8,128)S(1)} %collective-permute-d, ...), custom_call_target="tpu_custom_call" | custom-call | tf_op jit(solution)/shard_map/pallas_call | solution.py:43
  31.0 2.9 %collective-permute-start.5 = (f32[47,8,128]{2,1,0:T(8,128)S(1)}, f32[47,8,128]{2,1,0:T(8,128)S(1)}, u32[]{:S(2)}, u32[]{:S(2)}) collective-permute-start(f32[47,8,128]{2,1,0:T(8,128)S(1)} %get-tuple-element.53), channel_id=1, source_target_pairs={{0,4},{4,0},{8,12},{12,8},{16,20},{20,16},{24,28},{28,24},{1,5},{5... | collective-permute-start | bytes 577544 | tf_op jit(solution)/shard_map/ppermute | solution.py:705
  33.9 2.4 %collective-permute-start.6 = (f32[47,8,128]{2,1,0:T(8,128)S(1)}, f32[47,8,128]{2,1,0:T(8,128)S(1)}, u32[]{:S(2)}, u32[]{:S(2)}) collective-permute-start(f32[47,8,128]{2,1,0:T(8,128)S(1)} %get-tuple-element.54), channel_id=1, source_target_pairs={{0,8},{4,12},{8,0},{12,4},{16,24},{20,28},{24,16},{28,20},{1,9},{5... | collective-permute-start | bytes 577544 | tf_op jit(solution)/shard_map/ppermute | solution.py:705
  36.3 2.7 %collective-permute-start.8 = (f32[47,8,128]{2,1,0:T(8,128)S(1)}, f32[47,8,128]{2,1,0:T(8,128)S(1)}, u32[]{:S(2)}, u32[]{:S(2)}) collective-permute-start(f32[47,8,128]{2,1,0:T(8,128)S(1)} %get-tuple-element.56), channel_id=1, source_target_pairs={{0,16},{4,20},{8,24},{12,28},{16,0},{20,4},{24,8},{28,12},{1,17},{... | collective-permute-start | bytes 577544 | tf_op jit(solution)/shard_map/ppermute | solution.py:705
  39.0 1.2 %collective-permute-start.10 = (f32[47,8,128]{2,1,0:T(8,128)S(1)}, f32[47,8,128]{2,1,0:T(8,128)S(1)}, u32[]{:S(2)}, u32[]{:S(2)}) collective-permute-start(f32[47,8,128]{2,1,0:T(8,128)S(1)} %get-tuple-element.58), channel_id=1, source_target_pairs={{0,24},{4,28},{8,16},{12,20},{16,8},{20,12},{24,0},{28,4},{1,25},{... | collective-permute-start | bytes 577544 | tf_op jit(solution)/shard_map/ppermute | solution.py:705
  40.2 1.7 %collective-permute-done.6.refs_2_ = f32[47,8,128]{2,1,0:T(8,128)S(1)} collective-permute-done((f32[47,8,128]{2,1,0:T(8,128)S(1)}, f32[47,8,128]{2,1,0:T(8,128)S(1)}, u32[]{:S(2)}, u32[]{:S(2)}) %collective-permute-start.6) | collective-permute-done | bytes 192544 | tf_op jit(solution)/shard_map/ppermute | solution.py:705
  41.9 1.6 %collective-permute-start.11 = (f32[47,8,128]{2,1,0:T(8,128)S(1)}, f32[47,8,128]{2,1,0:T(8,128)S(1)}, u32[]{:S(2)}, u32[]{:S(2)}) collective-permute-start(f32[47,8,128]{2,1,0:T(8,128)S(1)} %get-tuple-element.59), channel_id=1, source_target_pairs={{0,28},{4,24},{8,20},{12,16},{16,12},{20,8},{24,4},{28,0},{1,29},{... | collective-permute-start | bytes 577544 | tf_op jit(solution)/shard_map/ppermute | solution.py:705
  44.1 1.5 %collective-permute-done.7.refs_3_ = f32[47,8,128]{2,1,0:T(8,128)S(1)} collective-permute-done((f32[47,8,128]{2,1,0:T(8,128)S(1)}, f32[47,8,128]{2,1,0:T(8,128)S(1)}, u32[]{:S(2)}, u32[]{:S(2)}) %collective-permute-start.7) | collective-permute-done | bytes 192544 | tf_op jit(solution)/shard_map/ppermute | solution.py:705
  45.6 2.5 %collective-permute-start.20 = (f32[256,8,128]{2,1,0:T(8,128)S(1)}, f32[256,8,128]{2,1,0:T(8,128)S(1)}, u32[]{:S(2)}, u32[]{:S(2)}) collective-permute-start(f32[256,8,128]{2,1,0:T(8,128)S(1)} %get-tuple-element.72), channel_id=1, source_target_pairs={{0,4},{4,8},{8,12},{12,16},{16,20},{20,24},{24,28},{1,5},{5,9},{9,... | collective-permute-start | bytes 3145736 | tf_op jit(solution)/shard_map/ppermute | solution.py:714
  48.1 19.0 %collective-permute-done.9.refs_5_ = f32[47,8,128]{2,1,0:T(8,128)S(1)} collective-permute-done((f32[47,8,128]{2,1,0:T(8,128)S(1)}, f32[47,8,128]{2,1,0:T(8,128)S(1)}, u32[]{:S(2)}, u32[]{:S(2)}) %collective-permute-start.9) | collective-permute-done | bytes 192544 | tf_op jit(solution)/shard_map/ppermute | solution.py:705
  67.2 5.2 %shard_map.56 = (f32[50,8,128]{2,1,0:T(8,128)S(1)}, f32[50,8,128]{2,1,0:T(8,128)S(1)}, f32[50,8,128]{2,1,0:T(8,128)S(1)}, f32[50,8,128]{2,1,0:T(8,128)S(1)}, f32...) custom-call(f32[278,8,128]{2,1,0:T(8,128)S(1)} %get-tuple-element.41, ...), custom_call_target="tpu_custom_call" | custom-call | tf_op jit(solution)/shard_map/pallas_call | solution.py:43
  72.5 1.8 %collective-permute-start.14 = (f32[50,8,128]{2,1,0:T(8,128)S(1)}, f32[50,8,128]{2,1,0:T(8,128)S(1)}, u32[]{:S(2)}, u32[]{:S(2)}) collective-permute-start(f32[50,8,128]{2,1,0:T(8,128)S(1)} %get-tuple-element.63), channel_id=1, source_target_pairs={{0,12},{4,8},{8,4},{12,0},{16,28},{20,24},{24,20},{28,16},{1,13},{... | collective-permute-start | bytes 614408 | tf_op jit(solution)/shard_map/ppermute | solution.py:705
  74.3 1.9 %collective-permute-start.15 = (f32[50,8,128]{2,1,0:T(8,128)S(1)}, f32[50,8,128]{2,1,0:T(8,128)S(1)}, u32[]{:S(2)}, u32[]{:S(2)}) collective-permute-start(f32[50,8,128]{2,1,0:T(8,128)S(1)} %get-tuple-element.64), channel_id=1, source_target_pairs={{0,16},{4,20},{8,24},{12,28},{16,0},{20,4},{24,8},{28,12},{1,17},{... | collective-permute-start | bytes 614408 | tf_op jit(solution)/shard_map/ppermute | solution.py:705
  76.5 4.0 %collective-permute-done.13.refs_2_ = f32[50,8,128]{2,1,0:T(8,128)S(1)} collective-permute-done((f32[50,8,128]{2,1,0:T(8,128)S(1)}, f32[50,8,128]{2,1,0:T(8,128)S(1)}, u32[]{:S(2)}, u32[]{:S(2)}) %collective-permute-start.13) | collective-permute-done | bytes 204832 | tf_op jit(solution)/shard_map/ppermute | solution.py:705
  80.5 1.7 %collective-permute-start.17 = (f32[50,8,128]{2,1,0:T(8,128)S(1)}, f32[50,8,128]{2,1,0:T(8,128)S(1)}, u32[]{:S(2)}, u32[]{:S(2)}) collective-permute-start(f32[50,8,128]{2,1,0:T(8,128)S(1)} %get-tuple-element.66), channel_id=1, source_target_pairs={{0,24},{4,28},{8,16},{12,20},{16,8},{20,12},{24,0},{28,4},{1,25},{... | collective-permute-start | bytes 614408 | tf_op jit(solution)/shard_map/ppermute | solution.py:705
  82.1 1.6 %collective-permute-done.14.refs_3_ = f32[50,8,128]{2,1,0:T(8,128)S(1)} collective-permute-done((f32[50,8,128]{2,1,0:T(8,128)S(1)}, f32[50,8,128]{2,1,0:T(8,128)S(1)}, u32[]{:S(2)}, u32[]{:S(2)}) %collective-permute-start.14) | collective-permute-done | bytes 204832 | tf_op jit(solution)/shard_map/ppermute | solution.py:705
  83.8 2.5 %collective-permute-start.18 = (f32[50,8,128]{2,1,0:T(8,128)S(1)}, f32[50,8,128]{2,1,0:T(8,128)S(1)}, u32[]{:S(2)}, u32[]{:S(2)}) collective-permute-start(f32[50,8,128]{2,1,0:T(8,128)S(1)} %get-tuple-element.67), channel_id=1, source_target_pairs={{0,28},{4,24},{8,20},{12,16},{16,12},{20,8},{24,4},{28,0},{1,29},{... | collective-permute-start | bytes 614408 | tf_op jit(solution)/shard_map/ppermute | solution.py:705
  86.2 8.9 %collective-permute-done.16.refs_5_ = f32[50,8,128]{2,1,0:T(8,128)S(1)} collective-permute-done((f32[50,8,128]{2,1,0:T(8,128)S(1)}, f32[50,8,128]{2,1,0:T(8,128)S(1)}, u32[]{:S(2)}, u32[]{:S(2)}) %collective-permute-start.16) | collective-permute-done | bytes 204832 | tf_op jit(solution)/shard_map/ppermute | solution.py:705
  95.4 1.2 %shard_map.57 = (f32[260,8,128]{2,1,0:T(8,128)S(1)}, f32[258,8,128]{2,1,0:T(8,128)S(1)}) custom-call(f32[278,8,128]{2,1,0:T(8,128)S(1)} %get-tuple-element.41.s_ext, f32[278,8,128]{2,1,0:T(8,128)S(1)} %get-tuple-element.42.w_ext, f32[50,8,128]{2,1,0:T(8,128)S(1)} %get-tuple-element.60.refs_0_, f32[50,8,128]{2,1,0:T(8,128)S(1)} %collective-permute-done.12.refs_1_, ...), custom_call_target="tpu_custom_call" | custom-call | tf_op jit(solution)/shard_map/pallas_call | solution.py:43
  97.2 4.4 %shard_map.59 = (f32[2,32,64,128]{3,2,1,0:T(8,128)}, f32[256,8,128]{2,1,0:T(8,128)S(1)}, f32[8,128]{1,0:T(8,128)S(1)}) custom-call(f32[2,32,64,128]{3,2,1,0:T(8,128)S(1)} %bitcast.29, f32[278,8,128]{2,1,0:T(8,128)S(1)} %get-tuple-element.41.s_ext, f32[278,8,128]{2,1,0:T(8,128)S(1)} %get-tuple-element.42.w_ext, f32[258,8,128]{2,1,0:T(8,128)S(1)} %get-tuple-element.50.base0, ...), custom_call_target="tpu_custom_call" | custom-call | tf_op jit(solution)/shard_map/pallas_call | solution.py:43
  102.0 15.4 %all_to_all.5 = f32[32,8,128]{2,1,0:T(8,128)S(1)} all-to-all(f32[32,8,128]{2,1,0:T(8,128)S(1)} %broadcast_in_dim.2), channel_id=1, replica_groups=mesh['tm'=8,'space'=4] {'tm','space'}, dimensions={0} | all-to-all | bytes 262144 | tf_op jit(solution)/shard_map/all_to_all | solution.py:760
  (37 shorter events, 3.7 us)
Async XLA Ops:
  0.6 3.9 %copy-start = (f32[2,256,1024]{2,1,0:T(8,128)S(1)}, f32[2,256,1024]{2,1,0:T(8,128)}, u32[]{:S(2)}) copy-start(f32[2,256,1024]{2,1,0:T(8,128)} %param.4) | copy-start | bytes 6291460
  0.6 3.9 %copy-start.4 = (f32[256,1024]{1,0:T(8,128)S(1)}, f32[256,1024]{1,0:T(8,128)}, u32[]{:S(2)}) copy-start(f32[256,1024]{1,0:T(8,128)} %param.5) | copy-start | bytes 3145732
  2.0 27.2 %collective-permute-start.2 = (f32[32,64,128]{2,1,0:T(8,128)S(1)}, f32[32,64,128]{2,1,0:T(8,128)S(1)}, u32[]{:S(2)}, u32[]{:S(2)}) collective-permute-start(f32[32,64,128]{2,1,0:T(8,128)S(1)} %shard_map.52), channel_id=1, source_target_pairs={{0,4},{4,8},{8,12},{12,16},{16,20},{20,24},{24,28},{1,5},{5,9},{9,... | collective-permute-start | bytes 3145736 | tf_op jit(solution)/shard_map/ppermute | solution.py:678
  4.5 1.6 %copy-start.2 = (f32[2,256,1024]{2,1,0:T(8,128)S(1)}, f32[2,256,1024]{2,1,0:T(8,128)}, u32[]{:S(2)}) copy-start(f32[2,256,1024]{2,1,0:T(8,128)} %param.3) | copy-start | bytes 6291460
  7.7 13.5 %copy-start.5 = (f32[256,1024]{1,0:T(8,128)S(1)}, f32[256,1024]{1,0:T(8,128)}, u32[]{:S(2)}) copy-start(f32[256,1024]{1,0:T(8,128)} %param.5) | copy-start | bytes 3145732
  7.7 21.6 %collective-permute-start.3 = (f32[256,8,128]{2,1,0:T(8,128)S(1)}, f32[256,8,128]{2,1,0:T(8,128)S(1)}, u32[]{:S(2)}, u32[]{:S(2)}) collective-permute-start(f32[256,8,128]{2,1,0:T(8,128)S(1)} %shard_map.53), channel_id=1, source_target_pairs={{0,4},{4,8},{8,12},{12,16},{16,20},{20,24},{24,28},{1,5},{5,9},{9,... | collective-permute-start | bytes 3145736 | tf_op jit(solution)/shard_map/ppermute | solution.py:687
  12.3 8.8 %copy-start.1 = (f32[2,256,1024]{2,1,0:T(8,128)S(1)}, f32[2,256,1024]{2,1,0:T(8,128)}, u32[]{:S(2)}) copy-start(f32[2,256,1024]{2,1,0:T(8,128)} %param.4) | copy-start | bytes 6291460
  12.3 8.8 %copy-start.3 = (f32[2,256,1024]{2,1,0:T(8,128)S(1)}, f32[2,256,1024]{2,1,0:T(8,128)}, u32[]{:S(2)}) copy-start(f32[2,256,1024]{2,1,0:T(8,128)} %param.3) | copy-start | bytes 6291460
  13.7 7.4 %collective-permute-start = (f32[55,8,128]{2,1,0:T(8,128)S(1)}, f32[55,8,128]{2,1,0:T(8,128)S(1)}, u32[]{:S(2)}, u32[]{:S(2)}) collective-permute-start(f32[55,8,128]{2,1,0:T(8,128)S(1)} %get-tuple-element.39), channel_id=1, source_target_pairs={{0,1},{2,3},{1,0},{3,2},{4,5},{6,7},{5,4},{7,6},{8,9},{10,11},{9,8... | collective-permute-start | bytes 675848 | tf_op jit(solution)/shard_map/ppermute | solution.py:682
  15.4 5.8 %collective-permute-start.1 = (f32[55,8,128]{2,1,0:T(8,128)S(1)}, f32[55,8,128]{2,1,0:T(8,128)S(1)}, u32[]{:S(2)}, u32[]{:S(2)}) collective-permute-start(f32[55,8,128]{2,1,0:T(8,128)S(1)} %get-tuple-element.40), channel_id=1, source_target_pairs={{1,2},{2,1},{5,6},{6,5},{9,10},{10,9},{13,14},{14,13},{17,18},{18,... | collective-permute-start | bytes 675848 | tf_op jit(solution)/shard_map/ppermute | solution.py:683
  27.0 2.2 %collective-permute-start.4 = (f32[22,8,128]{2,1,0:T(8,128)S(1)}, f32[22,8,128]{2,1,0:T(8,128)S(1)}, u32[]{:S(2)}, u32[]{:S(2)}) collective-permute-start(f32[22,8,128]{2,1,0:T(8,128)S(1)} %get-tuple-element.46), channel_id=1, source_target_pairs={{0,4},{4,8},{8,12},{12,16},{16,20},{20,24},{24,28},{1,5},{5,9},{9,... | collective-permute-start | bytes 270344 | tf_op jit(solution)/shard_map/ppermute | solution.py:694
  31.0 8.0 %collective-permute-start.5 = (f32[47,8,128]{2,1,0:T(8,128)S(1)}, f32[47,8,128]{2,1,0:T(8,128)S(1)}, u32[]{:S(2)}, u32[]{:S(2)}) collective-permute-start(f32[47,8,128]{2,1,0:T(8,128)S(1)} %get-tuple-element.53), channel_id=1, source_target_pairs={{0,4},{4,0},{8,12},{12,8},{16,20},{20,16},{24,28},{28,24},{1,5},{5... | collective-permute-start | bytes 577544 | tf_op jit(solution)/shard_map/ppermute | solution.py:705
  33.9 8.0 %collective-permute-start.6 = (f32[47,8,128]{2,1,0:T(8,128)S(1)}, f32[47,8,128]{2,1,0:T(8,128)S(1)}, u32[]{:S(2)}, u32[]{:S(2)}) collective-permute-start(f32[47,8,128]{2,1,0:T(8,128)S(1)} %get-tuple-element.54), channel_id=1, source_target_pairs={{0,8},{4,12},{8,0},{12,4},{16,24},{20,28},{24,16},{28,20},{1,9},{5... | collective-permute-start | bytes 577544 | tf_op jit(solution)/shard_map/ppermute | solution.py:705
  36.2 9.3 %collective-permute-start.7 = (f32[47,8,128]{2,1,0:T(8,128)S(1)}, f32[47,8,128]{2,1,0:T(8,128)S(1)}, u32[]{:S(2)}, u32[]{:S(2)}) collective-permute-start(f32[47,8,128]{2,1,0:T(8,128)S(1)} %get-tuple-element.55), channel_id=1, source_target_pairs={{0,12},{4,8},{8,4},{12,0},{16,28},{20,24},{24,20},{28,16},{1,13},{... | collective-permute-start | bytes 577544 | tf_op jit(solution)/shard_map/ppermute | solution.py:705
  36.3 11.8 %collective-permute-start.8 = (f32[47,8,128]{2,1,0:T(8,128)S(1)}, f32[47,8,128]{2,1,0:T(8,128)S(1)}, u32[]{:S(2)}, u32[]{:S(2)}) collective-permute-start(f32[47,8,128]{2,1,0:T(8,128)S(1)} %get-tuple-element.56), channel_id=1, source_target_pairs={{0,16},{4,20},{8,24},{12,28},{16,0},{20,4},{24,8},{28,12},{1,17},{... | collective-permute-start | bytes 577544 | tf_op jit(solution)/shard_map/ppermute | solution.py:705
  39.0 28.2 %collective-permute-start.9 = (f32[47,8,128]{2,1,0:T(8,128)S(1)}, f32[47,8,128]{2,1,0:T(8,128)S(1)}, u32[]{:S(2)}, u32[]{:S(2)}) collective-permute-start(f32[47,8,128]{2,1,0:T(8,128)S(1)} %get-tuple-element.57), channel_id=1, source_target_pairs={{0,20},{4,16},{8,28},{12,24},{16,4},{20,0},{24,12},{28,8},{1,21},{... | collective-permute-start | bytes 577544 | tf_op jit(solution)/shard_map/ppermute | solution.py:705
  39.0 28.2 %collective-permute-start.10 = (f32[47,8,128]{2,1,0:T(8,128)S(1)}, f32[47,8,128]{2,1,0:T(8,128)S(1)}, u32[]{:S(2)}, u32[]{:S(2)}) collective-permute-start(f32[47,8,128]{2,1,0:T(8,128)S(1)} %get-tuple-element.58), channel_id=1, source_target_pairs={{0,24},{4,28},{8,16},{12,20},{16,8},{20,12},{24,0},{28,4},{1,25},{... | collective-permute-start | bytes 577544 | tf_op jit(solution)/shard_map/ppermute | solution.py:705
  41.9 25.3 %collective-permute-start.11 = (f32[47,8,128]{2,1,0:T(8,128)S(1)}, f32[47,8,128]{2,1,0:T(8,128)S(1)}, u32[]{:S(2)}, u32[]{:S(2)}) collective-permute-start(f32[47,8,128]{2,1,0:T(8,128)S(1)} %get-tuple-element.59), channel_id=1, source_target_pairs={{0,28},{4,24},{8,20},{12,16},{16,12},{20,8},{24,4},{28,0},{1,29},{... | collective-permute-start | bytes 577544 | tf_op jit(solution)/shard_map/ppermute | solution.py:705
  45.6 56.1 %collective-permute-start.20 = (f32[256,8,128]{2,1,0:T(8,128)S(1)}, f32[256,8,128]{2,1,0:T(8,128)S(1)}, u32[]{:S(2)}, u32[]{:S(2)}) collective-permute-start(f32[256,8,128]{2,1,0:T(8,128)S(1)} %get-tuple-element.72), channel_id=1, source_target_pairs={{0,4},{4,8},{8,12},{12,16},{16,20},{20,24},{24,28},{1,5},{5,9},{9,... | collective-permute-start | bytes 3145736 | tf_op jit(solution)/shard_map/ppermute | solution.py:714
  72.4 3.8 %collective-permute-start.12 = (f32[50,8,128]{2,1,0:T(8,128)S(1)}, f32[50,8,128]{2,1,0:T(8,128)S(1)}, u32[]{:S(2)}, u32[]{:S(2)}) collective-permute-start(f32[50,8,128]{2,1,0:T(8,128)S(1)} %get-tuple-element.61), channel_id=1, source_target_pairs={{0,4},{4,0},{8,12},{12,8},{16,20},{20,16},{24,28},{28,24},{1,5},{5... | collective-permute-start | bytes 614408 | tf_op jit(solution)/shard_map/ppermute | solution.py:705
  72.5 8.0 %collective-permute-start.13 = (f32[50,8,128]{2,1,0:T(8,128)S(1)}, f32[50,8,128]{2,1,0:T(8,128)S(1)}, u32[]{:S(2)}, u32[]{:S(2)}) collective-permute-start(f32[50,8,128]{2,1,0:T(8,128)S(1)} %get-tuple-element.62), channel_id=1, source_target_pairs={{0,8},{4,12},{8,0},{12,4},{16,24},{20,28},{24,16},{28,20},{1,9},{5... | collective-permute-start | bytes 614408 | tf_op jit(solution)/shard_map/ppermute | solution.py:705
  72.5 11.2 %collective-permute-start.14 = (f32[50,8,128]{2,1,0:T(8,128)S(1)}, f32[50,8,128]{2,1,0:T(8,128)S(1)}, u32[]{:S(2)}, u32[]{:S(2)}) collective-permute-start(f32[50,8,128]{2,1,0:T(8,128)S(1)} %get-tuple-element.63), channel_id=1, source_target_pairs={{0,12},{4,8},{8,4},{12,0},{16,28},{20,24},{24,20},{28,16},{1,13},{... | collective-permute-start | bytes 614408 | tf_op jit(solution)/shard_map/ppermute | solution.py:705
  74.3 11.9 %collective-permute-start.15 = (f32[50,8,128]{2,1,0:T(8,128)S(1)}, f32[50,8,128]{2,1,0:T(8,128)S(1)}, u32[]{:S(2)}, u32[]{:S(2)}) collective-permute-start(f32[50,8,128]{2,1,0:T(8,128)S(1)} %get-tuple-element.64), channel_id=1, source_target_pairs={{0,16},{4,20},{8,24},{12,28},{16,0},{20,4},{24,8},{28,12},{1,17},{... | collective-permute-start | bytes 614408 | tf_op jit(solution)/shard_map/ppermute | solution.py:705
  76.2 19.0 %collective-permute-start.16 = (f32[50,8,128]{2,1,0:T(8,128)S(1)}, f32[50,8,128]{2,1,0:T(8,128)S(1)}, u32[]{:S(2)}, u32[]{:S(2)}) collective-permute-start(f32[50,8,128]{2,1,0:T(8,128)S(1)} %get-tuple-element.65), channel_id=1, source_target_pairs={{0,20},{4,16},{8,28},{12,24},{16,4},{20,0},{24,12},{28,8},{1,21},{... | collective-permute-start | bytes 614408 | tf_op jit(solution)/shard_map/ppermute | solution.py:705
  80.5 14.7 %collective-permute-start.17 = (f32[50,8,128]{2,1,0:T(8,128)S(1)}, f32[50,8,128]{2,1,0:T(8,128)S(1)}, u32[]{:S(2)}, u32[]{:S(2)}) collective-permute-start(f32[50,8,128]{2,1,0:T(8,128)S(1)} %get-tuple-element.66), channel_id=1, source_target_pairs={{0,24},{4,28},{8,16},{12,20},{16,8},{20,12},{24,0},{28,4},{1,25},{... | collective-permute-start | bytes 614408 | tf_op jit(solution)/shard_map/ppermute | solution.py:705
  83.8 11.4 %collective-permute-start.18 = (f32[50,8,128]{2,1,0:T(8,128)S(1)}, f32[50,8,128]{2,1,0:T(8,128)S(1)}, u32[]{:S(2)}, u32[]{:S(2)}) collective-permute-start(f32[50,8,128]{2,1,0:T(8,128)S(1)} %get-tuple-element.67), channel_id=1, source_target_pairs={{0,28},{4,24},{8,20},{12,16},{16,12},{20,8},{24,4},{28,0},{1,29},{... | collective-permute-start | bytes 614408 | tf_op jit(solution)/shard_map/ppermute | solution.py:705
  95.2 2.0 %collective-permute-start.19 = (f32[136,8,128]{2,1,0:T(8,128)S(1)}, f32[136,8,128]{2,1,0:T(8,128)S(1)}, u32[]{:S(2)}, u32[]{:S(2)}) collective-permute-start(f32[136,8,128]{2,1,0:T(8,128)S(1)} %shard_map.58), channel_id=1, source_target_pairs={{0,4},{4,0},{8,12},{12,8},{16,20},{20,16},{24,28},{28,24},{1,5},{5... | collective-permute-start | bytes 1671176 | tf_op jit(solution)/shard_map/ppermute | solution.py:743

commit v7 on v6

--- a/solution.py
+++ b/solution.py
@@ -351,7 +351,7 @@
         for level in range(1, LEVELS):
             w_win[level - 1, i] = DAMPING / (1.0 + 4.0 * 2.0**level * s)
 
-    loop(0, window, level_weights, unroll=4)
+    loop(0, window, level_weights, unroll=12)
 
     def own(i, value):
         return jnp.where((i >= first_own) & (i < last_own), value, 0.0)
@@ -372,7 +372,7 @@
                 else:
                     v_ref[p, i] = w * source[p, i]
 
-        loop(0, window, smooth, unroll=4)
+        loop(0, window, smooth, unroll=2)
 
         def descend(i, acc, level=level, points=points, source=source, base=base, target=target):
             s = 2.0**level * s_win[i]
@@ -550,7 +550,7 @@
             sol0[i] = base0[i] + part[i] + w * past[i + 1]
             sol1[i] = base1[i] + part[i] + w * e[i + 1]
 
-        loop(0, rows + 2, correct, unroll=16)
+        loop(0, rows + 2, correct, unroll=8)
 
         def last(g, acc):
             for k in range(8):
@@ -750,7 +750,7 @@
         functools.partial(finish, start_of, piece),
         [shape(2, groups, wide, 128), shape(rows, 8, 128), shape(8, 128)],
         scratch=[(rows + 2 * EDGE, 8, 128)] + [(rows + 2, 8, 128)] * 3 + [(2, groups, wide, 128)],
-        more=[pltpu.SemaphoreType.DMA(())] * 4,
+        more=[pltpu.SemaphoreType.DMA(())] * 8,
         out_specs=[pl.BlockSpec(memory_space=pl.ANY), vmem(), vmem()],
         n_in=8 + TEAM,
     )(rhs_t, s_ext, w_ext, base0, base1, own, own_spread, halves, *fields)

time: 118 us -> 119 us (level)
  no operation moved by 1% of the time
where the time goes in v7:
time: 119 us; the launch traced here: 118 us
  waiting for transfers between devices  43.5 us (37%)
  starting transfers between devices  32.4 us (27%)
  Pallas kernels  23.8 us (20%)
  blocking collectives  15.4 us (13%)
  local copies, waits for them, and re-layouts  1.63 us (1%)
    ppermute x14, waiting for transfers between devices, exchange(): moved[k] = lax.ppermute(parts[k], 'tm', [(i, i ^ k) for i in range(count)])  36.8 us
    pallas_call x11, Pallas kernels, call(): pl.pallas_call(body, out_shape=outs, grid=grid, in_specs=specs or [vmem()...  23.8 us
    ppermute x14, starting transfers between devices, exchange(): moved[k] = lax.ppermute(parts[k], 'tm', [(i, i ^ k) for i in range(count)])  19 us
    all_to_all x1, blocking collectives, body(): every = lax.all_to_all(every, ('tm', 'space'), 0, 0)  15.4 us
    ppermute x1, waiting for transfers between devices, body(): facing = lax.ppermute(facing, 'space', both(0))  5.12 us
    ppermute x1, starting transfers between devices, body(): got = lax.ppermute(send, 'tm', later)  4.63 us
    ppermute x1, starting transfers between devices, body(): back = lax.ppermute(back, 'tm', later)  2.53 us
    ppermute x1, starting transfers between devices, body(): g_prev = lax.ppermute(g_prev, 'tm', later)  2.46 us
  transfers between devices with their start and end apart: 21, of which 9 were waited for; matrix products, arithmetic and copies ran while one was open for 0% of the time, Pallas kernels for 17%

profile of v7, /device:TPU:0, one launch (start us, length us, event | category | flops | bytes accessed | tf_op | source)
XLA Modules:
  0.0 118.2 jit_solution(1873351750766762522)
XLA Ops:
  0.7 1.4 %shard_map.52 = f32[32,64,128]{2,1,0:T(8,128)S(1)} custom-call(f32[2,32,64,128]{3,2,1,0:T(8,128)} %bitcast.20), custom_call_target="tpu_custom_call" | custom-call | tf_op jit(solution)/shard_map/pallas_call | solution.py:43
  2.0 2.5 %collective-permute-start.2 = (f32[32,64,128]{2,1,0:T(8,128)S(1)}, f32[32,64,128]{2,1,0:T(8,128)S(1)}, u32[]{:S(2)}, u32[]{:S(2)}) collective-permute-start(f32[32,64,128]{2,1,0:T(8,128)S(1)} %shard_map.52), channel_id=1, source_target_pairs={{0,4},{4,8},{8,12},{12,16},{16,20},{20,24},{24,28},{1,5},{5,9},{9,... | collective-permute-start | bytes 3145736 | tf_op jit(solution)/shard_map/ppermute | solution.py:678
  4.5 1.6 %copy-done.2 = f32[2,256,1024]{2,1,0:T(8,128)S(1)} copy-done((f32[2,256,1024]{2,1,0:T(8,128)S(1)}, f32[2,256,1024]{2,1,0:T(8,128)}, u32[]{:S(2)}) %copy-start.2) | copy-done | bytes 2097176
  6.1 1.5 %shard_map.53 = f32[256,8,128]{2,1,0:T(8,128)S(1)} custom-call(f32[2,32,64,128]{3,2,1,0:T(8,128)S(1)} %bitcast.23, f32[2,32,64,128]{3,2,1,0:T(8,128)S(1)} %bitcast.27, f32[32,64,128]{2,1,0:T(8,128)S(1)} %bitcast.32), custom_call_target="tpu_custom_call" | custom-call | tf_op jit(solution)/shard_map/pallas_call | solution.py:43
  7.7 4.6 %collective-permute-start.3 = (f32[256,8,128]{2,1,0:T(8,128)S(1)}, f32[256,8,128]{2,1,0:T(8,128)S(1)}, u32[]{:S(2)}, u32[]{:S(2)}) collective-permute-start(f32[256,8,128]{2,1,0:T(8,128)S(1)} %shard_map.53), channel_id=1, source_target_pairs={{0,4},{4,8},{8,12},{12,16},{16,20},{20,24},{24,28},{1,5},{5,9},{9,... | collective-permute-start | bytes 3145736 | tf_op jit(solution)/shard_map/ppermute | solution.py:687
  12.3 1.4 %shard_map.50 = (f32[55,8,128]{2,1,0:T(8,128)S(1)}, f32[55,8,128]{2,1,0:T(8,128)S(1)}) custom-call(f32[2,32,64,128]{3,2,1,0:T(8,128)} %bitcast.21, f32[2,32,64,128]{3,2,1,0:T(8,128)} %bitcast.25, f32[32,64,128]{2,1,0:T(8,128)} %bitcast.30, f32[2,32,64,128]{3,2,1,0:T(8,128)} %bitcast.22, f32[2,32,64,128]{3,2,1,0:T(8,128)} %bitcast.26, f32[32,64,128]{2,1,0:T(8,128)} %bitcast.31), custom_call_target="tpu_custom_call" | custom-call | tf_op jit(solution)/shard_map/pallas_call | solution.py:43
  13.7 1.6 %collective-permute-start = (f32[55,8,128]{2,1,0:T(8,128)S(1)}, f32[55,8,128]{2,1,0:T(8,128)S(1)}, u32[]{:S(2)}, u32[]{:S(2)}) collective-permute-start(f32[55,8,128]{2,1,0:T(8,128)S(1)} %get-tuple-element.39), channel_id=1, source_target_pairs={{0,1},{2,3},{1,0},{3,2},{4,5},{6,7},{5,4},{7,6},{8,9},{10,11},{9,8... | collective-permute-start | bytes 675848 | tf_op jit(solution)/shard_map/ppermute | solution.py:682
  16.0 5.1 %collective-permute-done.pair = f32[55,8,128]{2,1,0:T(8,128)S(1)} collective-permute-done((f32[55,8,128]{2,1,0:T(8,128)S(1)}, f32[55,8,128]{2,1,0:T(8,128)S(1)}, u32[]{:S(2)}, u32[]{:S(2)}) %collective-permute-start) | collective-permute-done | bytes 225312 | tf_op jit(solution)/shard_map/ppermute | solution.py:682
  21.2 5.9 %shard_map.51 = (f32[278,8,128]{2,1,0:T(8,128)S(1)}, f32[278,8,128]{2,1,0:T(8,128)S(1)}, f32[278,8,128]{2,1,0:T(8,128)S(1)}, f32[278,8,128]{2,1,0:T(8,128)S(1)},...) custom-call(f32[2,32,64,128]{3,2,1,0:T(8,128)S(1)} %bitcast.24, ...), custom_call_target="tpu_custom_call" | custom-call | tf_op jit(solution)/shard_map/pallas_call | solution.py:43
  27.0 1.3 %collective-permute-start.4 = (f32[22,8,128]{2,1,0:T(8,128)S(1)}, f32[22,8,128]{2,1,0:T(8,128)S(1)}, u32[]{:S(2)}, u32[]{:S(2)}) collective-permute-start(f32[22,8,128]{2,1,0:T(8,128)S(1)} %get-tuple-element.46), channel_id=1, source_target_pairs={{0,4},{4,8},{8,12},{12,16},{16,20},{20,24},{24,28},{1,5},{5,9},{9,... | collective-permute-start | bytes 270344 | tf_op jit(solution)/shard_map/ppermute | solution.py:694
  28.3 0.9 collective-permute-done.4.edges
  29.3 1.7 %shard_map.54 = (f32[47,8,128]{2,1,0:T(8,128)S(1)}, f32[47,8,128]{2,1,0:T(8,128)S(1)}, f32[47,8,128]{2,1,0:T(8,128)S(1)}, f32[47,8,128]{2,1,0:T(8,128)S(1)}, f32...) custom-call(f32[32,64,128]{2,1,0:T(8,128)S(1)} %collective-permute-d, ...), custom_call_target="tpu_custom_call" | custom-call | tf_op jit(solution)/shard_map/pallas_call | solution.py:43
  31.0 2.9 %collective-permute-start.5 = (f32[47,8,128]{2,1,0:T(8,128)S(1)}, f32[47,8,128]{2,1,0:T(8,128)S(1)}, u32[]{:S(2)}, u32[]{:S(2)}) collective-permute-start(f32[47,8,128]{2,1,0:T(8,128)S(1)} %get-tuple-element.53), channel_id=1, source_target_pairs={{0,4},{4,0},{8,12},{12,8},{16,20},{20,16},{24,28},{28,24},{1,5},{5... | collective-permute-start | bytes 577544 | tf_op jit(solution)/shard_map/ppermute | solution.py:705
  33.9 2.4 %collective-permute-start.6 = (f32[47,8,128]{2,1,0:T(8,128)S(1)}, f32[47,8,128]{2,1,0:T(8,128)S(1)}, u32[]{:S(2)}, u32[]{:S(2)}) collective-permute-start(f32[47,8,128]{2,1,0:T(8,128)S(1)} %get-tuple-element.54), channel_id=1, source_target_pairs={{0,8},{4,12},{8,0},{12,4},{16,24},{20,28},{24,16},{28,20},{1,9},{5... | collective-permute-start | bytes 577544 | tf_op jit(solution)/shard_map/ppermute | solution.py:705
  36.3 2.7 %collective-permute-start.8 = (f32[47,8,128]{2,1,0:T(8,128)S(1)}, f32[47,8,128]{2,1,0:T(8,128)S(1)}, u32[]{:S(2)}, u32[]{:S(2)}) collective-permute-start(f32[47,8,128]{2,1,0:T(8,128)S(1)} %get-tuple-element.56), channel_id=1, source_target_pairs={{0,16},{4,20},{8,24},{12,28},{16,0},{20,4},{24,8},{28,12},{1,17},{... | collective-permute-start | bytes 577544 | tf_op jit(solution)/shard_map/ppermute | solution.py:705
  39.0 1.2 %collective-permute-start.10 = (f32[47,8,128]{2,1,0:T(8,128)S(1)}, f32[47,8,128]{2,1,0:T(8,128)S(1)}, u32[]{:S(2)}, u32[]{:S(2)}) collective-permute-start(f32[47,8,128]{2,1,0:T(8,128)S(1)} %get-tuple-element.58), channel_id=1, source_target_pairs={{0,24},{4,28},{8,16},{12,20},{16,8},{20,12},{24,0},{28,4},{1,25},{... | collective-permute-start | bytes 577544 | tf_op jit(solution)/shard_map/ppermute | solution.py:705
  40.2 1.7 %collective-permute-done.6.refs_2_ = f32[47,8,128]{2,1,0:T(8,128)S(1)} collective-permute-done((f32[47,8,128]{2,1,0:T(8,128)S(1)}, f32[47,8,128]{2,1,0:T(8,128)S(1)}, u32[]{:S(2)}, u32[]{:S(2)}) %collective-permute-start.6) | collective-permute-done | bytes 192544 | tf_op jit(solution)/shard_map/ppermute | solution.py:705
  41.9 1.6 %collective-permute-start.11 = (f32[47,8,128]{2,1,0:T(8,128)S(1)}, f32[47,8,128]{2,1,0:T(8,128)S(1)}, u32[]{:S(2)}, u32[]{:S(2)}) collective-permute-start(f32[47,8,128]{2,1,0:T(8,128)S(1)} %get-tuple-element.59), channel_id=1, source_target_pairs={{0,28},{4,24},{8,20},{12,16},{16,12},{20,8},{24,4},{28,0},{1,29},{... | collective-permute-start | bytes 577544 | tf_op jit(solution)/shard_map/ppermute | solution.py:705
  44.1 1.5 %collective-permute-done.7.refs_3_ = f32[47,8,128]{2,1,0:T(8,128)S(1)} collective-permute-done((f32[47,8,128]{2,1,0:T(8,128)S(1)}, f32[47,8,128]{2,1,0:T(8,128)S(1)}, u32[]{:S(2)}, u32[]{:S(2)}) %collective-permute-start.7) | collective-permute-done | bytes 192544 | tf_op jit(solution)/shard_map/ppermute | solution.py:705
  45.6 2.5 %collective-permute-start.20 = (f32[256,8,128]{2,1,0:T(8,128)S(1)}, f32[256,8,128]{2,1,0:T(8,128)S(1)}, u32[]{:S(2)}, u32[]{:S(2)}) collective-permute-start(f32[256,8,128]{2,1,0:T(8,128)S(1)} %get-tuple-element.72), channel_id=1, source_target_pairs={{0,4},{4,8},{8,12},{12,16},{16,20},{20,24},{24,28},{1,5},{5,9},{9,... | collective-permute-start | bytes 3145736 | tf_op jit(solution)/shard_map/ppermute | solution.py:714
  48.1 19.0 %collective-permute-done.9.refs_5_ = f32[47,8,128]{2,1,0:T(8,128)S(1)} collective-permute-done((f32[47,8,128]{2,1,0:T(8,128)S(1)}, f32[47,8,128]{2,1,0:T(8,128)S(1)}, u32[]{:S(2)}, u32[]{:S(2)}) %collective-permute-start.9) | collective-permute-done | bytes 192544 | tf_op jit(solution)/shard_map/ppermute | solution.py:705
  67.2 5.3 %shard_map.56 = (f32[50,8,128]{2,1,0:T(8,128)S(1)}, f32[50,8,128]{2,1,0:T(8,128)S(1)}, f32[50,8,128]{2,1,0:T(8,128)S(1)}, f32[50,8,128]{2,1,0:T(8,128)S(1)}, f32...) custom-call(f32[278,8,128]{2,1,0:T(8,128)S(1)} %get-tuple-element.41, ...), custom_call_target="tpu_custom_call" | custom-call | tf_op jit(solution)/shard_map/pallas_call | solution.py:43
  72.7 1.8 %collective-permute-start.14 = (f32[50,8,128]{2,1,0:T(8,128)S(1)}, f32[50,8,128]{2,1,0:T(8,128)S(1)}, u32[]{:S(2)}, u32[]{:S(2)}) collective-permute-start(f32[50,8,128]{2,1,0:T(8,128)S(1)} %get-tuple-element.63), channel_id=1, source_target_pairs={{0,12},{4,8},{8,4},{12,0},{16,28},{20,24},{24,20},{28,16},{1,13},{... | collective-permute-start | bytes 614408 | tf_op jit(solution)/shard_map/ppermute | solution.py:705
  74.4 1.9 %collective-permute-start.15 = (f32[50,8,128]{2,1,0:T(8,128)S(1)}, f32[50,8,128]{2,1,0:T(8,128)S(1)}, u32[]{:S(2)}, u32[]{:S(2)}) collective-permute-start(f32[50,8,128]{2,1,0:T(8,128)S(1)} %get-tuple-element.64), channel_id=1, source_target_pairs={{0,16},{4,20},{8,24},{12,28},{16,0},{20,4},{24,8},{28,12},{1,17},{... | collective-permute-start | bytes 614408 | tf_op jit(solution)/shard_map/ppermute | solution.py:705
  76.6 4.0 %collective-permute-done.13.refs_2_ = f32[50,8,128]{2,1,0:T(8,128)S(1)} collective-permute-done((f32[50,8,128]{2,1,0:T(8,128)S(1)}, f32[50,8,128]{2,1,0:T(8,128)S(1)}, u32[]{:S(2)}, u32[]{:S(2)}) %collective-permute-start.13) | collective-permute-done | bytes 204832 | tf_op jit(solution)/shard_map/ppermute | solution.py:705
  80.6 1.7 %collective-permute-start.17 = (f32[50,8,128]{2,1,0:T(8,128)S(1)}, f32[50,8,128]{2,1,0:T(8,128)S(1)}, u32[]{:S(2)}, u32[]{:S(2)}) collective-permute-start(f32[50,8,128]{2,1,0:T(8,128)S(1)} %get-tuple-element.66), channel_id=1, source_target_pairs={{0,24},{4,28},{8,16},{12,20},{16,8},{20,12},{24,0},{28,4},{1,25},{... | collective-permute-start | bytes 614408 | tf_op jit(solution)/shard_map/ppermute | solution.py:705
  82.3 1.6 %collective-permute-done.14.refs_3_ = f32[50,8,128]{2,1,0:T(8,128)S(1)} collective-permute-done((f32[50,8,128]{2,1,0:T(8,128)S(1)}, f32[50,8,128]{2,1,0:T(8,128)S(1)}, u32[]{:S(2)}, u32[]{:S(2)}) %collective-permute-start.14) | collective-permute-done | bytes 204832 | tf_op jit(solution)/shard_map/ppermute | solution.py:705
  83.9 2.5 %collective-permute-start.18 = (f32[50,8,128]{2,1,0:T(8,128)S(1)}, f32[50,8,128]{2,1,0:T(8,128)S(1)}, u32[]{:S(2)}, u32[]{:S(2)}) collective-permute-start(f32[50,8,128]{2,1,0:T(8,128)S(1)} %get-tuple-element.67), channel_id=1, source_target_pairs={{0,28},{4,24},{8,20},{12,16},{16,12},{20,8},{24,4},{28,0},{1,29},{... | collective-permute-start | bytes 614408 | tf_op jit(solution)/shard_map/ppermute | solution.py:705
  86.4 8.9 %collective-permute-done.16.refs_5_ = f32[50,8,128]{2,1,0:T(8,128)S(1)} collective-permute-done((f32[50,8,128]{2,1,0:T(8,128)S(1)}, f32[50,8,128]{2,1,0:T(8,128)S(1)}, u32[]{:S(2)}, u32[]{:S(2)}) %collective-permute-start.16) | collective-permute-done | bytes 204832 | tf_op jit(solution)/shard_map/ppermute | solution.py:705
  95.6 1.2 shard_map.57
  97.4 4.4 %shard_map.59 = (f32[2,32,64,128]{3,2,1,0:T(8,128)}, f32[256,8,128]{2,1,0:T(8,128)S(1)}, f32[8,128]{1,0:T(8,128)S(1)}) custom-call(f32[2,32,64,128]{3,2,1,0:T(8,128)S(1)} %bitcast.29, f32[278,8,128]{2,1,0:T(8,128)S(1)} %get-tuple-element.41.s_ext, f32[278,8,128]{2,1,0:T(8,128)S(1)} %get-tuple-element.42.w_ext, f32[258,8,128]{2,1,0:T(8,128)S(1)} %get-tuple-element.50.base0, ...), custom_call_target="tpu_custom_call" | custom-call | tf_op jit(solution)/shard_map/pallas_call | solution.py:43
  102.2 15.4 %all_to_all.5 = f32[32,8,128]{2,1,0:T(8,128)S(1)} all-to-all(f32[32,8,128]{2,1,0:T(8,128)S(1)} %broadcast_in_dim.2), channel_id=1, replica_groups=mesh['tm'=8,'space'=4] {'tm','space'}, dimensions={0} | all-to-all | bytes 262144 | tf_op jit(solution)/shard_map/all_to_all | solution.py:760
  (37 shorter events, 3.7 us)
Async XLA Ops:
  0.6 3.9 %copy-start = (f32[2,256,1024]{2,1,0:T(8,128)S(1)}, f32[2,256,1024]{2,1,0:T(8,128)}, u32[]{:S(2)}) copy-start(f32[2,256,1024]{2,1,0:T(8,128)} %param.4) | copy-start | bytes 6291460
  0.6 3.9 %copy-start.4 = (f32[256,1024]{1,0:T(8,128)S(1)}, f32[256,1024]{1,0:T(8,128)}, u32[]{:S(2)}) copy-start(f32[256,1024]{1,0:T(8,128)} %param.5) | copy-start | bytes 3145732
  2.0 27.2 %collective-permute-start.2 = (f32[32,64,128]{2,1,0:T(8,128)S(1)}, f32[32,64,128]{2,1,0:T(8,128)S(1)}, u32[]{:S(2)}, u32[]{:S(2)}) collective-permute-start(f32[32,64,128]{2,1,0:T(8,128)S(1)} %shard_map.52), channel_id=1, source_target_pairs={{0,4},{4,8},{8,12},{12,16},{16,20},{20,24},{24,28},{1,5},{5,9},{9,... | collective-permute-start | bytes 3145736 | tf_op jit(solution)/shard_map/ppermute | solution.py:678
  4.5 1.6 %copy-start.2 = (f32[2,256,1024]{2,1,0:T(8,128)S(1)}, f32[2,256,1024]{2,1,0:T(8,128)}, u32[]{:S(2)}) copy-start(f32[2,256,1024]{2,1,0:T(8,128)} %param.3) | copy-start | bytes 6291460
  7.7 13.5 %copy-start.5 = (f32[256,1024]{1,0:T(8,128)S(1)}, f32[256,1024]{1,0:T(8,128)}, u32[]{:S(2)}) copy-start(f32[256,1024]{1,0:T(8,128)} %param.5) | copy-start | bytes 3145732
  7.7 21.6 %collective-permute-start.3 = (f32[256,8,128]{2,1,0:T(8,128)S(1)}, f32[256,8,128]{2,1,0:T(8,128)S(1)}, u32[]{:S(2)}, u32[]{:S(2)}) collective-permute-start(f32[256,8,128]{2,1,0:T(8,128)S(1)} %shard_map.53), channel_id=1, source_target_pairs={{0,4},{4,8},{8,12},{12,16},{16,20},{20,24},{24,28},{1,5},{5,9},{9,... | collective-permute-start | bytes 3145736 | tf_op jit(solution)/shard_map/ppermute | solution.py:687
  12.3 8.8 %copy-start.1 = (f32[2,256,1024]{2,1,0:T(8,128)S(1)}, f32[2,256,1024]{2,1,0:T(8,128)}, u32[]{:S(2)}) copy-start(f32[2,256,1024]{2,1,0:T(8,128)} %param.4) | copy-start | bytes 6291460
  12.3 8.8 %copy-start.3 = (f32[2,256,1024]{2,1,0:T(8,128)S(1)}, f32[2,256,1024]{2,1,0:T(8,128)}, u32[]{:S(2)}) copy-start(f32[2,256,1024]{2,1,0:T(8,128)} %param.3) | copy-start | bytes 6291460
  13.7 7.4 %collective-permute-start = (f32[55,8,128]{2,1,0:T(8,128)S(1)}, f32[55,8,128]{2,1,0:T(8,128)S(1)}, u32[]{:S(2)}, u32[]{:S(2)}) collective-permute-start(f32[55,8,128]{2,1,0:T(8,128)S(1)} %get-tuple-element.39), channel_id=1, source_target_pairs={{0,1},{2,3},{1,0},{3,2},{4,5},{6,7},{5,4},{7,6},{8,9},{10,11},{9,8... | collective-permute-start | bytes 675848 | tf_op jit(solution)/shard_map/ppermute | solution.py:682
  15.4 5.8 %collective-permute-start.1 = (f32[55,8,128]{2,1,0:T(8,128)S(1)}, f32[55,8,128]{2,1,0:T(8,128)S(1)}, u32[]{:S(2)}, u32[]{:S(2)}) collective-permute-start(f32[55,8,128]{2,1,0:T(8,128)S(1)} %get-tuple-element.40), channel_id=1, source_target_pairs={{1,2},{2,1},{5,6},{6,5},{9,10},{10,9},{13,14},{14,13},{17,18},{18,... | collective-permute-start | bytes 675848 | tf_op jit(solution)/shard_map/ppermute | solution.py:683
  27.0 2.2 %collective-permute-start.4 = (f32[22,8,128]{2,1,0:T(8,128)S(1)}, f32[22,8,128]{2,1,0:T(8,128)S(1)}, u32[]{:S(2)}, u32[]{:S(2)}) collective-permute-start(f32[22,8,128]{2,1,0:T(8,128)S(1)} %get-tuple-element.46), channel_id=1, source_target_pairs={{0,4},{4,8},{8,12},{12,16},{16,20},{20,24},{24,28},{1,5},{5,9},{9,... | collective-permute-start | bytes 270344 | tf_op jit(solution)/shard_map/ppermute | solution.py:694
  31.0 8.0 %collective-permute-start.5 = (f32[47,8,128]{2,1,0:T(8,128)S(1)}, f32[47,8,128]{2,1,0:T(8,128)S(1)}, u32[]{:S(2)}, u32[]{:S(2)}) collective-permute-start(f32[47,8,128]{2,1,0:T(8,128)S(1)} %get-tuple-element.53), channel_id=1, source_target_pairs={{0,4},{4,0},{8,12},{12,8},{16,20},{20,16},{24,28},{28,24},{1,5},{5... | collective-permute-start | bytes 577544 | tf_op jit(solution)/shard_map/ppermute | solution.py:705
  33.9 8.0 %collective-permute-start.6 = (f32[47,8,128]{2,1,0:T(8,128)S(1)}, f32[47,8,128]{2,1,0:T(8,128)S(1)}, u32[]{:S(2)}, u32[]{:S(2)}) collective-permute-start(f32[47,8,128]{2,1,0:T(8,128)S(1)} %get-tuple-element.54), channel_id=1, source_target_pairs={{0,8},{4,12},{8,0},{12,4},{16,24},{20,28},{24,16},{28,20},{1,9},{5... | collective-permute-start | bytes 577544 | tf_op jit(solution)/shard_map/ppermute | solution.py:705
  36.2 9.3 %collective-permute-start.7 = (f32[47,8,128]{2,1,0:T(8,128)S(1)}, f32[47,8,128]{2,1,0:T(8,128)S(1)}, u32[]{:S(2)}, u32[]{:S(2)}) collective-permute-start(f32[47,8,128]{2,1,0:T(8,128)S(1)} %get-tuple-element.55), channel_id=1, source_target_pairs={{0,12},{4,8},{8,4},{12,0},{16,28},{20,24},{24,20},{28,16},{1,13},{... | collective-permute-start | bytes 577544 | tf_op jit(solution)/shard_map/ppermute | solution.py:705
  36.3 11.8 %collective-permute-start.8 = (f32[47,8,128]{2,1,0:T(8,128)S(1)}, f32[47,8,128]{2,1,0:T(8,128)S(1)}, u32[]{:S(2)}, u32[]{:S(2)}) collective-permute-start(f32[47,8,128]{2,1,0:T(8,128)S(1)} %get-tuple-element.56), channel_id=1, source_target_pairs={{0,16},{4,20},{8,24},{12,28},{16,0},{20,4},{24,8},{28,12},{1,17},{... | collective-permute-start | bytes 577544 | tf_op jit(solution)/shard_map/ppermute | solution.py:705
  39.0 28.2 %collective-permute-start.9 = (f32[47,8,128]{2,1,0:T(8,128)S(1)}, f32[47,8,128]{2,1,0:T(8,128)S(1)}, u32[]{:S(2)}, u32[]{:S(2)}) collective-permute-start(f32[47,8,128]{2,1,0:T(8,128)S(1)} %get-tuple-element.57), channel_id=1, source_target_pairs={{0,20},{4,16},{8,28},{12,24},{16,4},{20,0},{24,12},{28,8},{1,21},{... | collective-permute-start | bytes 577544 | tf_op jit(solution)/shard_map/ppermute | solution.py:705
  39.0 28.2 %collective-permute-start.10 = (f32[47,8,128]{2,1,0:T(8,128)S(1)}, f32[47,8,128]{2,1,0:T(8,128)S(1)}, u32[]{:S(2)}, u32[]{:S(2)}) collective-permute-start(f32[47,8,128]{2,1,0:T(8,128)S(1)} %get-tuple-element.58), channel_id=1, source_target_pairs={{0,24},{4,28},{8,16},{12,20},{16,8},{20,12},{24,0},{28,4},{1,25},{... | collective-permute-start | bytes 577544 | tf_op jit(solution)/shard_map/ppermute | solution.py:705
  41.9 25.3 %collective-permute-start.11 = (f32[47,8,128]{2,1,0:T(8,128)S(1)}, f32[47,8,128]{2,1,0:T(8,128)S(1)}, u32[]{:S(2)}, u32[]{:S(2)}) collective-permute-start(f32[47,8,128]{2,1,0:T(8,128)S(1)} %get-tuple-element.59), channel_id=1, source_target_pairs={{0,28},{4,24},{8,20},{12,16},{16,12},{20,8},{24,4},{28,0},{1,29},{... | collective-permute-start | bytes 577544 | tf_op jit(solution)/shard_map/ppermute | solution.py:705
  45.6 56.3 %collective-permute-start.20 = (f32[256,8,128]{2,1,0:T(8,128)S(1)}, f32[256,8,128]{2,1,0:T(8,128)S(1)}, u32[]{:S(2)}, u32[]{:S(2)}) collective-permute-start(f32[256,8,128]{2,1,0:T(8,128)S(1)} %get-tuple-element.72), channel_id=1, source_target_pairs={{0,4},{4,8},{8,12},{12,16},{16,20},{20,24},{24,28},{1,5},{5,9},{9,... | collective-permute-start | bytes 3145736 | tf_op jit(solution)/shard_map/ppermute | solution.py:714
  72.5 3.8 %collective-permute-start.12 = (f32[50,8,128]{2,1,0:T(8,128)S(1)}, f32[50,8,128]{2,1,0:T(8,128)S(1)}, u32[]{:S(2)}, u32[]{:S(2)}) collective-permute-start(f32[50,8,128]{2,1,0:T(8,128)S(1)} %get-tuple-element.61), channel_id=1, source_target_pairs={{0,4},{4,0},{8,12},{12,8},{16,20},{20,16},{24,28},{28,24},{1,5},{5... | collective-permute-start | bytes 614408 | tf_op jit(solution)/shard_map/ppermute | solution.py:705
  72.6 8.0 %collective-permute-start.13 = (f32[50,8,128]{2,1,0:T(8,128)S(1)}, f32[50,8,128]{2,1,0:T(8,128)S(1)}, u32[]{:S(2)}, u32[]{:S(2)}) collective-permute-start(f32[50,8,128]{2,1,0:T(8,128)S(1)} %get-tuple-element.62), channel_id=1, source_target_pairs={{0,8},{4,12},{8,0},{12,4},{16,24},{20,28},{24,16},{28,20},{1,9},{5... | collective-permute-start | bytes 614408 | tf_op jit(solution)/shard_map/ppermute | solution.py:705
  72.7 11.2 %collective-permute-start.14 = (f32[50,8,128]{2,1,0:T(8,128)S(1)}, f32[50,8,128]{2,1,0:T(8,128)S(1)}, u32[]{:S(2)}, u32[]{:S(2)}) collective-permute-start(f32[50,8,128]{2,1,0:T(8,128)S(1)} %get-tuple-element.63), channel_id=1, source_target_pairs={{0,12},{4,8},{8,4},{12,0},{16,28},{20,24},{24,20},{28,16},{1,13},{... | collective-permute-start | bytes 614408 | tf_op jit(solution)/shard_map/ppermute | solution.py:705
  74.4 11.9 %collective-permute-start.15 = (f32[50,8,128]{2,1,0:T(8,128)S(1)}, f32[50,8,128]{2,1,0:T(8,128)S(1)}, u32[]{:S(2)}, u32[]{:S(2)}) collective-permute-start(f32[50,8,128]{2,1,0:T(8,128)S(1)} %get-tuple-element.64), channel_id=1, source_target_pairs={{0,16},{4,20},{8,24},{12,28},{16,0},{20,4},{24,8},{28,12},{1,17},{... | collective-permute-start | bytes 614408 | tf_op jit(solution)/shard_map/ppermute | solution.py:705
  76.3 19.0 %collective-permute-start.16 = (f32[50,8,128]{2,1,0:T(8,128)S(1)}, f32[50,8,128]{2,1,0:T(8,128)S(1)}, u32[]{:S(2)}, u32[]{:S(2)}) collective-permute-start(f32[50,8,128]{2,1,0:T(8,128)S(1)} %get-tuple-element.65), channel_id=1, source_target_pairs={{0,20},{4,16},{8,28},{12,24},{16,4},{20,0},{24,12},{28,8},{1,21},{... | collective-permute-start | bytes 614408 | tf_op jit(solution)/shard_map/ppermute | solution.py:705
  80.6 14.7 %collective-permute-start.17 = (f32[50,8,128]{2,1,0:T(8,128)S(1)}, f32[50,8,128]{2,1,0:T(8,128)S(1)}, u32[]{:S(2)}, u32[]{:S(2)}) collective-permute-start(f32[50,8,128]{2,1,0:T(8,128)S(1)} %get-tuple-element.66), channel_id=1, source_target_pairs={{0,24},{4,28},{8,16},{12,20},{16,8},{20,12},{24,0},{28,4},{1,25},{... | collective-permute-start | bytes 614408 | tf_op jit(solution)/shard_map/ppermute | solution.py:705
  83.9 11.4 %collective-permute-start.18 = (f32[50,8,128]{2,1,0:T(8,128)S(1)}, f32[50,8,128]{2,1,0:T(8,128)S(1)}, u32[]{:S(2)}, u32[]{:S(2)}) collective-permute-start(f32[50,8,128]{2,1,0:T(8,128)S(1)} %get-tuple-element.67), channel_id=1, source_target_pairs={{0,28},{4,24},{8,20},{12,16},{16,12},{20,8},{24,4},{28,0},{1,29},{... | collective-permute-start | bytes 614408 | tf_op jit(solution)/shard_map/ppermute | solution.py:705
  95.4 2.0 %collective-permute-start.19 = (f32[136,8,128]{2,1,0:T(8,128)S(1)}, f32[136,8,128]{2,1,0:T(8,128)S(1)}, u32[]{:S(2)}, u32[]{:S(2)}) collective-permute-start(f32[136,8,128]{2,1,0:T(8,128)S(1)} %shard_map.58), channel_id=1, source_target_pairs={{0,4},{4,0},{8,12},{12,8},{16,20},{20,16},{24,28},{28,24},{1,5},{5... | collective-permute-start | bytes 1671176 | tf_op jit(solution)/shard_map/ppermute | solution.py:743
